TPU v7x, 32 devices: a whole 2x2x4 slice. The times are simulated.
32 devices in a mesh: dp: 16 (over z, y, core), tensor: 2 (over x).
Axes of the slice: x: 2, y: 2, z: 4, core: 2. Of those that a mesh axis runs over, the one named last changes fastest.
Arguments:
- tokens: bfloat16 [3, 8192, 512], P(None, ('dp', 'tensor')), may hold values from -6 to 6
- w_qkv: bfloat16 [512, 8, 192], P('dp', 'tensor'), may hold values from -0.25 to 0.25
- w_proj: bfloat16 [8, 64, 512], P('tensor', 'dp'), may hold values from -1 to 1
- w_in: bfloat16 [16, 512, 2048], P('dp', None, 'tensor'), may hold values from -0.25 to 0.25
- w_out: bfloat16 [16, 2048, 512], P('dp', 'tensor'), may hold values from -4 to 4
- w_router: bfloat16 [512, 16], P(('dp', 'tensor')), may hold values from -0.25 to 0.25
- gain_attn: bfloat16 [512], P(('dp', 'tensor')), may hold values from 0.5 to 1.5
- shift_attn: bfloat16 [512], P(('dp', 'tensor')), may hold values from -0.59765625 to 0.59765625
- gain_moe: bfloat16 [512], P(('dp', 'tensor')), may hold values from 0.5 to 1.5
- shift_moe: bfloat16 [512], P(('dp', 'tensor')), may hold values from -0.59765625 to 0.59765625
- live_rows: int32 [3, 8192], P(None, 'dp'), may hold values from 0 to 1, as said below
- chosen: int32 [3, 8192, 2], P(None, 'dp'), may hold values from 0 to 15, all different within a row
- priority: int32 [3, 16, 512], P(None, 'dp'), may hold values from 0 to 511, each once within a row
- cotangent: bfloat16 [3, 8192, 512], P(None, ('dp', 'tensor')), may hold values from -6 to 6
Outputs:
- output: bfloat16 [3, 8192, 512], P(None, ('dp', 'tensor'))
- grad_tokens: float32 [3, 8192, 512], P(None, ('dp', 'tensor'))
- grad_qkv: float32 [512, 8, 192], P('dp', 'tensor')
- grad_proj: float32 [8, 64, 512], P('tensor', 'dp')
- grad_in: float32 [16, 512, 2048], P('dp', None, 'tensor')
- grad_out: float32 [16, 2048, 512], P('dp', 'tensor')
- grad_router: float32 [512, 16], P(('dp', 'tensor'))
- grad_gain_attn: float32 [512], P(('dp', 'tensor'))
- grad_shift_attn: float32 [512], P(('dp', 'tensor'))
- grad_gain_moe: float32 [512], P(('dp', 'tensor'))
- grad_shift_moe: float32 [512], P(('dp', 'tensor'))
Inputs may be any that keep to these rules, and one draw needn't show every extreme that they name: live_rows is constant on each image of 197 rows of a dp group (image i is rows i * 197 to i * 197 + 196 of the group) and 0 on the group's rows from 394 on.
All inputs are finite; a program needn't handle non-finite values.
Results may differ from a plain program's by a relative error of at most 0.025.
Values may be sent and summed in bfloat16 or wider, within the bound.
A program may use at most 256 MiB of HBM per device.

v0:
```python
import jax
import jax.numpy as jnp
from jax import lax
from jax.sharding import PartitionSpec as P

SEQ = 197


norm_eps = 1e-06


def layer_norm(values, gain_vec, shift_vec):
    centre = jnp.mean(values, axis=-1, keepdims=True)
    centered = values - centre
    spread = jnp.mean(centered * centered, axis=-1, keepdims=True)
    return centered * lax.rsqrt(spread + norm_eps) * gain_vec + shift_vec


def tanh_gelu(values):
    return jax.nn.gelu(values, approximate=True)


def route_slots(picks, ranking, living, expert_count, capacity):
    row_count = picks.shape[0]
    row_ids = jnp.arange(row_count, dtype=jnp.int32)
    ordering = jnp.zeros((row_count,), jnp.int32).at[ranking].set(row_ids)
    sorted_picks = picks[ordering]
    sorted_live = living[ordering]
    labels = jnp.arange(expert_count, dtype=jnp.int32)
    first_hit = (sorted_picks[:, 0:1] == labels[None, :]).astype(jnp.int32) * sorted_live[:, None]
    second_hit = (sorted_picks[:, 1:2] == labels[None, :]).astype(jnp.int32) * sorted_live[:, None]
    first_before = jnp.cumsum(first_hit, axis=0, dtype=jnp.int32) - first_hit
    first_total = jnp.sum(first_hit, axis=0, dtype=jnp.int32)
    second_before = (
        jnp.cumsum(second_hit, axis=0, dtype=jnp.int32) - second_hit + first_total[None, :]
    )
    place_first = jnp.sum(first_before * first_hit, axis=1, dtype=jnp.int32)
    place_second = jnp.sum(second_before * second_hit, axis=1, dtype=jnp.int32)
    placed = jnp.stack([place_first, place_second], axis=1)
    sorted_keep = (placed < capacity) & (sorted_live[:, None] > 0)
    sorted_slot = jnp.where(sorted_keep, placed, capacity)
    slots = sorted_slot[ranking]
    keep_flag = slots < capacity
    flat_index = jnp.where(keep_flag, picks * capacity + slots, expert_count * capacity)
    owners = jnp.broadcast_to(row_ids[:, None], (row_count, 2)).reshape(-1)
    table = (
        jnp.full((expert_count * capacity + 1,), row_count, jnp.int32)
        .at[flat_index.reshape(-1)]
        .set(owners)
    )
    return (keep_flag, flat_index, table[: expert_count * capacity])


def local(
    tokens,
    w_qkv,
    w_proj,
    w_in,
    w_out,
    w_router,
    gain_attn,
    shift_attn,
    gain_moe,
    shift_moe,
    live_rows,
    chosen,
    priority,
    cotangent,
):
    batch_count, rows_dev, feature_dim = tokens.shape
    row_total = live_rows.shape[1]
    dp_count = lax.axis_size("dp")
    heads_here = w_qkv.shape[1]
    head_width = w_qkv.shape[2] // 3
    flat_heads = heads_here * head_width
    expert_count = w_in.shape[0] * dp_count
    capacity = 2 * row_total // expert_count
    image_count = row_total // SEQ
    span_rows = image_count * SEQ
    tail_rows = row_total - span_rows
    factor = head_width ** (-0.5)
    highest = lax.Precision.HIGHEST
    first_row = lax.axis_index("tensor") * rows_dev
    labels = jnp.arange(expert_count, dtype=jnp.int32)
    gathered_small = (
        lax.all_gather(gain_attn, ("dp", "tensor"), axis=0, tiled=True),
        lax.all_gather(shift_attn, ("dp", "tensor"), axis=0, tiled=True),
        lax.all_gather(gain_moe, ("dp", "tensor"), axis=0, tiled=True),
        lax.all_gather(shift_moe, ("dp", "tensor"), axis=0, tiled=True),
        lax.all_gather(w_router, ("dp", "tensor"), axis=0, tiled=True),
    )
    gain_one = gathered_small[0].astype(jnp.float32)
    shift_one = gathered_small[1].astype(jnp.float32)
    gain_two = gathered_small[2].astype(jnp.float32)
    shift_two = gathered_small[3].astype(jnp.float32)
    router = gathered_small[4]
    router_wide = router.astype(jnp.float32)
    acc_qkv = jnp.zeros((w_qkv.shape[0] * dp_count, heads_here, 3 * head_width), jnp.float32)
    acc_proj = jnp.zeros((heads_here, w_proj.shape[1] * dp_count, feature_dim), jnp.float32)
    acc_in = jnp.zeros((expert_count, feature_dim, w_in.shape[2]), jnp.float32)
    acc_out = jnp.zeros((expert_count, w_out.shape[1], feature_dim), jnp.float32)
    acc_router = jnp.zeros((feature_dim, expert_count), jnp.float32)
    acc_gain_one = jnp.zeros((feature_dim,), jnp.float32)
    acc_shift_one = jnp.zeros((feature_dim,), jnp.float32)
    acc_gain_two = jnp.zeros((feature_dim,), jnp.float32)
    acc_shift_two = jnp.zeros((feature_dim,), jnp.float32)
    results = []
    input_grads = []
    for batch_id in range(batch_count):
        qkv_full, proj_full, in_full, out_full = (
            lax.all_gather(w_qkv, "dp", axis=0, tiled=True),
            lax.all_gather(w_proj, "dp", axis=1, tiled=True),
            lax.all_gather(w_in, "dp", axis=0, tiled=True),
            lax.all_gather(w_out, "dp", axis=0, tiled=True),
        )
        own_rows = tokens[batch_id].astype(jnp.float32)
        live_all = live_rows[batch_id]
        live_own = lax.dynamic_slice_in_dim(live_all, first_row, rows_dev, 0).astype(jnp.float32)
        normed_one = layer_norm(own_rows, gain_one, shift_one)
        sent_one = normed_one.astype(jnp.bfloat16)
        gathered_one = lax.all_gather(sent_one, "tensor", axis=0, tiled=True)
        mixed = jnp.einsum(
            "rd,dhc->rhc", gathered_one[:span_rows], qkv_full, preferred_element_type=jnp.float32
        )
        query = (
            (mixed[:, :, :head_width] * factor)
            .astype(jnp.bfloat16)
            .reshape(image_count, SEQ, heads_here, head_width)
        )
        keys_img = (
            mixed[:, :, head_width : 2 * head_width]
            .astype(jnp.bfloat16)
            .reshape(image_count, SEQ, heads_here, head_width)
        )
        values_img = (
            mixed[:, :, 2 * head_width :]
            .astype(jnp.bfloat16)
            .reshape(image_count, SEQ, heads_here, head_width)
        )
        scores = jnp.einsum("iqhc,ikhc->ihqk", query, keys_img, preferred_element_type=jnp.float32)
        peak = jnp.max(scores, axis=-1, keepdims=True)
        raised = jnp.exp(scores - peak)
        summed = jnp.sum(raised, axis=-1, keepdims=True)
        probs = raised / summed
        log_total = peak + jnp.log(summed)
        attn_weights = probs.astype(jnp.bfloat16)
        context = jnp.einsum(
            "ihqk,ikhc->iqhc", attn_weights, values_img, preferred_element_type=jnp.float32
        )
        context_b = context.astype(jnp.bfloat16).reshape(span_rows, flat_heads)
        context_full = jnp.concatenate(
            [context_b, jnp.zeros((tail_rows, flat_heads), jnp.bfloat16)], axis=0
        )
        proj_flat = proj_full.reshape(flat_heads, feature_dim)
        attn_own = lax.psum_scatter(
            jnp.dot(context_full, proj_flat, preferred_element_type=jnp.float32).astype(
                jnp.bfloat16
            ),
            "tensor",
            scatter_dimension=0,
            tiled=True,
        ).astype(jnp.float32)
        hidden = own_rows + live_own[:, None] * attn_own
        normed_two = layer_norm(hidden, gain_two, shift_two)
        sent_two = normed_two.astype(jnp.bfloat16)
        gathered_two = lax.all_gather(sent_two, "tensor", axis=0, tiled=True)
        logits = jnp.dot(gathered_two, router, preferred_element_type=jnp.float32)
        gate_probs = jax.nn.softmax(logits, axis=-1)
        picks = chosen[batch_id]
        keep_flag, flat_index, table = route_slots(
            picks, priority[batch_id, 0], live_all, expert_count, capacity
        )
        keep_wide = keep_flag.astype(jnp.float32)
        hits = (picks[:, :, None] == labels[None, None, :]).astype(jnp.float32)
        gates = jnp.sum(hits * gate_probs[:, None, :], axis=-1) * keep_wide
        padded_two = jnp.concatenate(
            [gathered_two, jnp.zeros((1, feature_dim), jnp.bfloat16)], axis=0
        )
        expert_in = padded_two[table].reshape(expert_count, capacity, feature_dim)
        pre = jnp.einsum("ecd,edf->ecf", expert_in, in_full, preferred_element_type=jnp.float32)
        active = tanh_gelu(pre).astype(jnp.bfloat16)
        expert_part = jnp.einsum(
            "ecf,efd->ecd", active, out_full, preferred_element_type=jnp.float32
        ).reshape(-1, feature_dim)
        padded_part = jnp.concatenate(
            [expert_part, jnp.zeros((1, feature_dim), jnp.float32)], axis=0
        )
        moe_own = lax.psum_scatter(
            (
                gates[:, 0:1] * padded_part[flat_index[:, 0]]
                + gates[:, 1:2] * padded_part[flat_index[:, 1]]
            ).astype(jnp.bfloat16),
            "tensor",
            scatter_dimension=0,
            tiled=True,
        ).astype(jnp.float32)
        results.append((hidden + moe_own).astype(jnp.bfloat16))
        qkv_full, proj_full, in_full, out_full = (
            lax.all_gather(w_qkv, "dp", axis=0, tiled=True),
            lax.all_gather(w_proj, "dp", axis=1, tiled=True),
            lax.all_gather(w_in, "dp", axis=0, tiled=True),
            lax.all_gather(w_out, "dp", axis=0, tiled=True),
        )
        proj_flat = proj_full.reshape(flat_heads, feature_dim)
        grad_rows = cotangent[batch_id].astype(jnp.float32)
        sent_grad = grad_rows.astype(jnp.bfloat16)
        grad_mix_full = lax.all_gather(sent_grad, "tensor", axis=0, tiled=True)
        padded_grad = jnp.concatenate(
            [grad_mix_full, jnp.zeros((1, feature_dim), jnp.bfloat16)], axis=0
        )
        gate_slots = (
            jnp.zeros((expert_count * capacity + 1,), jnp.float32)
            .at[flat_index.reshape(-1)]
            .set(gates.reshape(-1))
        )
        grad_expert = (
            gate_slots[: expert_count * capacity, None] * padded_grad[table].astype(jnp.float32)
        ).astype(jnp.bfloat16)
        grad_expert = grad_expert.reshape(expert_count, capacity, feature_dim)
        picked_part = padded_part[flat_index]
        grad_gate_part = jnp.einsum("rkd,rd->rk", picked_part, grad_mix_full.astype(jnp.float32))
        grad_active = jnp.einsum(
            "ecd,efd->ecf", grad_expert, out_full, preferred_element_type=jnp.float32
        )
        _, gelu_back = jax.vjp(tanh_gelu, pre)
        grad_pre = gelu_back(grad_active)[0].astype(jnp.bfloat16)
        acc_out = acc_out + jnp.einsum(
            "ecf,ecd->efd", active, grad_expert, preferred_element_type=jnp.float32
        )
        acc_in = acc_in + jnp.einsum(
            "ecd,ecf->edf", expert_in, grad_pre, preferred_element_type=jnp.float32
        )
        grad_slots = jnp.einsum(
            "ecf,edf->ecd", grad_pre, in_full, preferred_element_type=jnp.float32
        ).reshape(-1, feature_dim)
        grad_rows_part = (
            jnp.zeros((row_total + 1, feature_dim), jnp.float32)
            .at[table]
            .add(grad_slots)[:row_total]
        )
        grad_two_own, grad_gate_own = (
            lax.psum_scatter(
                grad_rows_part.astype(jnp.bfloat16), "tensor", scatter_dimension=0, tiled=True
            ).astype(jnp.float32),
            lax.psum_scatter(
                grad_gate_part.astype(jnp.bfloat16), "tensor", scatter_dimension=0, tiled=True
            ).astype(jnp.float32),
        )
        logits_own = jnp.dot(sent_two, router, preferred_element_type=jnp.float32)
        probs_own = jax.nn.softmax(logits_own, axis=-1)
        picks_own = lax.dynamic_slice_in_dim(picks, first_row, rows_dev, 0)
        keep_own = lax.dynamic_slice_in_dim(keep_wide, first_row, rows_dev, 0)
        hits_own = (picks_own[:, :, None] == labels[None, None, :]).astype(jnp.float32)
        grad_probs = jnp.sum(hits_own * (grad_gate_own * keep_own)[:, :, None], axis=1)
        grad_logits = probs_own * (
            grad_probs - jnp.sum(grad_probs * probs_own, axis=-1, keepdims=True)
        )
        acc_router = acc_router + jnp.dot(
            sent_two.astype(jnp.float32).T, grad_logits, precision=highest
        )
        grad_two_own = grad_two_own + jnp.dot(grad_logits, router_wide.T, precision=highest)
        _, back_two = jax.vjp(layer_norm, hidden, gain_two, shift_two)
        grad_hidden_norm, grad_gain_two, grad_shift_two = back_two(grad_two_own)
        grad_hidden = grad_rows + grad_hidden_norm
        acc_gain_two = acc_gain_two + grad_gain_two
        acc_shift_two = acc_shift_two + grad_shift_two
        grad_attn = (live_own[:, None] * grad_hidden).astype(jnp.bfloat16)
        grad_attn_full = lax.all_gather(grad_attn, "tensor", axis=0, tiled=True)
        grad_attn_span = grad_attn_full[:span_rows]
        acc_proj = acc_proj + jnp.dot(
            context_b.T, grad_attn_span, preferred_element_type=jnp.float32
        ).reshape(heads_here, head_width, feature_dim)
        grad_context = lax.dot_general(
            grad_attn_span, proj_flat, (((1,), (1,)), ((), ())), preferred_element_type=jnp.float32
        )
        grad_context = grad_context.astype(jnp.bfloat16).reshape(
            image_count, SEQ, heads_here, head_width
        )
        scores_again = jnp.einsum(
            "iqhc,ikhc->ihqk", query, keys_img, preferred_element_type=jnp.float32
        )
        probs_again = jnp.exp(scores_again - log_total)
        weights_again = probs_again.astype(jnp.bfloat16)
        grad_values = jnp.einsum(
            "ihqk,iqhc->ikhc", weights_again, grad_context, preferred_element_type=jnp.float32
        ).astype(jnp.bfloat16)
        grad_weights = jnp.einsum(
            "iqhc,ikhc->ihqk", grad_context, values_img, preferred_element_type=jnp.float32
        )
        grad_scores = (
            probs_again
            * (grad_weights - jnp.sum(grad_weights * probs_again, axis=-1, keepdims=True))
        ).astype(jnp.bfloat16)
        grad_query = jnp.einsum(
            "ihqk,ikhc->iqhc", grad_scores, keys_img, preferred_element_type=jnp.float32
        ).astype(jnp.bfloat16)
        grad_keys = jnp.einsum(
            "ihqk,iqhc->ikhc", grad_scores, query, preferred_element_type=jnp.float32
        ).astype(jnp.bfloat16)
        grad_mixed = jnp.concatenate(
            [grad_query * jnp.bfloat16(factor), grad_keys, grad_values], axis=-1
        )
        grad_mixed = grad_mixed.reshape(span_rows, heads_here, 3 * head_width)
        acc_qkv = acc_qkv + jnp.einsum(
            "rd,rhc->dhc", gathered_one[:span_rows], grad_mixed, preferred_element_type=jnp.float32
        )
        grad_one_span = jnp.einsum(
            "rhc,dhc->rd", grad_mixed, qkv_full, preferred_element_type=jnp.float32
        )
        grad_one_part = jnp.concatenate(
            [grad_one_span, jnp.zeros((tail_rows, feature_dim), jnp.float32)], axis=0
        )
        grad_one_own = lax.psum_scatter(
            grad_one_part.astype(jnp.bfloat16), "tensor", scatter_dimension=0, tiled=True
        ).astype(jnp.float32)
        _, back_one = jax.vjp(layer_norm, own_rows, gain_one, shift_one)
        grad_input_norm, grad_gain_one, grad_shift_one = back_one(grad_one_own)
        acc_gain_one = acc_gain_one + grad_gain_one
        acc_shift_one = acc_shift_one + grad_shift_one
        input_grads.append(grad_hidden + grad_input_norm)
    weight_grads = (
        lax.psum_scatter(
            acc_qkv.astype(jnp.bfloat16), "dp", scatter_dimension=0, tiled=True
        ).astype(jnp.float32),
        lax.psum_scatter(
            acc_proj.astype(jnp.bfloat16), "dp", scatter_dimension=1, tiled=True
        ).astype(jnp.float32),
        lax.psum_scatter(acc_in.astype(jnp.bfloat16), "dp", scatter_dimension=0, tiled=True).astype(
            jnp.float32
        ),
        lax.psum_scatter(
            acc_out.astype(jnp.bfloat16), "dp", scatter_dimension=0, tiled=True
        ).astype(jnp.float32),
    )
    small_grads = (
        lax.psum_scatter(acc_router, ("dp", "tensor"), scatter_dimension=0, tiled=True),
        lax.psum_scatter(acc_gain_one, ("dp", "tensor"), scatter_dimension=0, tiled=True),
        lax.psum_scatter(acc_shift_one, ("dp", "tensor"), scatter_dimension=0, tiled=True),
        lax.psum_scatter(acc_gain_two, ("dp", "tensor"), scatter_dimension=0, tiled=True),
        lax.psum_scatter(acc_shift_two, ("dp", "tensor"), scatter_dimension=0, tiled=True),
    )
    return (
        jnp.stack(results),
        jnp.stack(input_grads),
        weight_grads[0],
        weight_grads[1],
        weight_grads[2],
        weight_grads[3],
        small_grads[0],
        small_grads[1],
        small_grads[2],
        small_grads[3],
        small_grads[4],
    )


def solution(mesh):
    return jax.shard_map(
        local,
        mesh=mesh,
        in_specs=(
            P(None, ("dp", "tensor"), None),
            P("dp", "tensor", None),
            P("tensor", "dp", None),
            P("dp", None, "tensor"),
            P("dp", "tensor", None),
            P(("dp", "tensor"), None),
            P(("dp", "tensor")),
            P(("dp", "tensor")),
            P(("dp", "tensor")),
            P(("dp", "tensor")),
            P(None, "dp"),
            P(None, "dp", None),
            P(None, "dp", None),
            P(None, ("dp", "tensor"), None),
        ),
        out_specs=(
            P(None, ("dp", "tensor"), None),
            P(None, ("dp", "tensor"), None),
            P("dp", "tensor", None),
            P("tensor", "dp", None),
            P("dp", None, "tensor"),
            P("dp", "tensor", None),
            P(("dp", "tensor"), None),
            P(("dp", "tensor")),
            P(("dp", "tensor")),
            P(("dp", "tensor")),
            P(("dp", "tensor")),
        ),
        check_vma=False,
    )
```

profile of v0, /device:TPU:0, one launch (start us, length us, event | category | flops | bytes accessed | tf_op | source)
XLA Modules:
  0.0 1385.7 jit_solution(13148830530030804282)
XLA Ops:
  11.5 42.0 %all-reduce.25 = (bf16[512]{0:T(512)(128)(2,1)S(1)}, bf16[512]{0:T(512)(128)(2,1)S(1)}, bf16[512]{0:T(512)(128)(2,1)S(1)}, bf16[512]{0:T(512)(128)(2,1)S(1)}) all-reduce(bf16[512]{0:T(512)(128)(2,1)S(1)} %dynamic-update-slice.3, bf16[512]{0:T(512)(128)(2,1)S(1)} %dynamic-update-slice.2, ...), channel_id=1, replica_groups=mesh['dp'=16,'tensor'=2] {'dp','tensor'}, use_global_device_ids=true, to_apply=%add.18 | all-reduce | flops 2048 | bytes 8192
  57.6 21.7 %all_gather.87 = bf16[4,64,512]{2,0,1:T(4,128)(2,1)S(1)} all-gather(bf16[4,4,512]{2,0,1:T(4,128)(2,1)S(1)} %copy.558), channel_id=1, replica_groups=mesh['dp'=16,'tensor'=2] {'dp'}, dimensions={1}, use_global_device_ids=true | all-gather | bytes 278528 | tf_op jit(solution)/shard_map/all_gather | solution.py:112
  88.8 20.6 %all_gather.86 = bf16[512,4,192]{2,0,1:T(8,128)(2,1)S(1)} all-gather(bf16[32,4,192]{2,0,1:T(8,128)(2,1)S(1)} %copy.552), channel_id=1, replica_groups=mesh['dp'=16,'tensor'=2] {'dp'}, dimensions={0}, use_global_device_ids=true | all-gather | bytes 835584 | tf_op jit(solution)/shard_map/all_gather | solution.py:111
  215.0 67.8 %all_gather.91 = bf16[512,16]{1,0:T(8,128)(2,1)S(1)} all-gather(bf16[16,16]{1,0:T(8,128)(2,1)S(1)} %copy-done.166), channel_id=1, replica_groups=mesh['dp'=16,'tensor'=2] {'dp','tensor'}, dimensions={0}, use_global_device_ids=true | all-gather | bytes 16896 | tf_op jit(solution)/shard_map/all_gather | solution.py:90
  324.5 15.8 %all_gather.96 = bf16[512,512]{1,0:T(8,128)(2,1)S(1)} all-gather(bf16[256,512]{1,0:T(8,128)(2,1)} %get-tuple-element.169), channel_id=1, replica_groups=mesh['dp'=16,'tensor'=2] {'tensor'}, dimensions={0}, use_global_device_ids=true | all-gather | bytes 786432 | tf_op jit(solution)/shard_map/all_gather | solution.py:121
  355.5 14.0 %all-gather.8.cloned.1.call-done = bf16[16,1024,512]{2,1,0:T(8,128)(2,1)} async-done(((bf16[1,1024,512]{2,1,0:T(8,128)(2,1)}), bf16[16,1024,512]{2,1,0:T(8,128)(2,1)}) %all-gather.8.cloned.1.call-update) | async-done | bytes 16777232 | tf_op jit(solution)/shard_map/all_gather | solution.py:114
  416.7 11.1 fusion.6
  427.9 13.0 fusion.280
  467.2 14.2 %reduce-scatter.29.cloned.1.call-done = bf16[256,512]{1,0:T(8,128)(2,1)} async-done(((bf16[512,512]{1,0:T(8,128)(2,1)}), bf16[256,512]{1,0:T(8,128)(2,1)}) %reduce-scatter.29.cloned.1.call-update) | async-done | bytes 262160 | tf_op jit(solution)/shard_map/reduce_scatter | solution.py:188
  582.8 11.1 fusion.13
  593.9 12.9 fusion.281
  624.4 11.4 fusion.20
  635.7 13.0 fusion.282
  659.8 18.3 %fusion.55 = f32[16,1024,512]{2,1,0:T(8,128)} fusion(bf16[16,64,512]{2,1,0:T(8,128)(2,1)} %bitcast.591, f32[16,64]{1,0:T(8,128)S(1)} %mul.1015, f32[16,64,1024]{2,1,0:T(8,128)} %fusion.277), kind=kOutput, calls=%fused_computation.156 | convolution fusion | flops 1084751872 | bytes 38801408 | tf_op jit(solution)/shard_map/ecf,ecd->efd/dot_general | solution.py:227
  710.6 14.5 %reduce-scatter.33.cloned.1.call-done = bf16[256,512]{1,0:T(8,128)(2,1)} async-done(((bf16[512,512]{1,0:T(8,128)(2,1)}), bf16[256,512]{1,0:T(8,128)(2,1)}) %reduce-scatter.33.cloned.1.call-update) | async-done | bytes 262160 | tf_op jit(solution)/shard_map/reduce_scatter | solution.py:188
  790.5 16.1 %fusion.61 = f32[16,1024,512]{2,1,0:T(8,128)} fusion(bf16[16,64,512]{2,1,0:T(8,128)(2,1)S(1)} %bitcast.589, f32[16,64]{1,0:T(8,128)S(1)} %copy-done.119, f32[16,64,1024]{2,1,0:T(8,128)} %copy-done.4), kind=kOutput, calls=%fused_computation.158 | convolution fusion | flops 1084751872 | bytes 38801408 | tf_op jit(solution)/shard_map/ecf,ecd->efd/dot_general | solution.py:227
  812.2 30.5 %add_convert_fusion = bf16[16,1024,512]{2,1,0:T(8,128)(2,1)} fusion(f32[16,1024,512]{2,1,0:T(8,128)} %fusion.55, f32[16,1024,512]{2,1,0:T(8,128)} %fusion.61, bf16[16,64,512]{2,1,0:T(8,128)(2,1)S(1)} %bitcast.581, f32[16,64]{1,0:T(8,128)S(1)} %copy-done.106, f32[16,64,1024]{2,1,0:T(8,128)} %copy-done.1), kind=kOutput, calls=%fused_computation.36 | convolution fusion | flops 1109917696 | bytes 89133056 | tf_op jit(solution)/shard_map/ecf,ecd->efd/dot_general | solution.py:227
  844.7 13.2 fusion.283
  857.9 13.2 fusion.284
  871.1 32.3 %add_convert_fusion.1 = bf16[16,512,1024]{2,1,0:T(8,128)(2,1)} fusion(f32[16,512,1024]{2,1,0:T(8,128)} %fusion.283, f32[16,512,1024]{2,1,0:T(8,128)} %fusion.284, bf16[16,64,512]{2,1,0:T(8,128)(2,1)S(1)} %bitcast.572, bf16[16,64,1024]{2,1,0:T(8,128)(2,1)S(1)} %copy-done.12), kind=kOutput, calls=%fused_computation.37 | convolution fusion | flops 1098907648 | bytes 87031808 | tf_op jit(solution)/shard_map/ecd,ecf->edf/dot_general | solution.py:230
  916.5 43.1 %all-reduce.24 = (f32[512]{0:T(512)S(1)}, f32[512]{0:T(512)S(1)}, f32[512]{0:T(512)S(1)}, f32[512]{0:T(512)S(1)}) all-reduce(f32[512]{0:T(512)S(1)} %add_add_fusion.9, f32[512]{0:T(512)S(1)} %add_add_fusion.8, f32[512]{0:T(512)S(1)} %add_add_fusion.7, ...), channel_id=25, replica_groups=mesh['dp'=16,'tensor'=2] {'dp','tensor'}, use_global_device_ids=true, to_apply=%region_110.111.clone | all-reduce | flops 2048 | bytes 16384
  963.4 96.8 %reduce-scatter.55.cloned.1.call-done = bf16[1,1024,512]{2,1,0:T(8,128)(2,1)} async-done(((bf16[16,1024,512]{2,1,0:T(8,128)(2,1)}), bf16[1,1024,512]{2,1,0:T(8,128)(2,1)}) %reduce-scatter.55.cloned.1.call-update) | async-done | bytes 1048592 | tf_op jit(solution)/shard_map/reduce_scatter | solution.py:331
  1063.0 177.6 %reduce-scatter.53.cloned.1.call-done = bf16[1,512,1024]{2,1,0:T(8,128)(2,1)} async-done(((bf16[16,512,1024]{2,1,0:T(8,128)(2,1)}), bf16[1,512,1024]{2,1,0:T(8,128)(2,1)}) %reduce-scatter.53.cloned.1.call-update) | async-done | bytes 1048592 | tf_op jit(solution)/shard_map/reduce_scatter | solution.py:328
  1243.4 134.8 %reduce-scatter.57.cloned.1.call-done = f32[16,16]{1,0:T(8,128)} async-done(((f32[512,16]{1,0:T(8,128)}), f32[16,16]{1,0:T(8,128)}) %reduce-scatter.57.cloned.1.call-update) | async-done | bytes 1040 | tf_op jit(solution)/shard_map/reduce_scatter | solution.py:336
  (806 shorter events, 506.9 us)
Async XLA Ops:
  8.0 280.3 %reduce-scatter.27.cloned.1.call-start = ((), (), s32[]{:S(2)}) async-start(), calls=%async_computation.19 | async-start | bytes 786432 | tf_op jit(solution)/shard_map/reduce_scatter | solution.py:155
  53.5 237.9 %copy-start.110 = (f32[512]{0:T(512)}, f32[512]{0:T(512)S(1)}, u32[]{:S(2)}) copy-start(f32[512]{0:T(512)S(1)} %convert_element_type.410) | copy-start | bytes 6148
  79.4 260.9 %copy-start.40 = (bf16[4,64,512]{2,1,0:T(8,128)(2,1)}, bf16[4,64,512]{2,1,0:T(8,128)(2,1)S(1)}, u32[]{:S(2)}) copy-start(bf16[4,64,512]{2,1,0:T(8,128)(2,1)S(1)} %copy.559) | copy-start | bytes 786436
  116.4 228.4 %all-gather.6.cloned.1.call-start = ((), (), s32[]{:S(2)}) async-start(), calls=%async_computation.20 | async-start | bytes 17825792 | tf_op jit(solution)/shard_map/all_gather | solution.py:113
  116.9 252.6 %all-gather.8.cloned.1.call-start = ((), (), s32[]{:S(2)}) async-start(), calls=%async_computation.21 | async-start | bytes 17825792 | tf_op jit(solution)/shard_map/all_gather | solution.py:114
  117.5 342.9 %reduce-scatter.59.cloned.1.call-start = ((), (), s32[]{:S(2)}) async-start(), calls=%async_computation.37 | async-start | bytes 196608
  392.7 68.7 %reduce-scatter.31.cloned.1.call-start = ((), (), s32[]{:S(2)}) async-start(), calls=%async_computation.23 | async-start | bytes 786432 | tf_op jit(solution)/shard_map/reduce_scatter | solution.py:155
  396.5 65.0 %reduce-scatter.35.cloned.1.call-start = ((), (), s32[]{:S(2)}) async-start(), calls=%async_computation.25 | async-start | bytes 786432 | tf_op jit(solution)/shard_map/reduce_scatter | solution.py:155
  416.5 48.1 %reduce-scatter.39.cloned.1.call-start = ((), (), s32[]{:S(2)}) async-start(), calls=%async_computation.27 | async-start | bytes 786432 | tf_op jit(solution)/shard_map/reduce_scatter | solution.py:242
  451.4 30.0 %reduce-scatter.29.cloned.1.call-start = ((), (), s32[]{:S(2)}) async-start(), calls=%async_computation.22 | async-start | bytes 786432 | tf_op jit(solution)/shard_map/reduce_scatter | solution.py:188
  459.9 235.1 %reduce-scatter.63.cloned.1.call-start = ((), (), s32[]{:S(2)}) async-start(), calls=%async_computation.39 | async-start | bytes 196608
  541.4 154.7 %reduce-scatter.61.cloned.1.call-start = ((), (), s32[]{:S(2)}) async-start(), calls=%async_computation.38 | async-start | bytes 196608
  582.5 114.6 %reduce-scatter.43.cloned.1.call-start = ((), (), s32[]{:S(2)}) async-start(), calls=%async_computation.29 | async-start | bytes 786432 | tf_op jit(solution)/shard_map/reduce_scatter | solution.py:242
  623.9 74.8 %reduce-scatter.47.cloned.1.call-start = ((), (), s32[]{:S(2)}) async-start(), calls=%async_computation.31 | async-start | bytes 786432 | tf_op jit(solution)/shard_map/reduce_scatter | solution.py:242
  659.6 48.7 %reduce-scatter.37.cloned.1.call-start = ((), (), s32[]{:S(2)}) async-start(), calls=%async_computation.26 | async-start | bytes 786432 | tf_op jit(solution)/shard_map/reduce_scatter | solution.py:188
  693.6 31.5 %reduce-scatter.33.cloned.1.call-start = ((), (), s32[]{:S(2)}) async-start(), calls=%async_computation.24 | async-start | bytes 786432 | tf_op jit(solution)/shard_map/reduce_scatter | solution.py:188
  695.0 213.9 %all-reduce.28.cloned.1.call-start = ((), (), s32[]{:S(2)}) async-start(), calls=%async_computation.40 | async-start | bytes 524288
  761.4 148.8 %reduce-scatter.49.cloned.1.call-start = ((), (), s32[]{:S(2)}) async-start(), calls=%async_computation.32 | async-start | bytes 786432 | tf_op jit(solution)/shard_map/reduce_scatter | solution.py:313
  769.3 141.0 %reduce-scatter.41.cloned.1.call-start = ((), (), s32[]{:S(2)}) async-start(), calls=%async_computation.28 | async-start | bytes 786432 | tf_op jit(solution)/shard_map/reduce_scatter | solution.py:313
  780.9 129.4 %reduce-scatter.45.cloned.1.call-start = ((), (), s32[]{:S(2)}) async-start(), calls=%async_computation.30 | async-start | bytes 786432 | tf_op jit(solution)/shard_map/reduce_scatter | solution.py:313
  790.4 171.5 %reduce-scatter.51.cloned.1.call-start = ((), (), s32[]{:S(2)}) async-start(), calls=%async_computation.33 | async-start | bytes 1114112 | tf_op jit(solution)/shard_map/reduce_scatter | solution.py:322
  811.0 249.2 %reduce-scatter.55.cloned.1.call-start = ((), (), s32[]{:S(2)}) async-start(), calls=%async_computation.35 | async-start | bytes 17825792 | tf_op jit(solution)/shard_map/reduce_scatter | solution.py:331
  842.8 397.9 %reduce-scatter.53.cloned.1.call-start = ((), (), s32[]{:S(2)}) async-start(), calls=%async_computation.34 | async-start | bytes 17825792 | tf_op jit(solution)/shard_map/reduce_scatter | solution.py:328
  903.7 474.5 %reduce-scatter.57.cloned.1.call-start = ((), (), s32[]{:S(2)}) async-start(), calls=%async_computation.36 | async-start | bytes 270336 | tf_op jit(solution)/shard_map/reduce_scatter | solution.py:336
  (173 other events, 2020.3 us)
Sparse Core Ops, SparseCore 0:
  116.5 12.0 reduce-scatter.26
  392.8 8.5 reduce-scatter.58
  404.2 14.6 reduce-scatter.30
  421.0 14.6 reduce-scatter.34
  451.5 13.0 reduce-scatter.38
  466.7 14.6 reduce-scatter.28
  541.6 10.3 reduce-scatter.62
  582.6 10.3 reduce-scatter.60
  624.0 14.8 reduce-scatter.42
  659.7 14.5 reduce-scatter.46
  693.7 14.5 reduce-scatter.36
  710.4 14.6 reduce-scatter.32
  769.4 14.6 reduce-scatter.48
  786.2 14.6 reduce-scatter.40
  803.0 14.6 reduce-scatter.44
  821.1 57.6 reduce-scatter.50
  882.7 177.4 reduce-scatter.54
  1064.2 176.4 reduce-scatter.52
  1243.4 134.7 reduce-scatter.56
Sparse Core Ops, SparseCore 1:
  119.0 123.9 all-gather.5
  245.0 124.4 all-gather.7
  761.5 90.1 all-reduce.27
where the time goes:
time: 1400 us; the launch traced here: 1390 us
  waiting for transfers between devices  463 us (33%)
  matrix products  316 us (23%)
  blocking collectives  300 us (21%)
  local copies, waits for them, and re-layouts  200 us (14%)
  other arithmetic  85.1 us (6%)
  between operations  19.8 us (1%)
    reduce_scatter x1, waiting for transfers between devices, local(): lax.psum_scatter(acc_in.astype(jnp.bfloat16), 'dp', scatter_dimension=0,...  178 us
    reduce_scatter x1, waiting for transfers between devices, local(): lax.psum_scatter(acc_router, ('dp', 'tensor'), scatter_dimension=0, tiled...  135 us
    reduce_scatter x1, waiting for transfers between devices, local(): lax.psum_scatter(acc_out.astype(jnp.bfloat16), 'dp', scatter_dimension=0,...  96.8 us
    unnamed x2, blocking collectives  85 us
    all_gather x1, blocking collectives, local(): lax.all_gather(w_router, ('dp', 'tensor'), axis=0, tiled=True)  67.8 us
    dot_general x3, matrix products, local(): jnp.einsum('ecf,ecd->efd', active, grad_expert, preferred_element_type=jn...  64.9 us
    dot_general x3, matrix products, local(): jnp.einsum('ecd,ecf->edf', expert_in, grad_pre, preferred_element_type=jn...  58.7 us
    dot_general x3, matrix products, local(): jnp.einsum('ecf,edf->ecd', grad_pre, in_full, preferred_element_type=jnp....  38.9 us
  transfers between devices with their start and end apart: 22, of which 8 were waited for; matrix products, arithmetic and copies ran while one was open for 36% of the time, Pallas kernels for 0%

commit v1 on v0

v1 whole, which is shorter than its diff:
```python
import functools

import jax
import jax.numpy as jnp
from jax import lax
from jax.experimental import pallas as pl
from jax.experimental.pallas import tpu as pltpu
from jax.sharding import PartitionSpec as P

SEQ = 197
EPS = 1e-06
F32 = jnp.float32
BF16 = jnp.bfloat16
GELU_A = 0.7978845608028654
GELU_B = 0.044715


def dot(a, b, dims):
    return lax.dot_general(a, b, (dims, ((), ())), preferred_element_type=F32)


def layer_norm(values, gain_vec, shift_vec):
    centre = jnp.mean(values, axis=-1, keepdims=True)
    centered = values - centre
    spread = jnp.mean(centered * centered, axis=-1, keepdims=True)
    return centered * lax.rsqrt(spread + EPS) * gain_vec + shift_vec


def expert_kernel(x_ref, dp_ref, win_ref, wout_ref, y_ref, dx_ref, gin_ref, gout_ref, y_acc, dx_acc):
    step = pl.program_id(0)
    last = pl.num_programs(0) - 1
    x = x_ref[...]
    dprod = dp_ref[...]
    win = win_ref[...]
    wout = wout_ref[...]
    pre = dot(x, win, ((1,), (0,)))
    square = pre * pre
    th = jnp.tanh(GELU_A * pre * (1.0 + GELU_B * square))
    active = (0.5 * pre * (1.0 + th)).astype(BF16)
    slope = 0.5 * (1.0 + th) + 0.5 * pre * (1.0 - th * th) * (GELU_A * (1.0 + 3.0 * GELU_B * square))
    dact = dot(dprod, wout, ((1,), (1,)))
    dpre = (dact * slope).astype(BF16)
    gin_ref[...] = dot(x, dpre, ((0,), (0,))).astype(BF16)
    gout_ref[...] = dot(active, dprod, ((0,), (0,))).astype(BF16)
    part_y = dot(active, wout, ((1,), (0,)))
    part_dx = dot(dpre, win, ((1,), (1,)))

    @pl.when(step == 0)
    def _():
        y_acc[...] = part_y
        dx_acc[...] = part_dx

    @pl.when(step > 0)
    def _():
        y_acc[...] += part_y
        dx_acc[...] += part_dx

    @pl.when(step == last)
    def _():
        y_ref[...] = y_acc[...].astype(BF16)
        dx_ref[...] = dx_acc[...].astype(BF16)


def expert(x, dprod, win, wout, tile=256):
    n, d = x.shape
    ff = win.shape[1]
    return pl.pallas_call(
        expert_kernel,
        grid=(ff // tile,),
        in_specs=[
            pl.BlockSpec((n, d), lambda i: (0, 0)),
            pl.BlockSpec((n, d), lambda i: (0, 0)),
            pl.BlockSpec((d, tile), lambda i: (0, i)),
            pl.BlockSpec((tile, d), lambda i: (i, 0)),
        ],
        out_specs=[
            pl.BlockSpec((n, d), lambda i: (0, 0)),
            pl.BlockSpec((n, d), lambda i: (0, 0)),
            pl.BlockSpec((d, tile), lambda i: (0, i)),
            pl.BlockSpec((tile, d), lambda i: (i, 0)),
        ],
        out_shape=[
            jax.ShapeDtypeStruct((n, d), BF16),
            jax.ShapeDtypeStruct((n, d), BF16),
            jax.ShapeDtypeStruct((d, ff), BF16),
            jax.ShapeDtypeStruct((ff, d), BF16),
        ],
        scratch_shapes=[pltpu.VMEM((n, d), F32), pltpu.VMEM((n, d), F32)],
        compiler_params=pltpu.CompilerParams(vmem_limit_bytes=60 * 1024 * 1024),
        cost_estimate=pl.CostEstimate(
            flops=12 * n * d * ff, transcendentals=n * ff, bytes_accessed=8 * n * d + 8 * d * ff
        ),
    )(x, dprod, win, wout)


def local(
    tokens,
    w_qkv,
    w_proj,
    w_in,
    w_out,
    w_router,
    gain_attn,
    shift_attn,
    gain_moe,
    shift_moe,
    live_rows,
    chosen,
    priority,
    cotangent,
):
    batches, own_rows, d = tokens.shape
    rows = live_rows.shape[1]
    n_dp = lax.axis_size("dp")
    n_t = lax.axis_size("tensor")
    t = lax.axis_index("tensor")
    heads_here = w_qkv.shape[1]
    heads = heads_here * n_t
    width = w_qkv.shape[2] // 3
    experts = w_in.shape[0] * n_dp
    cap = 2 * rows // experts
    share = cap // n_t
    images = rows // SEQ
    span = images * SEQ
    per = -(-images // n_t)
    work = per * SEQ
    total = n_t * work
    factor = width ** (-0.5)
    highest = lax.Precision.HIGHEST

    small = jnp.concatenate(
        [w_router] + [v[:, None] for v in (gain_attn, shift_attn, gain_moe, shift_moe)], axis=1
    )
    small = lax.all_gather(small, ("dp", "tensor"), axis=0, tiled=True)
    router = small[:, :experts]
    gain_one, shift_one, gain_two, shift_two = (small[:, experts + i].astype(F32) for i in range(4))
    qkv = lax.all_gather(w_qkv.reshape(-1, 128), ("dp", "tensor"), axis=0, tiled=False)
    qkv = qkv.reshape(n_dp, n_t, w_qkv.shape[0], heads_here, 3, width)
    qkv = qkv.transpose(0, 2, 4, 1, 3, 5).reshape(d, 3 * heads * width)
    proj = lax.all_gather(w_proj.reshape(-1, 128), ("dp", "tensor"), axis=0, tiled=False)
    proj = proj.reshape(n_dp, n_t, heads_here, w_proj.shape[1], d)
    proj = proj.transpose(1, 2, 0, 3, 4).reshape(heads * width, d)
    win = lax.all_gather(w_in[0], "tensor", axis=1, tiled=True)
    wout = lax.all_gather(w_out[0], "tensor", axis=0, tiled=True)
    cot_all = lax.all_gather(cotangent, "tensor", axis=1, tiled=True)

    def pad_rows(v, n):
        return jnp.pad(v, ((0, 0), (0, n - v.shape[1])) + ((0, 0),) * (v.ndim - 2))

    def own(v):
        return lax.dynamic_slice_in_dim(v, t * work, work, 1)

    edge = own_rows - work
    direct = n_t == 2 and per == 1 and edge >= 0
    if direct:
        moved = lax.ppermute(tokens[:, work:], "tensor", [(0, 1)])
        x = jnp.where(
            t == 0, tokens[:, :work], jnp.concatenate([moved, tokens[:, : work - edge]], axis=1)
        )
    else:
        x = own(pad_rows(lax.all_gather(tokens, "tensor", axis=1, tiled=True)[:, :span], total))
    x = x.astype(F32)
    live = live_rows[:, :span]
    live_all = pad_rows(live, total)
    live_own = own(live_all).astype(F32)[:, :, None]
    cot_all = pad_rows(cot_all[:, :span], total)
    dy = own(cot_all).astype(F32)

    rank = priority[:, 0, :span]
    first, second = chosen[:, :span, 0], chosen[:, :span, 1]
    labels = jnp.arange(experts, dtype=jnp.int32)
    earlier = (rank[:, None, :] < rank[:, :, None]).astype(BF16)
    hit_one = (first[:, :, None] == labels).astype(F32)
    hit_two = (second[:, :, None] == labels).astype(F32)
    live_one = hit_one * live[:, :, None].astype(F32)
    live_two = hit_two * live[:, :, None].astype(F32)
    counts = jnp.einsum(
        "mrs,mse->mre",
        earlier,
        jnp.concatenate([live_one, live_two], axis=-1).astype(BF16),
        preferred_element_type=F32,
    )
    first_total = jnp.sum(live_one, axis=1, keepdims=True)
    slot_one = jnp.sum(counts[:, :, :experts] * hit_one, axis=-1).astype(jnp.int32)
    slot_two = jnp.sum((counts[:, :, experts:] + first_total) * hit_two, axis=-1).astype(jnp.int32)
    keep_one = (live > 0) & (slot_one < cap)
    keep_two = (live > 0) & (slot_two < cap)
    flat_one = jnp.where(keep_one, first * cap + slot_one, -1)
    flat_two = jnp.where(keep_two, second * cap + slot_two, -1)

    def spread(v, fill):
        return jnp.pad(v, ((0, 0), (0, total - span)), constant_values=fill)

    flat_one, flat_two = spread(flat_one, -1), spread(flat_two, -1)
    keep_one, keep_two = spread(keep_one, False), spread(keep_two, False)
    first, second = spread(first, 0), spread(second, 0)
    codes = (jnp.arange(experts)[:, None] * cap + t * share + jnp.arange(share)[None, :]).reshape(-1)
    pick_one = flat_one[:, None, :] == codes[None, :, None]
    pick_two = flat_two[:, None, :] == codes[None, :, None]

    normed_one = layer_norm(x, gain_one, shift_one).astype(BF16)
    mixed = dot(normed_one, qkv, ((2,), (0,)))
    split = heads * width
    shape = (batches * per, SEQ, heads, width)
    query = (mixed[..., :split] * factor).astype(BF16).reshape(shape)
    keys = mixed[..., split : 2 * split].astype(BF16).reshape(shape)
    values = mixed[..., 2 * split :].astype(BF16).reshape(shape)
    scores = jnp.einsum("iqhc,ikhc->ihqk", query, keys, preferred_element_type=F32)
    probs = jax.nn.softmax(scores, axis=-1)
    weights = probs.astype(BF16)
    context = jnp.einsum("ihqk,ikhc->iqhc", weights, values, preferred_element_type=F32)
    context = context.astype(BF16).reshape(batches, work, split)
    attn = dot(context, proj, ((2,), (0,)))
    hidden = x + live_own * attn
    normed_two = layer_norm(hidden, gain_two, shift_two).astype(BF16)

    c_all = lax.all_gather(normed_two, "tensor", axis=1, tiled=True)
    gate_probs = jax.nn.softmax(dot(c_all, router, ((2,), (0,))), axis=-1)
    hits_one = (first[:, :, None] == labels).astype(F32)
    hits_two = (second[:, :, None] == labels).astype(F32)
    gate_one = jnp.sum(gate_probs * hits_one, axis=-1) * keep_one
    gate_two = jnp.sum(gate_probs * hits_two, axis=-1) * keep_two
    picked = (pick_one | pick_two).astype(BF16)
    sent = jnp.einsum(
        "mqr,mrd->mqd",
        picked,
        jnp.concatenate([c_all, cot_all], axis=-1),
        preferred_element_type=F32,
    )
    gate_slot = jnp.sum(
        jnp.where(pick_one, gate_one[:, None, :], 0.0) + jnp.where(pick_two, gate_two[:, None, :], 0.0),
        axis=-1,
        keepdims=True,
    )
    sent = jnp.concatenate(
        [sent[..., :d].astype(BF16), (sent[..., d:] * gate_slot).astype(BF16)], axis=-1
    )
    sent = sent.reshape(batches, experts, share, 2 * d)
    got = lax.all_to_all(sent, "dp", 1, 1, tiled=True).reshape(-1, 2 * d)
    produced, d_in, grad_in, grad_out = expert(got[:, :d], got[:, d:], win, wout)
    back = jnp.concatenate([produced, d_in], axis=-1).reshape(batches, n_dp, share, 2 * d)
    back = lax.all_to_all(back, "dp", 1, 1, tiled=True).reshape(batches, experts * share, 2 * d)
    grad_in = lax.psum_scatter(grad_in, "tensor", scatter_dimension=1, tiled=True).astype(F32)
    grad_out = lax.psum_scatter(grad_out, "tensor", scatter_dimension=0, tiled=True).astype(F32)

    part_one = jnp.einsum("mqr,mqd->mrd", pick_one.astype(BF16), back[..., :d], preferred_element_type=F32)
    part_two = jnp.einsum("mqr,mqd->mrd", pick_two.astype(BF16), back[..., :d], preferred_element_type=F32)
    d_rows = jnp.einsum("mqr,mqd->mrd", picked, back[..., d:], preferred_element_type=F32)
    mixture = gate_one[:, :, None] * part_one + gate_two[:, :, None] * part_two
    cot_wide = cot_all.astype(F32)
    dgate_one = jnp.sum(part_one * cot_wide, axis=-1, keepdims=True)
    dgate_two = jnp.sum(part_two * cot_wide, axis=-1, keepdims=True)
    dgates = jnp.concatenate([dgate_one, dgate_two], axis=-1)
    payload = jnp.concatenate(
        [mixture, d_rows, jnp.pad(dgates, ((0, 0), (0, 0), (0, 126)))], axis=-1
    ).astype(BF16)
    payload = lax.psum_scatter(payload, "tensor", scatter_dimension=1, tiled=True).astype(F32)
    output = (hidden + payload[..., :d]).astype(BF16)
    dgates = payload[..., 2 * d : 2 * d + 2]

    own_probs = own(gate_probs)
    dprobs = own(hits_one) * dgates[..., 0:1] * own(keep_one)[:, :, None]
    dprobs = dprobs + own(hits_two) * dgates[..., 1:2] * own(keep_two)[:, :, None]
    dlogits = own_probs * (dprobs - jnp.sum(dprobs * own_probs, axis=-1, keepdims=True))
    grad_router = lax.dot_general(
        normed_two.astype(F32), dlogits, (((0, 1), (0, 1)), ((), ())), precision=highest
    )
    dc = payload[..., d : 2 * d] + lax.dot_general(
        dlogits, router.astype(F32), (((2,), (1,)), ((), ())), precision=highest
    )
    _, back_two = jax.vjp(layer_norm, hidden, gain_two, shift_two)
    dnorm, grad_gain_two, grad_shift_two = back_two(dc)
    dhidden = dy + dnorm
    dattn = (live_own * dhidden).astype(BF16)

    grad_proj = dot(context, dattn, ((0, 1), (0, 1)))
    dcontext = dot(dattn, proj, ((2,), (1,))).astype(BF16).reshape(shape)
    dvalues = jnp.einsum("ihqk,iqhc->ikhc", weights, dcontext, preferred_element_type=F32).astype(BF16)
    dweights = jnp.einsum("iqhc,ikhc->ihqk", dcontext, values, preferred_element_type=F32)
    dscores = (probs * (dweights - jnp.sum(dweights * probs, axis=-1, keepdims=True))).astype(BF16)
    dquery = jnp.einsum("ihqk,ikhc->iqhc", dscores, keys, preferred_element_type=F32).astype(BF16)
    dkeys = jnp.einsum("ihqk,iqhc->ikhc", dscores, query, preferred_element_type=F32).astype(BF16)
    dmixed = jnp.concatenate(
        [v.reshape(batches, work, split) for v in (dquery * BF16(factor), dkeys, dvalues)], axis=-1
    )
    grad_qkv = dot(normed_one, dmixed, ((0, 1), (0, 1)))
    da = dot(dmixed, qkv, ((2,), (1,)))
    _, back_one = jax.vjp(layer_norm, x, gain_one, shift_one)
    dnorm, grad_gain_one, grad_shift_one = back_one(da)
    grad_x = dhidden + dnorm

    if direct:
        out_edge = lax.ppermute(output[:, :edge], "tensor", [(1, 0)])
        grad_edge = lax.ppermute(grad_x[:, :edge], "tensor", [(1, 0)])
        result = jnp.where(
            t == 0,
            jnp.concatenate([output, out_edge], axis=1),
            jnp.concatenate([output[:, edge:], tokens[:, work - edge :]], axis=1),
        )
        grad_tokens = jnp.where(
            t == 0,
            jnp.concatenate([grad_x, grad_edge], axis=1),
            jnp.concatenate([grad_x[:, edge:], cotangent[:, work - edge :].astype(F32)], axis=1),
        )
    else:
        here = (t * own_rows + jnp.arange(own_rows) < span)[None, :, None]

        def home(v, rest):
            full = pad_rows(lax.all_gather(v, "tensor", axis=1, tiled=True)[:, :span], rows)
            return jnp.where(here, lax.dynamic_slice_in_dim(full, t * own_rows, own_rows, 1), rest)

        result = home(output, tokens)
        grad_tokens = home(grad_x, cotangent.astype(F32))

    grad_qkv = grad_qkv.astype(BF16).reshape(n_dp, -1, 3, n_t, heads_here, width)
    grad_qkv = grad_qkv.transpose(0, 3, 1, 4, 2, 5).reshape(n_dp * n_t * w_qkv.shape[0], heads_here * 3 * width)
    grad_qkv = lax.psum_scatter(grad_qkv, ("dp", "tensor"), scatter_dimension=0, tiled=True)
    grad_proj = grad_proj.astype(BF16).reshape(n_t, heads_here, n_dp, -1, d)
    grad_proj = grad_proj.transpose(2, 0, 1, 3, 4).reshape(-1, d)
    grad_proj = lax.psum_scatter(grad_proj, ("dp", "tensor"), scatter_dimension=0, tiled=True)
    smalls = jnp.concatenate(
        [grad_router] + [v[:, None] for v in (grad_gain_one, grad_shift_one, grad_gain_two, grad_shift_two)],
        axis=1,
    )
    smalls = lax.psum_scatter(smalls, ("dp", "tensor"), scatter_dimension=0, tiled=True)
    return (
        result,
        grad_tokens,
        grad_qkv.astype(F32).reshape(w_qkv.shape),
        grad_proj.astype(F32).reshape(w_proj.shape),
        grad_in[None],
        grad_out[None],
        smalls[:, :experts],
        smalls[:, experts],
        smalls[:, experts + 1],
        smalls[:, experts + 2],
        smalls[:, experts + 3],
    )


def solution(mesh):
    both = ("dp", "tensor")
    return jax.shard_map(
        local,
        mesh=mesh,
        in_specs=(
            P(None, both, None),
            P("dp", "tensor", None),
            P("tensor", "dp", None),
            P("dp", None, "tensor"),
            P("dp", "tensor", None),
            P(both, None),
            P(both),
            P(both),
            P(both),
            P(both),
            P(None, "dp"),
            P(None, "dp", None),
            P(None, "dp", None),
            P(None, both, None),
        ),
        out_specs=(
            P(None, both, None),
            P(None, both, None),
            P("dp", "tensor", None),
            P("tensor", "dp", None),
            P("dp", None, "tensor"),
            P("dp", "tensor", None),
            P(both, None),
            P(both),
            P(both),
            P(both),
            P(both),
        ),
        check_vma=False,
    )
```

time: 1400 us -> 964 us (0.69)
  matrix products: 316 us -> 43.8 us
  local copies, waits for them, and re-layouts: 200 us -> 84.6 us
  blocking collectives: 300 us -> 212 us
  waiting for transfers between devices: 463 us -> 518 us
  other arithmetic: 85.1 us -> 35.3 us
  Pallas kernels: 0 us -> 35.3 us
    dot_general x69 -> x18, matrix products: 316 us -> 39.4 us  [the longest x6 11.4 us: dot(): return lax.dot_general(a, b, (dims, ((), ())), preferred_element_type=F32)]
    reduce_scatter x16 -> x4, waiting for transfers between devices: 447 us -> 224 us  [the longest x1 126 us: local(): lax.psum_scatter(grad_proj, ('dp', 'tensor'), scatter_dimension=0, tiled=...]
    unnamed x26 -> x13, waiting for transfers between devices: 1.44 us -> 208 us
    gather x33 -> x0, local copies, waits for them, and re-layouts: 85.8 us -> none  [the longest x6 22.9 us: local(): picked_part = padded_part[flat_index]]
    unnamed x2 -> x0, blocking collectives: 85 us -> none
    all_gather x15 -> x2, blocking collectives: 215 us -> 134 us  [the longest x1 69.7 us: local(): lax.all_gather(w_proj.reshape(-1, 128), ('dp', 'tensor'), axis=0, tiled=F...]
    all_to_all x0 -> x1, blocking collectives: none -> 78.5 us  [local(): lax.all_to_all(back, 'dp', 1, 1, tiled=True)]
    all_to_all x0 -> x1, waiting for transfers between devices: none -> 58.1 us  [local(): got = lax.all_to_all(sent, 'dp', 1, 1, tiled=True).reshape(-1, 2 * d)]
  transfers between devices with their start and end apart: 22 -> 15, of which waited for: 8 -> 7; matrix products, arithmetic and copies ran while one was open for 36% -> 13% of each run, Pallas kernels for 0% -> 0%
where the time goes in v1:
time: 964 us; the launch traced here: 959 us
  waiting for transfers between devices  518 us (54%)
  blocking collectives  212 us (22%)
  local copies, waits for them, and re-layouts  84.6 us (9%)
  matrix products  43.8 us (5%)
  other arithmetic  35.3 us (4%)
  Pallas kernels  35.3 us (4%)
  between operations  15.8 us (2%)
  starting transfers between devices  14 us (1%)
    unnamed x13, waiting for transfers between devices  208 us
    reduce_scatter x1, waiting for transfers between devices, local(): lax.psum_scatter(grad_proj, ('dp', 'tensor'), scatter_dimension=0, tiled=...  126 us
    reduce_scatter x1, waiting for transfers between devices, local(): lax.psum_scatter(grad_qkv, ('dp', 'tensor'), scatter_dimension=0, tiled=T...  97.9 us
    all_to_all x1, blocking collectives, local(): lax.all_to_all(back, 'dp', 1, 1, tiled=True)  78.5 us
    all_gather x1, blocking collectives, local(): lax.all_gather(w_proj.reshape(-1, 128), ('dp', 'tensor'), axis=0, tiled=F...  69.7 us
    all_gather x1, blocking collectives, local(): small = lax.all_gather(small, ('dp', 'tensor'), axis=0, tiled=True)  64.2 us
    all_to_all x1, waiting for transfers between devices, local(): got = lax.all_to_all(sent, 'dp', 1, 1, tiled=True).reshape(-1, 2 * d)  58.1 us
    pallas_call x1, Pallas kernels, expert(): pl.pallas_call(expert_kernel, grid=(ff // tile,), in_specs=[pl.BlockSpec(...  35.3 us
  transfers between devices with their start and end apart: 15, of which 7 were waited for; matrix products, arithmetic and copies ran while one was open for 13% of the time, Pallas kernels for 0%

profile of v1, /device:TPU:0, one launch (start us, length us, event | category | flops | bytes accessed | tf_op | source)
XLA Modules:
  0.0 959.4 jit_solution(3320138925285863355)
XLA Ops:
  9.9 4.9 collective-permute-start
  16.9 69.7 %all_gather.23 = bf16[32,64,128]{2,1,0:T(8,128)(2,1)S(1)} all-gather(bf16[1,64,128]{2,1,0:T(8,128)(2,1)S(1)} %all_gather_reshape.7), channel_id=1, replica_groups=mesh['dp'=16,'tensor'=2] {'dp','tensor'}, dimensions={0}, use_global_device_ids=true | all-gather | bytes 540672 | tf_op jit(solution)/shard_map/all_gather | solution.py:140
  89.1 64.2 %all_gather.21 = bf16[512,20]{1,0:T(8,128)(2,1)S(1)} all-gather(bf16[16,20]{1,0:T(8,128)(2,1)S(1)} %concatenate.46), channel_id=1, replica_groups=mesh['dp'=16,'tensor'=2] {'dp','tensor'}, dimensions={0}, use_global_device_ids=true | all-gather | bytes 21120 | tf_op jit(solution)/shard_map/all_gather | solution.py:134
  155.0 8.9 reshape.229
  163.9 5.6 copy.139
  169.4 5.1 reshape.265
  181.2 3.8 fusion.96
  195.3 22.3 %all-gather.10.cloned.1.call-done = bf16[3,394,512]{2,0,1:T(4,128)(2,1)} async-done(((bf16[3,197,512]{2,0,1:T(4,128)(2,1)}), bf16[3,394,512]{2,0,1:T(4,128)(2,1)}) %all-gather.10.cloned.1.call-update) | async-done | bytes 1210384 | tf_op jit(solution)/shard_map/all_gather | solution.py:217
  221.5 3.8 fusion.13
  229.5 5.7 all-to-all-start
  236.4 58.1 %all-to-all-done = bf16[3,16,32,1024]{3,2,0,1:T(8,128)(2,1)} async-done(((bf16[3,16,32,1024]{3,2,0,1:T(8,128)(2,1)}), bf16[3,16,32,1024]{3,2,0,1:T(8,128)(2,1)}, u32[]{:S(2)}, u32[]{:S(2)}) %all-to-all-start) | async-done | bytes 3145760 | tf_op jit(solution)/shard_map/all_to_all | solution.py:239
  298.9 6.4 all-gather.16.cloned.1.call-done
  305.2 35.3 %shard_map.221 = (bf16[1536,512]{1,0:T(8,128)(2,1)}, bf16[1536,512]{1,0:T(8,128)(2,1)}, bf16[512,2048]{1,0:T(8,128)(2,1)}, bf16[2048,512]{1,0:T(8,128)(2,1)}) custom-call(bf16[1536,512]{1,0:T(8,128)(2,1)} %get-tuple-element.104.x_ref, bf16[1536,512]{1,0:T(8,128)(2,1)} %get-tuple-element.103.dp_ref, bf16[512,2048]{1,0:T(8,128)(2,1)} %bitcast.161, ...), custom_call_target="tpu_custom_call" | custom-call | flops 19327352832 | bytes 14680064 | tf_op jit(solution)/shard_map/pallas_call | solution.py:67
  343.1 78.5 %all_to_all.10 = bf16[3,16,32,1024]{3,2,0,1:T(8,128)(2,1)S(1)} all-to-all(bf16[3,16,32,1024]{3,2,0,1:T(8,128)(2,1)S(1)} %copy.153), channel_id=1, replica_groups=mesh['dp'=16,'tensor'=2] {'dp'}, dimensions={1} | all-to-all | bytes 6291456 | tf_op jit(solution)/shard_map/all_to_all | solution.py:242
  428.9 3.5 pad_maximum_fusion.2
  434.9 74.8 %all-reduce.4.cloned.1.call-done = bf16[3,394,1152]{2,1,0:T(8,128)(2,1)} async-done(((bf16[3,394,1152]{2,1,0:T(8,128)(2,1)}), bf16[3,394,1152]{2,1,0:T(8,128)(2,1)}) %all-reduce.4.cloned.1.call-update) | async-done | bytes 2723344
  518.1 4.3 multiply_reduce_fusion
  532.4 4.6 convolution_convert_fusion
  551.5 3.2 reshape.245
  554.7 6.1 copy.196
  560.8 8.2 reshape.246
  586.7 131.1 %reduce-scatter.17.cloned.1.call-done = f32[16,20]{1,0:T(8,128)} async-done(((f32[512,20]{1,0:T(8,128)}), f32[16,20]{1,0:T(8,128)}) %reduce-scatter.17.cloned.1.call-update) | async-done | bytes 1296
  726.0 125.7 %reduce-scatter.11.cloned.1.call-done = bf16[16,512]{1,0:T(8,128)(2,1)} async-done(((bf16[512,512]{1,0:T(8,128)(2,1)}), bf16[16,512]{1,0:T(8,128)(2,1)}) %reduce-scatter.11.cloned.1.call-update) | async-done | bytes 16400 | tf_op jit(solution)/shard_map/reduce_scatter | solution.py:320
  853.0 97.9 %reduce-scatter.9.cloned.1.call-done = bf16[32,768]{1,0:T(8,128)(2,1)} async-done(((bf16[1024,768]{1,0:T(8,128)(2,1)}), bf16[32,768]{1,0:T(8,128)(2,1)}) %reduce-scatter.9.cloned.1.call-update) | async-done | bytes 49168 | tf_op jit(solution)/shard_map/reduce_scatter | solution.py:317
  (264 shorter events, 112.1 us)
Async XLA Ops:
  7.2 80.1 %copy-start.50 = (bf16[16]{0:T(256)(128)(2,1)S(1)}, bf16[16]{0:T(256)(128)(2,1)}, u32[]{:S(2)}) copy-start(bf16[16]{0:T(256)(128)(2,1)} %param.20) | copy-start | bytes 100
  7.2 80.2 %copy-start.51 = (bf16[16]{0:T(256)(128)(2,1)S(1)}, bf16[16]{0:T(256)(128)(2,1)}, u32[]{:S(2)}) copy-start(bf16[16]{0:T(256)(128)(2,1)} %param.21) | copy-start | bytes 100
  7.2 80.2 %copy-start.52 = (bf16[16]{0:T(256)(128)(2,1)S(1)}, bf16[16]{0:T(256)(128)(2,1)}, u32[]{:S(2)}) copy-start(bf16[16]{0:T(256)(128)(2,1)} %param.22) | copy-start | bytes 100
  7.2 80.3 %copy-start.53 = (bf16[16]{0:T(256)(128)(2,1)S(1)}, bf16[16]{0:T(256)(128)(2,1)}, u32[]{:S(2)}) copy-start(bf16[16]{0:T(256)(128)(2,1)} %param.23) | copy-start | bytes 100
  7.2 147.8 %all-gather.8.cloned.1.call-start = ((), (), s32[]{:S(2)}) async-start(), calls=%async_computation.7 | async-start | bytes 1622016 | tf_op jit(solution)/shard_map/all_gather | solution.py:137
  8.9 184.0 %all-gather.12.cloned.1.call-start = ((), (), s32[]{:S(2)}) async-start(), calls=%async_computation.9 | async-start | bytes 2359296 | tf_op jit(solution)/shard_map/all_gather | solution.py:145
  9.9 144.3 %collective-permute-start = (bf16[3,59,512]{2,1,0:T(8,128)(2,1)S(1)}, bf16[3,59,512]{2,1,0:T(8,128)(2,1)S(1)}, u32[]{:S(2)}, u32[]{:S(2)}) collective-permute-start(bf16[3,59,512]{2,1,0:T(8,128)(2,1)S(1)} %slice.125), channel_id=1, source_target_pairs={{0,1},{2,3},{4,5},{6,7},{8,9},{10,11},{12,13},{14,15},{16,17},{18,... | collective-permute-start | bytes 543752 | tf_op jit(solution)/shard_map/ppermute | solution.py:156
  14.8 202.8 %all-gather.10.cloned.1.call-start = ((), (), s32[]{:S(2)}) async-start(), calls=%async_computation.8 | async-start | bytes 2420736 | tf_op jit(solution)/shard_map/all_gather | solution.py:217
  87.8 66.4 %copy-start.13 = (bf16[3,256,512]{2,1,0:T(8,128)(2,1)S(1)}, bf16[3,256,512]{2,1,0:T(8,128)(2,1)}, u32[]{:S(2)}) copy-start(bf16[3,256,512]{2,1,0:T(8,128)(2,1)} %param.14) | copy-start | bytes 2359300
  87.9 66.3 %slice-start.2 = ((bf16[3,256,512]{2,1,0:T(8,128)(2,1)}), bf16[3,138,512]{2,1,0:T(8,128)(2,1)S(1)}, s32[]{:S(2)}) async-start(bf16[3,256,512]{2,1,0:T(8,128)(2,1)} %param.14), calls=%async_computation.20 | async-start | bytes 884736 | tf_op jit(solution)/shard_map/slice | solution.py:158
  229.5 65.0 %all-to-all-start = ((bf16[3,16,32,1024]{3,2,0,1:T(8,128)(2,1)}), bf16[3,16,32,1024]{3,2,0,1:T(8,128)(2,1)}, u32[]{:S(2)}, u32[]{:S(2)}) async-start(bf16[3,16,32,1024]{3,2,0,1:T(8,128)(2,1)} %copy.151), calls=%async_computation | async-start | bytes 6291456 | tf_op jit(solution)/shard_map/all_to_all | solution.py:239
  235.2 63.7 %all-gather.14.cloned.1.call-start = ((), (), s32[]{:S(2)}) async-start(), calls=%async_computation.14 | async-start | bytes 3145728 | tf_op jit(solution)/shard_map/all_gather | solution.py:143
  235.8 69.4 %all-gather.16.cloned.1.call-start = ((), (), s32[]{:S(2)}) async-start(), calls=%async_computation.15 | async-start | bytes 3145728 | tf_op jit(solution)/shard_map/all_gather | solution.py:144
  236.4 273.3 %all-reduce.4.cloned.1.call-start = ((), (), s32[]{:S(2)}) async-start(), calls=%async_computation.17 | async-start | bytes 5529600
  432.4 140.5 %reduce-scatter.15.cloned.1.call-start = ((), (), s32[]{:S(2)}) async-start(), calls=%async_computation.13 | async-start | bytes 3145728 | tf_op jit(solution)/shard_map/reduce_scatter | solution.py:244
  433.2 146.8 %reduce-scatter.13.cloned.1.call-start = ((), (), s32[]{:S(2)}) async-start(), calls=%async_computation.12 | async-start | bytes 3145728 | tf_op jit(solution)/shard_map/reduce_scatter | solution.py:243
  434.7 77.1 %copy-start.24 = (f32[3,394,16]{1,2,0:T(8,128)S(1)}, f32[3,394,16]{1,2,0:T(8,128)}, u32[]{:S(2)}) copy-start(f32[3,394,16]{1,2,0:T(8,128)} %get-tuple-element.99) | copy-start | bytes 226948
  434.7 77.2 %copy-start.33 = (f32[512]{0:T(512)S(1)}, f32[512]{0:T(512)}, u32[]{:S(2)}) copy-start(f32[512]{0:T(512)} %get-tuple-element.85) | copy-start | bytes 6148
  434.7 283.1 %reduce-scatter.17.cloned.1.call-start = ((), (), s32[]{:S(2)}) async-start(), calls=%async_computation.16 | async-start | bytes 270336
  545.3 306.4 %reduce-scatter.11.cloned.1.call-start = ((), (), s32[]{:S(2)}) async-start(), calls=%async_computation.11 | async-start | bytes 540672 | tf_op jit(solution)/shard_map/reduce_scatter | solution.py:320
  548.5 402.4 %reduce-scatter.9.cloned.1.call-start = ((), (), s32[]{:S(2)}) async-start(), calls=%async_computation.10 | async-start | bytes 1622016 | tf_op jit(solution)/shard_map/reduce_scatter | solution.py:317
  578.6 144.8 %collective-permute-start.2 = (f32[3,59,512]{2,1,0:T(8,128)}, f32[3,59,512]{2,1,0:T(8,128)}, u32[]{:S(2)}, u32[]{:S(2)}) collective-permute-start(f32[3,59,512]{2,1,0:T(8,128)} %slice.186), channel_id=1, source_target_pairs={{1,0},{3,2},{5,4},{7,6},{9,8},{11,10},{13,12},{15,14},{17,16},{19,... | collective-permute-start | bytes 1087496 | tf_op jit(solution)/shard_map/ppermute | solution.py:294
  584.7 138.8 %copy-start.15 = (f32[3,118,512]{2,1,0:T(8,128)S(1)}, f32[3,118,512]{2,1,0:T(8,128)}, u32[]{:S(2)}) copy-start(f32[3,118,512]{2,1,0:T(8,128)} %slice_convert_fusion.1) | copy-start | bytes 2174980
  585.4 135.7 %collective-permute-start.1 = (bf16[3,59,512]{2,1,0:T(8,128)(2,1)}, bf16[3,59,512]{2,1,0:T(8,128)(2,1)}, u32[]{:S(2)}, u32[]{:S(2)}) collective-permute-start(bf16[3,59,512]{2,1,0:T(8,128)(2,1)} %slice.181), channel_id=1, source_target_pairs={{1,0},{3,2},{5,4},{7,6},{9,8},{11,10},{13,12},{15,14},{17,16},{19,... | collective-permute-start | bytes 543752 | tf_op jit(solution)/shard_map/ppermute | solution.py:293
  (50 other events, 161.0 us)
Sparse Core Ops, SparseCore 0:
  11.5 58.4 all-gather.7
  71.6 27.1 all-gather.11
  191.9 25.6 all-gather.9
  237.3 33.4 all-gather.13
  272.1 33.0 all-gather.15
  432.5 77.1 all-reduce.3
  512.5 31.9 reduce-scatter.14
  547.4 31.8 reduce-scatter.12
  582.1 135.6 reduce-scatter.16
  719.9 131.7 reduce-scatter.10
  857.0 93.9 reduce-scatter.8

commit v2 on v1

--- a/solution.py
+++ b/solution.py
@@ -91,6 +91,241 @@
             flops=12 * n * d * ff, transcendentals=n * ff, bytes_accessed=8 * n * d + 8 * d * ff
         ),
     )(x, dprod, win, wout)
+
+
+MESH = pl.DeviceIdType.MESH
+ANYWHERE = pl.BlockSpec(memory_space=pltpu.VMEM)
+
+
+def grid_sizes(n_dp):
+    ny = 1
+    while 2 * ny * 2 * ny <= n_dp // 2:
+        ny *= 2
+    return n_dp // (2 * ny), ny
+
+
+def position(ny):
+    dp = lax.axis_index("dp")
+    return dp, lax.axis_index("tensor"), dp % 2, (dp // 2) % ny, dp // (2 * ny)
+
+
+def neighbours(ny, nz, n_t):
+    dp, t, c, y, z = position(ny)
+
+    def along_core(k):
+        return (dp - c + (c + k) % 2, t)
+
+    def along_tensor(k):
+        return (dp, (t + k) % n_t)
+
+    def along_y(k):
+        return (dp + ((y + k) % ny - y) * 2, t)
+
+    def along_z(k):
+        return (dp + ((z + k) % nz - z) * 2 * ny, t)
+
+    return {"core": (2, along_core), "tensor": (n_t, along_tensor), "y": (ny, along_y), "z": (nz, along_z)}
+
+
+def greet(stages):
+    barrier = pltpu.get_barrier_semaphore()
+    count = 0
+    for size, device in stages.values():
+        for k in range(1, size):
+            pl.semaphore_signal(barrier, inc=1, device_id=device(k), device_id_type=MESH)
+            count += 1
+    pl.semaphore_wait(barrier, count)
+
+
+def gather_kernel(ny, nz, n_t, qkv, proj, small, qkv_out, proj_out, small_out, send, recv, copied):
+    _, t, c, y, z = position(ny)
+    stages = neighbours(ny, nz, n_t)
+    greet(stages)
+    cols = qkv.shape[1]
+
+    def views(zs, ys, cs, ts):
+        lanes = pl.ds(pl.multiple_of(ts * cols, 128), cols)
+        return (
+            qkv_out.at[zs, ys, cs, :, lanes],
+            proj_out.at[zs, ys, cs, ts],
+            small_out.at[zs, ys, cs, ts],
+        )
+
+    whole = slice(None)
+    mine = views(z, y, c, t)
+    local = [
+        pltpu.make_async_copy(src, dst, copied.at[i])
+        for i, (src, dst) in enumerate(zip((qkv, proj, small), mine))
+    ]
+    for copy in local:
+        copy.start()
+    slot = 0
+    for name in ("z", "y", "tensor", "core"):
+        size, device = stages[name]
+        if name == "z":
+            sources, targets = (qkv, proj, small), mine
+        elif name == "y":
+            sources = targets = views(whole, y, c, t)
+        elif name == "tensor":
+            sources = targets = views(whole, whole, c, t)
+        else:
+            sources = targets = (
+                qkv_out.at[:, :, c],
+                proj_out.at[:, :, c],
+                small_out.at[:, :, c],
+            )
+        copies = []
+        for k in range(1, size):
+            for src, dst in zip(sources, targets):
+                copies.append(
+                    pltpu.make_async_remote_copy(
+                        src_ref=src,
+                        dst_ref=dst,
+                        send_sem=send.at[slot],
+                        recv_sem=recv.at[slot],
+                        device_id=device(k),
+                        device_id_type=MESH,
+                    )
+                )
+                slot += 1
+        for copy in copies:
+            copy.start()
+        if name == "z":
+            for copy in local:
+                copy.wait()
+        for copy in copies:
+            copy.wait()
+
+
+def gather_weights(qkv, proj, small, n_dp, n_t):
+    nz, ny = grid_sizes(n_dp)
+    slots = 3 * (1 + (n_t - 1) + (ny - 1) + (nz - 1))
+    outs = pl.pallas_call(
+        functools.partial(gather_kernel, ny, nz, n_t),
+        out_shape=[
+            jax.ShapeDtypeStruct((nz, ny, 2, qkv.shape[0], n_t * qkv.shape[1]), BF16),
+            jax.ShapeDtypeStruct((nz, ny, 2, n_t) + proj.shape, BF16),
+            jax.ShapeDtypeStruct((nz, ny, 2, n_t) + small.shape, BF16),
+        ],
+        in_specs=[ANYWHERE] * 3,
+        out_specs=[ANYWHERE] * 3,
+        scratch_shapes=[
+            pltpu.SemaphoreType.DMA((slots,)),
+            pltpu.SemaphoreType.DMA((slots,)),
+            pltpu.SemaphoreType.DMA((3,)),
+        ],
+        compiler_params=pltpu.CompilerParams(collective_id=0, has_side_effects=True),
+    )(qkv, proj, small)
+    qkv_all = outs[0].reshape(n_dp * qkv.shape[0], n_t * qkv.shape[1])
+    return qkv_all, outs[1].reshape((n_dp, n_t) + proj.shape), outs[2].reshape(-1, small.shape[1])
+
+
+def scatter_kernel(ny, nz, n_t, *refs):
+    ins, refs = refs[:3], refs[3:]
+    outs, refs = refs[:3], refs[3:]
+    got = [refs[3 * i : 3 * i + 3] for i in range(4)]
+    held = [refs[12 + 3 * i : 15 + 3 * i] for i in range(3)]
+    send, recv = refs[21], refs[22]
+    _, t, c, y, z = position(ny)
+    stages = neighbours(ny, nz, n_t)
+    greet(stages)
+    cols = outs[0].shape[1]
+    slot = 0
+
+    def lanes(ts):
+        return pl.ds(pl.multiple_of(ts * cols, 128), cols)
+
+    def exchange(name, me, piece):
+        nonlocal slot
+        size, device = stages[name]
+        level = ("core", "tensor", "y", "z").index(name)
+        copies = []
+        for k in range(1, size):
+            for i, src in enumerate(piece((me + k) % size)):
+                copies.append(
+                    pltpu.make_async_remote_copy(
+                        src_ref=src,
+                        dst_ref=got[level][i].at[k - 1],
+                        send_sem=send.at[slot],
+                        recv_sem=recv.at[slot],
+                        device_id=device(k),
+                        device_id_type=MESH,
+                    )
+                )
+                slot += 1
+        for copy in copies:
+            copy.start()
+        for copy in copies:
+            copy.wait()
+
+    def total(own, level, index, i):
+        value = own.astype(F32)
+        for k in range(got[level][i].shape[0]):
+            value = value + got[level][i][(k,) + index].astype(F32)
+        return value
+
+    def over_zy(body):
+        def step(n, carry):
+            body(n // ny, n % ny)
+            return carry
+
+        lax.fori_loop(0, nz * ny, step, 0)
+
+    exchange("core", c, lambda j: [ref.at[:, :, j] for ref in ins])
+
+    def add_core(zi, yi):
+        for i in range(3):
+            held[0][i][zi, yi] = total(ins[i][zi, yi, c], 0, (zi, yi), i).astype(held[0][i].dtype)
+
+    over_zy(add_core)
+    exchange(
+        "tensor",
+        t,
+        lambda j: [held[0][0].at[:, :, :, lanes(j)], held[0][1].at[:, :, j], held[0][2].at[:, :, j]],
+    )
+
+    def add_tensor(zi, yi):
+        owns = (held[0][0][zi, yi, :, lanes(t)], held[0][1][zi, yi, t], held[0][2][zi, yi, t])
+        for i in range(3):
+            held[1][i][zi, yi] = total(owns[i], 1, (zi, yi), i).astype(held[1][i].dtype)
+
+    over_zy(add_tensor)
+    exchange("y", y, lambda j: [ref.at[:, j] for ref in held[1]])
+
+    def add_y(zi, carry):
+        for i in range(3):
+            held[2][i][zi] = total(held[1][i][zi, y], 2, (zi,), i).astype(held[2][i].dtype)
+        return carry
+
+    lax.fori_loop(0, nz, add_y, 0)
+    exchange("z", z, lambda j: [ref.at[j] for ref in held[2]])
+    for i in range(3):
+        outs[i][...] = total(held[2][i][z], 3, (), i)
+
+
+def scatter_grads(qkv, proj, small, n_dp, n_t):
+    nz, ny = qkv.shape[:2]
+    rows, cols = qkv.shape[3], qkv.shape[4] // n_t
+    tails = [(rows, cols), proj.shape[4:], small.shape[4:]]
+    kinds = [BF16, BF16, F32]
+    wide = [(rows, n_t * cols), (n_t,) + proj.shape[4:], (n_t,) + small.shape[4:]]
+    scratch = [pltpu.VMEM((1, nz, ny) + wide[i], kinds[i]) for i in range(3)]
+    scratch += [pltpu.VMEM((n_t - 1, nz, ny) + tails[i], kinds[i]) for i in range(3)]
+    scratch += [pltpu.VMEM((ny - 1, nz) + tails[i], kinds[i]) for i in range(3)]
+    scratch += [pltpu.VMEM((nz - 1,) + tails[i], kinds[i]) for i in range(3)]
+    scratch += [pltpu.VMEM((nz, ny) + wide[i], kinds[i]) for i in range(3)]
+    scratch += [pltpu.VMEM((nz, ny) + tails[i], kinds[i]) for i in range(3)]
+    scratch += [pltpu.VMEM((nz,) + tails[i], kinds[i]) for i in range(3)]
+    slots = 3 * (1 + (n_t - 1) + (ny - 1) + (nz - 1))
+    scratch += [pltpu.SemaphoreType.DMA((slots,)), pltpu.SemaphoreType.DMA((slots,))]
+    return pl.pallas_call(
+        functools.partial(scatter_kernel, ny, nz, n_t),
+        out_shape=[jax.ShapeDtypeStruct(tail, F32) for tail in tails],
+        in_specs=[ANYWHERE] * 3,
+        out_specs=[ANYWHERE] * 3,
+        scratch_shapes=scratch,
+        compiler_params=pltpu.CompilerParams(collective_id=1, has_side_effects=True),
+    )(qkv, proj, small)
 
 
 def local(
@@ -131,13 +366,15 @@
     small = jnp.concatenate(
         [w_router] + [v[:, None] for v in (gain_attn, shift_attn, gain_moe, shift_moe)], axis=1
     )
-    small = lax.all_gather(small, ("dp", "tensor"), axis=0, tiled=True)
+    small = jnp.pad(small, ((0, 0), (0, 128 - small.shape[1])))
+    block = heads_here * width
+    qkv_block = w_qkv.reshape(-1, heads_here, 3, width).transpose(0, 2, 1, 3).reshape(-1, 3 * block)
+    fill = -3 * block % 128
+    qkv_block = jnp.pad(qkv_block, ((0, 0), (0, fill)))
+    qkv, proj, small = gather_weights(qkv_block, w_proj.reshape(-1, d), small, n_dp, n_t)
+    qkv = qkv.reshape(d, n_t, 3 * block + fill)[:, :, : 3 * block].reshape(d, -1)
     router = small[:, :experts]
     gain_one, shift_one, gain_two, shift_two = (small[:, experts + i].astype(F32) for i in range(4))
-    qkv = lax.all_gather(w_qkv.reshape(-1, 128), ("dp", "tensor"), axis=0, tiled=False)
-    qkv = qkv.reshape(n_dp, n_t, w_qkv.shape[0], heads_here, 3, width)
-    qkv = qkv.transpose(0, 2, 4, 1, 3, 5).reshape(d, 3 * heads * width)
-    proj = lax.all_gather(w_proj.reshape(-1, 128), ("dp", "tensor"), axis=0, tiled=False)
     proj = proj.reshape(n_dp, n_t, heads_here, w_proj.shape[1], d)
     proj = proj.transpose(1, 2, 0, 3, 4).reshape(heads * width, d)
     win = lax.all_gather(w_in[0], "tensor", axis=1, tiled=True)
@@ -202,9 +439,10 @@
     mixed = dot(normed_one, qkv, ((2,), (0,)))
     split = heads * width
     shape = (batches * per, SEQ, heads, width)
-    query = (mixed[..., :split] * factor).astype(BF16).reshape(shape)
-    keys = mixed[..., split : 2 * split].astype(BF16).reshape(shape)
-    values = mixed[..., 2 * split :].astype(BF16).reshape(shape)
+    mixed = mixed.reshape(batches, work, n_t, 3, block)
+    query = (mixed[:, :, :, 0] * factor).astype(BF16).reshape(shape)
+    keys = mixed[:, :, :, 1].astype(BF16).reshape(shape)
+    values = mixed[:, :, :, 2].astype(BF16).reshape(shape)
     scores = jnp.einsum("iqhc,ikhc->ihqk", query, keys, preferred_element_type=F32)
     probs = jax.nn.softmax(scores, axis=-1)
     weights = probs.astype(BF16)
@@ -254,7 +492,16 @@
     payload = jnp.concatenate(
         [mixture, d_rows, jnp.pad(dgates, ((0, 0), (0, 0), (0, 126)))], axis=-1
     ).astype(BF16)
-    payload = lax.psum_scatter(payload, "tensor", scatter_dimension=1, tiled=True).astype(F32)
+    pieces = payload.reshape(batches, n_t, work, payload.shape[-1])
+
+    def piece(k):
+        return lax.dynamic_index_in_dim(pieces, (t + k) % n_t, 1, keepdims=False)
+
+    payload = piece(0).astype(F32)
+    for k in range(1, n_t):
+        payload = payload + lax.ppermute(
+            piece(k), "tensor", [(j, (j + k) % n_t) for j in range(n_t)]
+        ).astype(F32)
     output = (hidden + payload[..., :d]).astype(BF16)
     dgates = payload[..., 2 * d : 2 * d + 2]
 
@@ -280,9 +527,9 @@
     dscores = (probs * (dweights - jnp.sum(dweights * probs, axis=-1, keepdims=True))).astype(BF16)
     dquery = jnp.einsum("ihqk,ikhc->iqhc", dscores, keys, preferred_element_type=F32).astype(BF16)
     dkeys = jnp.einsum("ihqk,iqhc->ikhc", dscores, query, preferred_element_type=F32).astype(BF16)
-    dmixed = jnp.concatenate(
-        [v.reshape(batches, work, split) for v in (dquery * BF16(factor), dkeys, dvalues)], axis=-1
-    )
+    dmixed = jnp.stack(
+        [v.reshape(batches, work, n_t, block) for v in (dquery * BF16(factor), dkeys, dvalues)], axis=3
+    ).reshape(batches, work, 3 * split)
     grad_qkv = dot(normed_one, dmixed, ((0, 1), (0, 1)))
     da = dot(dmixed, qkv, ((2,), (1,)))
     _, back_one = jax.vjp(layer_norm, x, gain_one, shift_one)
@@ -312,22 +559,23 @@
         result = home(output, tokens)
         grad_tokens = home(grad_x, cotangent.astype(F32))
 
-    grad_qkv = grad_qkv.astype(BF16).reshape(n_dp, -1, 3, n_t, heads_here, width)
-    grad_qkv = grad_qkv.transpose(0, 3, 1, 4, 2, 5).reshape(n_dp * n_t * w_qkv.shape[0], heads_here * 3 * width)
-    grad_qkv = lax.psum_scatter(grad_qkv, ("dp", "tensor"), scatter_dimension=0, tiled=True)
+    nz, ny = grid_sizes(n_dp)
+    grad_qkv = jnp.pad(grad_qkv.astype(BF16).reshape(d, n_t, 3 * block), ((0, 0), (0, 0), (0, fill)))
+    grad_qkv = grad_qkv.reshape(nz, ny, 2, d // n_dp, -1)
     grad_proj = grad_proj.astype(BF16).reshape(n_t, heads_here, n_dp, -1, d)
-    grad_proj = grad_proj.transpose(2, 0, 1, 3, 4).reshape(-1, d)
-    grad_proj = lax.psum_scatter(grad_proj, ("dp", "tensor"), scatter_dimension=0, tiled=True)
+    grad_proj = grad_proj.transpose(2, 0, 1, 3, 4).reshape(nz, ny, 2, n_t, -1, d)
     smalls = jnp.concatenate(
         [grad_router] + [v[:, None] for v in (grad_gain_one, grad_shift_one, grad_gain_two, grad_shift_two)],
         axis=1,
     )
-    smalls = lax.psum_scatter(smalls, ("dp", "tensor"), scatter_dimension=0, tiled=True)
+    smalls = jnp.pad(smalls, ((0, 0), (0, 128 - smalls.shape[1]))).reshape(nz, ny, 2, n_t, -1, 128)
+    grad_qkv, grad_proj, smalls = scatter_grads(grad_qkv, grad_proj, smalls, n_dp, n_t)
+    grad_qkv = grad_qkv[:, : 3 * block].reshape(-1, 3, heads_here, width).transpose(0, 2, 1, 3)
     return (
         result,
         grad_tokens,
-        grad_qkv.astype(F32).reshape(w_qkv.shape),
-        grad_proj.astype(F32).reshape(w_proj.shape),
+        grad_qkv.reshape(w_qkv.shape),
+        grad_proj.reshape(w_proj.shape),
         grad_in[None],
         grad_out[None],
         smalls[:, :experts],

time: 964 us -> 527 us (0.55)
  waiting for transfers between devices: 518 us -> 199 us
  blocking collectives: 212 us -> 0 us
  Pallas kernels: 35.3 us -> 118 us
    reduce_scatter x2 -> x0, waiting for transfers between devices: 224 us -> none  [the longest x1 126 us: local(): lax.psum_scatter(grad_proj, ('dp', 'tensor'), scatter_dimension=0, tiled=...]
    unnamed x13 -> x6, waiting for transfers between devices: 208 us -> 2.8 us
    all_gather x2 -> x0, blocking collectives: 134 us -> none  [the longest x1 69.7 us: local(): lax.all_gather(w_proj.reshape(-1, 128), ('dp', 'tensor'), axis=0, tiled=F...]
    pallas_call x0 -> x2, Pallas kernels: none -> 82.8 us  [the longest x1 50.9 us: scatter_grads(): pl.pallas_call(functools.partial(scatter_kernel, ny, nz, n_t), out_shape=...]
    all_to_all x1 -> x0, blocking collectives: 78.5 us -> none  [local(): lax.all_to_all(back, 'dp', 1, 1, tiled=True)]
    all_to_all x0 -> x1, waiting for transfers between devices: none -> 58.1 us  [local(): lax.all_to_all(back, 'dp', 1, 1, tiled=True)]
    reshape x12 -> x9, local copies, waits for them, and re-layouts: 42.3 us -> 12.9 us  [the longest x1 4.73 us: local(): dmixed = jnp.stack([v.reshape(batches, work, n_t, block) for v in (dquery...]
    ppermute x0 -> x1, waiting for transfers between devices: none -> 24.2 us  [local(): lax.ppermute(piece(k), 'tensor', [(j, (j + k) % n_t) for j in range(n_t)])]
  transfers between devices with their start and end apart: 15 -> 12, of which waited for: 7 -> 6; matrix products, arithmetic and copies ran while one was open for 13% -> 14% of each run, Pallas kernels for 0% -> 16%
where the time goes in v2:
time: 527 us; the launch traced here: 519 us
  waiting for transfers between devices  199 us (38%)
  Pallas kernels  118 us (22%)
  local copies, waits for them, and re-layouts  82.1 us (16%)
  matrix products  40.9 us (8%)
  other arithmetic  39.8 us (8%)
  starting transfers between devices  23.6 us (4%)
  between operations  15.4 us (3%)
    all_to_all x1, waiting for transfers between devices, local(): lax.all_to_all(back, 'dp', 1, 1, tiled=True)  58.1 us
    all_to_all x1, waiting for transfers between devices, local(): got = lax.all_to_all(sent, 'dp', 1, 1, tiled=True).reshape(-1, 2 * d)  58 us
    pallas_call x1, Pallas kernels, scatter_grads(): pl.pallas_call(functools.partial(scatter_kernel, ny, nz, n_t), out_shape=...  50.9 us
    pallas_call x1, Pallas kernels, expert(): pl.pallas_call(expert_kernel, grid=(ff // tile,), in_specs=[pl.BlockSpec(...  35.3 us
    pallas_call x1, Pallas kernels, gather_weights(): pl.pallas_call(functools.partial(gather_kernel, ny, nz, n_t), out_shape=[...  31.9 us
    all_gather x1, waiting for transfers between devices, local(): c_all = lax.all_gather(normed_two, 'tensor', axis=1, tiled=True)  25.4 us
    ppermute x1, waiting for transfers between devices, local(): lax.ppermute(piece(k), 'tensor', [(j, (j + k) % n_t) for j in range(n_t)])  24.2 us
    all_gather x1, waiting for transfers between devices, local(): cot_all = lax.all_gather(cotangent, 'tensor', axis=1, tiled=True)  24 us
  transfers between devices with their start and end apart: 12, of which 6 were waited for; matrix products, arithmetic and copies ran while one was open for 14% of the time, Pallas kernels for 16%

profile of v2, /device:TPU:0, one launch (start us, length us, event | category | flops | bytes accessed | tf_op | source)
XLA Modules:
  0.0 518.9 jit_solution(11837125399147198332)
XLA Ops:
  8.9 5.5 %collective-permute-start = (bf16[3,59,512]{2,1,0:T(8,128)(2,1)}, bf16[3,59,512]{2,1,0:T(8,128)(2,1)}, u32[]{:S(2)}, u32[]{:S(2)}) collective-permute-start(bf16[3,59,512]{2,1,0:T(8,128)(2,1)} %slice.125), channel_id=1, source_target_pairs={{0,1},{2,3},{4,5},{6,7},{8,9},{10,11},{12,13},{14,15},{16,17},{18,... | collective-permute-start | bytes 543752 | tf_op jit(solution)/shard_map/ppermute | solution.py:393
  21.9 31.9 %shard_map.221 = (bf16[4,2,2,32,1536]{4,3,2,1,0:T(8,128)(2,1)}, bf16[4,2,2,2,16,512]{5,4,3,2,1,0:T(8,128)(2,1)}, bf16[4,2,2,2,16,128]{5,4,3,2,1,0:T(8,128)(2,1)}) custom-call(bf16[32,768]{1,0:T(8,128)(2,1)} %reshape.239.qkv, bf16[16,512]{1,0:T(8,128)(2,1)} %reshape.240.proj, bf16[16,128]{1,0:T(8,128)(2,1)} %pad.13.small), custom_call_target="tpu_custom_call" | custom-call | tf_op jit(solution)/shard_map/pallas_call | solution.py:203
  65.1 3.0 fusion.93
  73.0 3.8 fusion.94
  76.8 3.1 convolution_convert_fusion.3
  85.8 25.4 %all-gather.7.cloned.1.call-done = bf16[3,394,512]{2,0,1:T(4,128)(2,1)} async-done(((bf16[3,197,512]{2,0,1:T(4,128)(2,1)}), bf16[3,394,512]{2,0,1:T(4,128)(2,1)}) %all-gather.7.cloned.1.call-update) | async-done | bytes 1210384 | tf_op jit(solution)/shard_map/all_gather | solution.py:455
  116.0 24.0 %all-gather.9.cloned.1.call-done = bf16[3,512,512]{2,1,0:T(8,128)(2,1)} async-done(((bf16[3,256,512]{2,1,0:T(8,128)(2,1)}), bf16[3,512,512]{2,1,0:T(8,128)(2,1)}) %all-gather.9.cloned.1.call-update) | async-done | bytes 1572880 | tf_op jit(solution)/shard_map/all_gather | solution.py:382
  146.5 5.7 %all-to-all-start = ((bf16[3,16,32,1024]{3,2,0,1:T(8,128)(2,1)}), bf16[3,16,32,1024]{3,2,0,1:T(8,128)(2,1)}, u32[]{:S(2)}, u32[]{:S(2)}) async-start(bf16[3,16,32,1024]{3,2,0,1:T(8,128)(2,1)} %copy.137), calls=%async_computation | async-start | bytes 6291456 | tf_op jit(solution)/shard_map/all_to_all | solution.py:477
  153.5 58.0 %all-to-all-done = bf16[3,16,32,1024]{3,2,0,1:T(8,128)(2,1)} async-done(((bf16[3,16,32,1024]{3,2,0,1:T(8,128)(2,1)}), bf16[3,16,32,1024]{3,2,0,1:T(8,128)(2,1)}, u32[]{:S(2)}, u32[]{:S(2)}) %all-to-all-start) | async-done | bytes 3145760 | tf_op jit(solution)/shard_map/all_to_all | solution.py:477
  215.9 6.6 %all-gather.13.cloned.1.call-done = bf16[1,2048,512]{2,1,0:T(8,128)(2,1)} async-done(((bf16[1,1024,512]{2,1,0:T(8,128)(2,1)}), bf16[1,2048,512]{2,1,0:T(8,128)(2,1)}) %all-gather.13.cloned.1.call-update) | async-done | bytes 2097168 | tf_op jit(solution)/shard_map/all_gather | solution.py:381
  222.5 35.3 %shard_map.222 = (bf16[1536,512]{1,0:T(8,128)(2,1)}, bf16[1536,512]{1,0:T(8,128)(2,1)}, bf16[512,2048]{1,0:T(8,128)(2,1)}, bf16[2048,512]{1,0:T(8,128)(2,1)}) custom-call(bf16[1536,512]{1,0:T(8,128)(2,1)} %get-tuple-element.94.x_ref, bf16[1536,512]{1,0:T(8,128)(2,1)} %get-tuple-element.93.dp_ref, bf16[512,2048]{1,0:T(8,128)(2,1)} %bitcast.207, ...), custom_call_target="tpu_custom_call" | custom-call | flops 19327352832 | bytes 14680064 | tf_op jit(solution)/shard_map/pallas_call | solution.py:67
  262.2 8.8 %all-to-all-start.1 = ((bf16[3,16,32,1024]{3,2,0,1:T(8,128)(2,1)}), bf16[3,16,32,1024]{3,2,0,1:T(8,128)(2,1)}, u32[]{:S(2)}, u32[]{:S(2)}) async-start(bf16[3,16,32,1024]{3,2,0,1:T(8,128)(2,1)} %copy.139), calls=%async_computation.1 | async-start | bytes 6291456 | tf_op jit(solution)/shard_map/all_to_all | solution.py:480
  272.2 58.1 %all-to-all-done.1 = bf16[3,16,32,1024]{3,2,0,1:T(8,128)(2,1)} async-done(((bf16[3,16,32,1024]{3,2,0,1:T(8,128)(2,1)}), bf16[3,16,32,1024]{3,2,0,1:T(8,128)(2,1)}, u32[]{:S(2)}, u32[]{:S(2)}) %all-to-all-start.1) | async-done | bytes 3145760 | tf_op jit(solution)/shard_map/all_to_all | solution.py:480
  340.4 4.0 fusion.9
  362.3 2.9 bitcast_convert_fusion.1
  365.3 24.2 %collective-permute-done.1 = bf16[3,197,1152]{2,1,0:T(8,128)(2,1)} collective-permute-done((bf16[3,197,1152]{2,1,0:T(8,128)(2,1)}, bf16[3,197,1152]{2,1,0:T(8,128)(2,1)}, u32[]{:S(2)}, u32[]{:S(2)}) %collective-permute-start.1) | collective-permute-done | bytes 1361696 | tf_op jit(solution)/shard_map/ppermute | solution.py:502
  397.2 4.1 multiply_reduce_fusion
  409.1 3.3 copy.149
  412.3 3.9 copy.150
  416.2 3.7 copy.151
  419.9 6.7 %pad_maximum_fusion.3 = bf16[3,197,2,3,256]{4,3,2,1,0:T(4,128)(2,1)} fusion(bf16[3,197,2,1,256]{4,3,2,1,0:T(2,128)(2,1)} %copy.151, bf16[3,197,2,1,256]{4,3,2,1,0:T(2,128)(2,1)} %copy.150, bf16[3,197,2,1,256]{4,3,2,1,0:T(2,128)(2,1)S(1)} %copy.149), kind=kLoop, calls=%fused_computation.36 | loop fusion | flops 5446656 | bytes 3631104 | tf_op jit(solution)/shard_map/stack | solution.py:530
  426.6 4.7 reshape.249
  431.3 4.4 fusion.8
  446.9 50.9 %shard_map.223 = (f32[32,768]{1,0:T(8,128)}, f32[16,512]{1,0:T(8,128)}, f32[16,128]{1,0:T(8,128)}) custom-call(bf16[4,2,2,32,1536]{4,3,2,1,0:T(8,128)(2,1)} %bitcast.166, bf16[4,2,2,2,16,512]{5,4,3,2,1,0:T(8,128)(2,1)} %reshape.252.refs_1_, f32[4,2,2,2,16,128]{5,4,3,2,1,0:T(8,128)} %bitcast.167), custom_call_target="tpu_custom_call" | custom-call | tf_op jit(solution)/shard_map/pallas_call | solution.py:321
  (246 shorter events, 121.5 us)
Async XLA Ops:
  7.2 48.9 %copy-start.38 = (s32[3,512]{1,0:T(4,128)S(1)}, s32[3,512]{1,0:T(4,128)}, u32[]{:S(2)}) copy-start(s32[3,512]{1,0:T(4,128)} %param.24) | copy-start | bytes 18436
  7.2 104.0 %all-gather.7.cloned.1.call-start = ((), (), s32[]{:S(2)}) async-start(), calls=%async_computation.4 | async-start | bytes 2420736 | tf_op jit(solution)/shard_map/all_gather | solution.py:455
  8.9 54.5 %collective-permute-start = (bf16[3,59,512]{2,1,0:T(8,128)(2,1)}, bf16[3,59,512]{2,1,0:T(8,128)(2,1)}, u32[]{:S(2)}, u32[]{:S(2)}) collective-permute-start(bf16[3,59,512]{2,1,0:T(8,128)(2,1)} %slice.125), channel_id=1, source_target_pairs={{0,1},{2,3},{4,5},{6,7},{8,9},{10,11},{12,13},{14,15},{16,17},{18,... | collective-permute-start | bytes 543752 | tf_op jit(solution)/shard_map/ppermute | solution.py:393
  56.3 8.8 %copy-start.36 = (f32[512,1]{0,1:T(1,128)}, f32[512,1]{0,1:T(1,128)S(1)}, u32[]{:S(2)}) copy-start(f32[512,1]{0,1:T(1,128)S(1)} %copy.176) | copy-start | bytes 6148
  62.3 18.9 %copy-start.34 = (f32[512,1]{0,1:T(1,128)}, f32[512,1]{0,1:T(1,128)S(1)}, u32[]{:S(2)}) copy-start(f32[512,1]{0,1:T(1,128)S(1)} %copy.177) | copy-start | bytes 6148
  63.4 16.5 %copy-start.39 = (f32[3,197]{1,0:T(4,128)}, f32[3,197]{1,0:T(4,128)S(1)}, u32[]{:S(2)}) copy-start(f32[3,197]{1,0:T(4,128)S(1)} %dynamic-slice_convert_fusion) | copy-start | bytes 7096
  83.6 56.3 %all-gather.9.cloned.1.call-start = ((), (), s32[]{:S(2)}) async-start(), calls=%async_computation.5 | async-start | bytes 2359296 | tf_op jit(solution)/shard_map/all_gather | solution.py:382
  85.1 27.8 %copy-start.13 = (bf16[4,2,2,2,16,128]{5,4,3,2,1,0:T(8,128)(2,1)S(1)}, bf16[4,2,2,2,16,128]{5,4,3,2,1,0:T(8,128)(2,1)}, u32[]{:S(2)}) copy-start(bf16[4,2,2,2,16,128]{5,4,3,2,1,0:T(8,128)(2,1)} %get-tuple-element.21) | copy-start | bytes 393220
  115.0 28.3 %copy-start.43 = (pred[3,394]{1,0:T(4,128)(4,1)}, pred[3,394]{1,0:T(4,128)(4,1)S(1)}, u32[]{:S(2)}) copy-start(pred[3,394]{1,0:T(4,128)(4,1)S(1)} %get-tuple-element.85) | copy-start | bytes 3550
  115.0 28.3 %copy-start.41 = (pred[3,394]{1,0:T(4,128)(4,1)}, pred[3,394]{1,0:T(4,128)(4,1)S(1)}, u32[]{:S(2)}) copy-start(pred[3,394]{1,0:T(4,128)(4,1)S(1)} %get-tuple-element.88) | copy-start | bytes 3550
  146.5 65.0 %all-to-all-start = ((bf16[3,16,32,1024]{3,2,0,1:T(8,128)(2,1)}), bf16[3,16,32,1024]{3,2,0,1:T(8,128)(2,1)}, u32[]{:S(2)}, u32[]{:S(2)}) async-start(bf16[3,16,32,1024]{3,2,0,1:T(8,128)(2,1)} %copy.137), calls=%async_computation | async-start | bytes 6291456 | tf_op jit(solution)/shard_map/all_to_all | solution.py:477
  152.2 63.7 %all-gather.11.cloned.1.call-start = ((), (), s32[]{:S(2)}) async-start(), calls=%async_computation.8 | async-start | bytes 3145728 | tf_op jit(solution)/shard_map/all_gather | solution.py:380
  152.9 69.6 %all-gather.13.cloned.1.call-start = ((), (), s32[]{:S(2)}) async-start(), calls=%async_computation.9 | async-start | bytes 3145728 | tf_op jit(solution)/shard_map/all_gather | solution.py:381
  262.2 68.1 %all-to-all-start.1 = ((bf16[3,16,32,1024]{3,2,0,1:T(8,128)(2,1)}), bf16[3,16,32,1024]{3,2,0,1:T(8,128)(2,1)}, u32[]{:S(2)}, u32[]{:S(2)}) async-start(bf16[3,16,32,1024]{3,2,0,1:T(8,128)(2,1)} %copy.139), calls=%async_computation.1 | async-start | bytes 6291456 | tf_op jit(solution)/shard_map/all_to_all | solution.py:480
  271.0 88.5 %reduce-scatter.5.cloned.1.call-start = ((), (), s32[]{:S(2)}) async-start(), calls=%async_computation.7 | async-start | bytes 3145728 | tf_op jit(solution)/shard_map/reduce_scatter | solution.py:482
  271.6 90.7 %reduce-scatter.3.cloned.1.call-start = ((), (), s32[]{:S(2)}) async-start(), calls=%async_computation.6 | async-start | bytes 3145728 | tf_op jit(solution)/shard_map/reduce_scatter | solution.py:481
  356.0 33.5 %collective-permute-start.1 = (bf16[3,197,1152]{2,1,0:T(8,128)(2,1)}, bf16[3,197,1152]{2,1,0:T(8,128)(2,1)}, u32[]{:S(2)}, u32[]{:S(2)}) collective-permute-start(bf16[3,197,1152]{2,1,0:T(8,128)(2,1)} %dynamic-slice_bitcast_fusion), channel_id=1, source_target_pairs={{0,1},{1,0},{2,3},{3,2},{4,5},{5,4},{6,7},{7,6},{8,9},{9,8},{10,11... | collective-permute-start | bytes 4085000 | tf_op jit(solution)/shard_map/ppermute | solution.py:502
  362.3 27.1 %copy-start.1 = (bf16[3,2,197,1152]{3,2,0,1:T(8,128)(2,1)S(1)}, bf16[3,2,197,1152]{3,2,0,1:T(8,128)(2,1)}, u32[]{:S(2)}) copy-start(bf16[3,2,197,1152]{3,2,0,1:T(8,128)(2,1)} %copy-done) | copy-start | bytes 8169988
  365.3 26.2 %copy-start.28 = (f32[3,394,16]{1,2,0:T(8,128)S(1)}, f32[3,394,16]{1,2,0:T(8,128)}, u32[]{:S(2)}) copy-start(f32[3,394,16]{1,2,0:T(8,128)} %get-tuple-element.89) | copy-start | bytes 226948
  365.3 26.4 %copy-start.35 = (f32[512,1]{0,1:T(1,128)S(1)}, f32[512,1]{0,1:T(1,128)}, u32[]{:S(2)}) copy-start(f32[512,1]{0,1:T(1,128)} %copy-done.34) | copy-start | bytes 6148
  439.9 68.6 %collective-permute-start.3 = (f32[3,59,512]{2,1,0:T(8,128)}, f32[3,59,512]{2,1,0:T(8,128)}, u32[]{:S(2)}, u32[]{:S(2)}) collective-permute-start(f32[3,59,512]{2,1,0:T(8,128)} %slice.186), channel_id=1, source_target_pairs={{1,0},{3,2},{5,4},{7,6},{9,8},{11,10},{13,12},{15,14},{17,16},{19,... | collective-permute-start | bytes 1087496 | tf_op jit(solution)/shard_map/ppermute | solution.py:541
  441.9 64.2 %collective-permute-start.2 = (bf16[3,59,512]{2,1,0:T(8,128)(2,1)}, bf16[3,59,512]{2,1,0:T(8,128)(2,1)}, u32[]{:S(2)}, u32[]{:S(2)}) collective-permute-start(bf16[3,59,512]{2,1,0:T(8,128)(2,1)} %slice.181), channel_id=1, source_target_pairs={{1,0},{3,2},{5,4},{7,6},{9,8},{11,10},{13,12},{15,14},{17,16},{19,... | collective-permute-start | bytes 543752 | tf_op jit(solution)/shard_map/ppermute | solution.py:540
  446.9 59.2 %copy-start.7 = (bf16[3,197,512]{2,1,0:T(8,128)(2,1)S(1)}, bf16[3,197,512]{2,1,0:T(8,128)(2,1)}, u32[]{:S(2)}) copy-start(bf16[3,197,512]{2,1,0:T(8,128)(2,1)} %get-tuple-element.97) | copy-start | bytes 1815556
  499.6 8.9 %copy-start.18 = (f32[3,118,512]{2,1,0:T(8,128)S(1)}, f32[3,118,512]{2,1,0:T(8,128)}, u32[]{:S(2)}) copy-start(f32[3,118,512]{2,1,0:T(8,128)} %slice_convert_fusion.1) | copy-start | bytes 2174980
  (40 other events, 104.8 us)
Sparse Core Ops, SparseCore 0:
  83.8 27.3 all-gather.6
  112.7 27.1 all-gather.8
  154.5 33.4 all-gather.10
  189.4 33.0 all-gather.12
  274.3 32.2 reduce-scatter.4
  309.3 31.8 reduce-scatter.2

commit v3 on v2

--- a/solution.py
+++ b/solution.py
@@ -328,6 +328,312 @@
     )(qkv, proj, small)
 
 
+def moe_kernel(
+    experts,
+    c_own,
+    cot_all,
+    router,
+    flat_row,
+    flat_col,
+    expert_col,
+    code_row,
+    code_col,
+    win,
+    wout,
+    mix,
+    dx,
+    dgate,
+    gin_out,
+    gout_out,
+    c_all,
+    gates,
+    sent,
+    got,
+    back,
+    ret,
+    pay,
+    paid,
+    y_acc,
+    dx_acc,
+    gin,
+    gout,
+    gin_half,
+    gout_half,
+    gin_got,
+    gout_got,
+    c_sems,
+    go_send,
+    go_recv,
+    back_send,
+    back_recv,
+    pay_sems,
+    grad_sems,
+):
+    batches, rows, d = c_own.shape
+    n_dp = lax.axis_size("dp")
+    dp, t = lax.axis_index("dp"), lax.axis_index("tensor")
+    share = sent.shape[1] // n_dp
+    hidden = win.shape[1]
+    half = hidden // 2
+    other = 1 - t
+    partner = (dp, other)
+
+    barrier = pltpu.get_barrier_semaphore()
+    pl.semaphore_signal(barrier, inc=1, device_id=partner, device_id_type=MESH)
+
+    def hello(k, carry):
+        pl.semaphore_signal(barrier, inc=1, device_id=((dp + k) % n_dp, t), device_id_type=MESH)
+        return carry
+
+    lax.fori_loop(1, n_dp, hello, 0)
+    pl.semaphore_wait(barrier, n_dp)
+
+    def image(i):
+        return pl.ds(pl.multiple_of(i * rows, 16), rows)
+
+    def part(i):
+        return pl.ds(pl.multiple_of(i * share, 16), share)
+
+    def remote(src, dst, sems, i, j, device):
+        return pltpu.make_async_remote_copy(
+            src_ref=src,
+            dst_ref=dst,
+            send_sem=sems[0].at[i, j],
+            recv_sem=sems[1].at[i, j],
+            device_id=device,
+            device_id_type=MESH,
+        )
+
+    def c_copy(m):
+        return pltpu.make_async_remote_copy(
+            src_ref=c_own.at[m],
+            dst_ref=c_all.at[m, image(t)],
+            send_sem=c_sems.at[0, m],
+            recv_sem=c_sems.at[1, m],
+            device_id=partner,
+            device_id_type=MESH,
+        )
+
+    def go_copy(m, k):
+        to = (dp + k) % n_dp
+        return remote(sent.at[m, part(to)], got.at[m, part(dp)], (go_send, go_recv), m, k - 1, (to, t))
+
+    def back_copy(m, k):
+        to = (dp + k) % n_dp
+        return remote(back.at[m, part(to)], ret.at[m, part(dp)], (back_send, back_recv), m, k - 1, (to, t))
+
+    def pay_copy(m):
+        return pltpu.make_async_remote_copy(
+            src_ref=pay.at[m],
+            dst_ref=paid.at[m],
+            send_sem=pay_sems.at[0, m],
+            recv_sem=pay_sems.at[1, m],
+            device_id=partner,
+            device_id_type=MESH,
+        )
+
+    def grad_copy(i):
+        return pltpu.make_async_remote_copy(
+            src_ref=(gin_half, gout_half)[i],
+            dst_ref=(gin_got, gout_got)[i],
+            send_sem=grad_sems.at[0, i],
+            recv_sem=grad_sems.at[1, i],
+            device_id=partner,
+            device_id_type=MESH,
+        )
+
+    def every(body):
+        def step(k, carry):
+            body(k)
+            return carry
+
+        lax.fori_loop(1, n_dp, step, 0)
+
+    for m in range(batches):
+        c_copy(m).start()
+        c_all[m, image(t)] = c_own[m]
+
+    lane = lax.broadcasted_iota(jnp.int32, (2 * rows, router.shape[1]), 1)
+
+    def dispatch(m, carry):
+        c_copy(m).wait_recv()
+        c = c_all[m]
+        logits = jnp.where(lane < experts, dot(c, router[...], ((1,), (0,))), -1e30)
+        raised = jnp.exp(logits - jnp.max(logits, axis=-1, keepdims=True))
+        probs = raised / jnp.sum(raised, axis=-1, keepdims=True)
+        cot = cot_all[m].astype(F32)
+        scaled = []
+        for k in range(2):
+            gate = jnp.sum(jnp.where(lane == expert_col[m, :, k : k + 1], probs, 0.0), axis=-1, keepdims=True)
+            gates[m, :, k : k + 1] = gate
+            scaled.append((gate * cot).astype(BF16))
+        codes = code_col[...]
+        picks = [(flat_row[m, k : k + 1, :] == codes).astype(F32).astype(BF16) for k in range(2)]
+        sent[m, :, :d] = dot(picks[0] + picks[1], c, ((1,), (0,))).astype(BF16)
+        moved = dot(picks[0], scaled[0], ((1,), (0,))) + dot(picks[1], scaled[1], ((1,), (0,)))
+        sent[m, :, d:] = moved.astype(BF16)
+        every(lambda k: go_copy(m, k).start())
+        got[m, part(dp)] = sent[m, part(dp)]
+        return carry
+
+    lax.fori_loop(0, batches, dispatch, 0)
+
+    tile = 256
+
+    def clear(i, carry):
+        cols = pl.ds(pl.multiple_of(i * tile, tile), tile)
+        gin[:, cols] = jnp.zeros((d, tile), F32)
+        gout[cols, :] = jnp.zeros((tile, d), F32)
+        return carry
+
+    lax.fori_loop(0, hidden // tile, clear, 0)
+
+    def expert_step(m, carry):
+        every(lambda k: go_copy(m, k).wait_recv())
+        y_acc[...] = jnp.zeros_like(y_acc)
+        dx_acc[...] = jnp.zeros_like(dx_acc)
+
+        def chunk(i, inner):
+            cols = pl.ds(pl.multiple_of(i * tile, tile), tile)
+            x = got[m, :, :d]
+            dprod = got[m, :, d:]
+            w1 = win[:, cols]
+            w2 = wout[cols, :]
+            pre = dot(x, w1, ((1,), (0,)))
+            square = pre * pre
+            th = jnp.tanh(GELU_A * pre * (1.0 + GELU_B * square))
+            active = (0.5 * pre * (1.0 + th)).astype(BF16)
+            slope = 0.5 * (1.0 + th) + 0.5 * pre * (1.0 - th * th) * (GELU_A * (1.0 + 3.0 * GELU_B * square))
+            dpre = (dot(dprod, w2, ((1,), (1,))) * slope).astype(BF16)
+            gin[:, cols] += dot(x, dpre, ((0,), (0,)))
+            gout[cols, :] += dot(active, dprod, ((0,), (0,)))
+            y_acc[...] += dot(active, w2, ((1,), (0,)))
+            dx_acc[...] += dot(dpre, w1, ((1,), (1,)))
+            return inner
+
+        lax.fori_loop(0, hidden // tile, chunk, 0)
+        back[m, :, :d] = y_acc[...].astype(BF16)
+        back[m, :, d:] = dx_acc[...].astype(BF16)
+        every(lambda k: back_copy(m, k).start())
+        ret[m, part(dp)] = back[m, part(dp)]
+        return carry
+
+    lax.fori_loop(0, batches, expert_step, 0)
+
+    gin_half[...] = gin[:, pl.ds(pl.multiple_of(other * half, 128), half)].astype(BF16)
+    gout_half[...] = gout[pl.ds(pl.multiple_of(other * half, 128), half), :].astype(BF16)
+    grad_copy(0).start()
+    grad_copy(1).start()
+
+    def combine(m, carry):
+        every(lambda k: back_copy(m, k).wait_recv())
+        codes = code_row[...]
+        for i in (other, t):
+            picks = [(flat_col[m, image(i), k : k + 1] == codes).astype(F32).astype(BF16) for k in range(2)]
+            one = dot(picks[0], ret[m, :, :d], ((1,), (0,)))
+            two = dot(picks[1], ret[m, :, :d], ((1,), (0,)))
+            d_rows = dot(picks[0] + picks[1], ret[m, :, d:], ((1,), (0,)))
+            cot = cot_all[m, image(i)].astype(F32)
+            gate = gates[m, image(i)]
+            mixture = gate[:, 0:1] * one + gate[:, 1:2] * two
+            col = lax.broadcasted_iota(jnp.int32, (rows, 128), 1)
+            dg = jnp.where(col == 0, jnp.sum(one * cot, axis=-1, keepdims=True), 0.0)
+            dg = dg + jnp.where(col == 1, jnp.sum(two * cot, axis=-1, keepdims=True), 0.0)
+            if i is other:
+                pay[m, :, :d] = mixture.astype(BF16)
+                pay[m, :, d : 2 * d] = d_rows.astype(BF16)
+                pay[m, :, 2 * d :] = dg.astype(BF16)
+                pay_copy(m).start()
+            else:
+                mix[m] = mixture
+                dx[m] = d_rows
+                dgate[m] = dg
+        return carry
+
+    lax.fori_loop(0, batches, combine, 0)
+
+    def settle(m, carry):
+        pay_copy(m).wait_recv()
+        mix[m] += paid[m, :, :d].astype(F32)
+        dx[m] += paid[m, :, d : 2 * d].astype(F32)
+        dgate[m] += paid[m, :, 2 * d :].astype(F32)
+        return carry
+
+    lax.fori_loop(0, batches, settle, 0)
+    grad_copy(0).wait()
+    grad_copy(1).wait()
+    gin_out[...] = gin[:, pl.ds(pl.multiple_of(t * half, 128), half)] + gin_got[...].astype(F32)
+    gout_out[...] = gout[pl.ds(pl.multiple_of(t * half, 128), half), :] + gout_got[...].astype(F32)
+
+    def drain(m, carry):
+        c_copy(m).wait_send()
+        pay_copy(m).wait_send()
+        every(lambda k: go_copy(m, k).wait_send())
+        every(lambda k: back_copy(m, k).wait_send())
+        return carry
+
+    lax.fori_loop(0, batches, drain, 0)
+
+
+def moe(c_own, cot_all, router, flat, expert_of, codes, win, wout, experts, n_dp):
+    batches, rows, d = c_own.shape
+    slots = codes.shape[0]
+    hidden = win.shape[1]
+    half = hidden // 2
+    dma = pltpu.SemaphoreType.DMA
+    return pl.pallas_call(
+        functools.partial(moe_kernel, experts),
+        out_shape=[
+            jax.ShapeDtypeStruct((batches, rows, d), F32),
+            jax.ShapeDtypeStruct((batches, rows, d), F32),
+            jax.ShapeDtypeStruct((batches, rows, 128), F32),
+            jax.ShapeDtypeStruct((d, half), F32),
+            jax.ShapeDtypeStruct((half, d), F32),
+        ],
+        in_specs=[ANYWHERE] * 10,
+        out_specs=[ANYWHERE] * 5,
+        scratch_shapes=[
+            pltpu.VMEM((batches, 2 * rows, d), BF16),
+            pltpu.VMEM((batches, 2 * rows, 128), F32),
+            pltpu.VMEM((batches, slots, 2 * d), BF16),
+            pltpu.VMEM((batches, slots, 2 * d), BF16),
+            pltpu.VMEM((batches, slots, 2 * d), BF16),
+            pltpu.VMEM((batches, slots, 2 * d), BF16),
+            pltpu.VMEM((batches, rows, 2 * d + 128), BF16),
+            pltpu.VMEM((batches, rows, 2 * d + 128), BF16),
+            pltpu.VMEM((slots, d), F32),
+            pltpu.VMEM((slots, d), F32),
+            pltpu.VMEM((d, hidden), F32),
+            pltpu.VMEM((hidden, d), F32),
+            pltpu.VMEM((d, half), BF16),
+            pltpu.VMEM((half, d), BF16),
+            pltpu.VMEM((d, half), BF16),
+            pltpu.VMEM((half, d), BF16),
+            dma((2, batches)),
+            dma((batches, n_dp - 1)),
+            dma((batches, n_dp - 1)),
+            dma((batches, n_dp - 1)),
+            dma((batches, n_dp - 1)),
+            dma((2, batches)),
+            dma((2, 2)),
+        ],
+        compiler_params=pltpu.CompilerParams(
+            collective_id=2, has_side_effects=True, vmem_limit_bytes=62 * 1024 * 1024
+        ),
+    )(
+        c_own,
+        cot_all,
+        router,
+        flat,
+        flat.transpose(0, 2, 1),
+        expert_of.transpose(0, 2, 1),
+        codes[None, :],
+        codes[:, None],
+        win,
+        wout,
+    )
+
+
 def local(
     tokens,
     w_qkv,
@@ -452,67 +758,98 @@
     hidden = x + live_own * attn
     normed_two = layer_norm(hidden, gain_two, shift_two).astype(BF16)
 
-    c_all = lax.all_gather(normed_two, "tensor", axis=1, tiled=True)
-    gate_probs = jax.nn.softmax(dot(c_all, router, ((2,), (0,))), axis=-1)
-    hits_one = (first[:, :, None] == labels).astype(F32)
-    hits_two = (second[:, :, None] == labels).astype(F32)
-    gate_one = jnp.sum(gate_probs * hits_one, axis=-1) * keep_one
-    gate_two = jnp.sum(gate_probs * hits_two, axis=-1) * keep_two
-    picked = (pick_one | pick_two).astype(BF16)
-    sent = jnp.einsum(
-        "mqr,mrd->mqd",
-        picked,
-        jnp.concatenate([c_all, cot_all], axis=-1),
-        preferred_element_type=F32,
-    )
-    gate_slot = jnp.sum(
-        jnp.where(pick_one, gate_one[:, None, :], 0.0) + jnp.where(pick_two, gate_two[:, None, :], 0.0),
-        axis=-1,
-        keepdims=True,
-    )
-    sent = jnp.concatenate(
-        [sent[..., :d].astype(BF16), (sent[..., d:] * gate_slot).astype(BF16)], axis=-1
-    )
-    sent = sent.reshape(batches, experts, share, 2 * d)
-    got = lax.all_to_all(sent, "dp", 1, 1, tiled=True).reshape(-1, 2 * d)
-    produced, d_in, grad_in, grad_out = expert(got[:, :d], got[:, d:], win, wout)
-    back = jnp.concatenate([produced, d_in], axis=-1).reshape(batches, n_dp, share, 2 * d)
-    back = lax.all_to_all(back, "dp", 1, 1, tiled=True).reshape(batches, experts * share, 2 * d)
-    grad_in = lax.psum_scatter(grad_in, "tensor", scatter_dimension=1, tiled=True).astype(F32)
-    grad_out = lax.psum_scatter(grad_out, "tensor", scatter_dimension=0, tiled=True).astype(F32)
-
-    part_one = jnp.einsum("mqr,mqd->mrd", pick_one.astype(BF16), back[..., :d], preferred_element_type=F32)
-    part_two = jnp.einsum("mqr,mqd->mrd", pick_two.astype(BF16), back[..., :d], preferred_element_type=F32)
-    d_rows = jnp.einsum("mqr,mqd->mrd", picked, back[..., d:], preferred_element_type=F32)
-    mixture = gate_one[:, :, None] * part_one + gate_two[:, :, None] * part_two
-    cot_wide = cot_all.astype(F32)
-    dgate_one = jnp.sum(part_one * cot_wide, axis=-1, keepdims=True)
-    dgate_two = jnp.sum(part_two * cot_wide, axis=-1, keepdims=True)
-    dgates = jnp.concatenate([dgate_one, dgate_two], axis=-1)
-    payload = jnp.concatenate(
-        [mixture, d_rows, jnp.pad(dgates, ((0, 0), (0, 0), (0, 126)))], axis=-1
-    ).astype(BF16)
-    pieces = payload.reshape(batches, n_t, work, payload.shape[-1])
-
-    def piece(k):
-        return lax.dynamic_index_in_dim(pieces, (t + k) % n_t, 1, keepdims=False)
-
-    payload = piece(0).astype(F32)
-    for k in range(1, n_t):
-        payload = payload + lax.ppermute(
-            piece(k), "tensor", [(j, (j + k) % n_t) for j in range(n_t)]
-        ).astype(F32)
-    output = (hidden + payload[..., :d]).astype(BF16)
-    dgates = payload[..., 2 * d : 2 * d + 2]
-
-    own_probs = own(gate_probs)
+    padded = -(-SEQ // 16) * 16
+    if direct:
+        def lay(v, fill=0):
+            v = v.reshape((batches, n_t, work) + v.shape[2:])
+            v = jnp.pad(v, ((0, 0), (0, 0), (0, padded - work)) + ((0, 0),) * (v.ndim - 3), constant_values=fill)
+            return v.reshape((batches, n_t * padded) + v.shape[3:])
+
+        flat = jnp.stack([lay(flat_one, -1), lay(flat_two, -1)], axis=1)
+        expert_of = jnp.stack(
+            [lay(jnp.where(keep_one, first, -1), -1), lay(jnp.where(keep_two, second, -1), -1)], axis=1
+        )
+        mixture, d_rows, dgates, grad_in, grad_out = moe(
+            jnp.pad(normed_two, ((0, 0), (0, padded - work), (0, 0))),
+            lay(cot_all),
+            jnp.pad(router, ((0, 0), (0, 128 - experts))),
+            flat,
+            expert_of,
+            codes,
+            win,
+            wout,
+            experts,
+            n_dp,
+        )
+        output = (hidden + mixture[:, :work]).astype(BF16)
+        d_rows = d_rows[:, :work]
+        dgates = dgates[:, :work, :2]
+        own_probs = jax.nn.softmax(dot(normed_two, router, ((2,), (0,))), axis=-1)
+        hits_one = (first[:, :, None] == labels).astype(F32)
+        hits_two = (second[:, :, None] == labels).astype(F32)
+    else:
+        c_all = lax.all_gather(normed_two, "tensor", axis=1, tiled=True)
+        gate_probs = jax.nn.softmax(dot(c_all, router, ((2,), (0,))), axis=-1)
+        hits_one = (first[:, :, None] == labels).astype(F32)
+        hits_two = (second[:, :, None] == labels).astype(F32)
+        gate_one = jnp.sum(gate_probs * hits_one, axis=-1) * keep_one
+        gate_two = jnp.sum(gate_probs * hits_two, axis=-1) * keep_two
+        picked = (pick_one | pick_two).astype(BF16)
+        sent = jnp.einsum(
+            "mqr,mrd->mqd",
+            picked,
+            jnp.concatenate([c_all, cot_all], axis=-1),
+            preferred_element_type=F32,
+        )
+        gate_slot = jnp.sum(
+            jnp.where(pick_one, gate_one[:, None, :], 0.0) + jnp.where(pick_two, gate_two[:, None, :], 0.0),
+            axis=-1,
+            keepdims=True,
+        )
+        sent = jnp.concatenate(
+            [sent[..., :d].astype(BF16), (sent[..., d:] * gate_slot).astype(BF16)], axis=-1
+        )
+        sent = sent.reshape(batches, experts, share, 2 * d)
+        got = lax.all_to_all(sent, "dp", 1, 1, tiled=True).reshape(-1, 2 * d)
+        produced, d_in, grad_in, grad_out = expert(got[:, :d], got[:, d:], win, wout)
+        back = jnp.concatenate([produced, d_in], axis=-1).reshape(batches, n_dp, share, 2 * d)
+        back = lax.all_to_all(back, "dp", 1, 1, tiled=True).reshape(batches, experts * share, 2 * d)
+        grad_in = lax.psum_scatter(grad_in, "tensor", scatter_dimension=1, tiled=True).astype(F32)
+        grad_out = lax.psum_scatter(grad_out, "tensor", scatter_dimension=0, tiled=True).astype(F32)
+
+        part_one = jnp.einsum("mqr,mqd->mrd", pick_one.astype(BF16), back[..., :d], preferred_element_type=F32)
+        part_two = jnp.einsum("mqr,mqd->mrd", pick_two.astype(BF16), back[..., :d], preferred_element_type=F32)
+        d_rows = jnp.einsum("mqr,mqd->mrd", picked, back[..., d:], preferred_element_type=F32)
+        mixture = gate_one[:, :, None] * part_one + gate_two[:, :, None] * part_two
+        cot_wide = cot_all.astype(F32)
+        dgate_one = jnp.sum(part_one * cot_wide, axis=-1, keepdims=True)
+        dgate_two = jnp.sum(part_two * cot_wide, axis=-1, keepdims=True)
+        dgates = jnp.concatenate([dgate_one, dgate_two], axis=-1)
+        payload = jnp.concatenate(
+            [mixture, d_rows, jnp.pad(dgates, ((0, 0), (0, 0), (0, 126)))], axis=-1
+        ).astype(BF16)
+        pieces = payload.reshape(batches, n_t, work, payload.shape[-1])
+
+        def piece(k):
+            return lax.dynamic_index_in_dim(pieces, (t + k) % n_t, 1, keepdims=False)
+
+        payload = piece(0).astype(F32)
+        for k in range(1, n_t):
+            payload = payload + lax.ppermute(
+                piece(k), "tensor", [(j, (j + k) % n_t) for j in range(n_t)]
+            ).astype(F32)
+        output = (hidden + payload[..., :d]).astype(BF16)
+        dgates = payload[..., 2 * d : 2 * d + 2]
+        d_rows = payload[..., d : 2 * d]
+        own_probs = own(gate_probs)
+
     dprobs = own(hits_one) * dgates[..., 0:1] * own(keep_one)[:, :, None]
     dprobs = dprobs + own(hits_two) * dgates[..., 1:2] * own(keep_two)[:, :, None]
     dlogits = own_probs * (dprobs - jnp.sum(dprobs * own_probs, axis=-1, keepdims=True))
     grad_router = lax.dot_general(
         normed_two.astype(F32), dlogits, (((0, 1), (0, 1)), ((), ())), precision=highest
     )
-    dc = payload[..., d : 2 * d] + lax.dot_general(
+    dc = d_rows + lax.dot_general(
         dlogits, router.astype(F32), (((2,), (1,)), ((), ())), precision=highest
     )
     _, back_two = jax.vjp(layer_norm, hidden, gain_two, shift_two)

time: 527 us -> 434 us (0.82); the launches traced: 519 us -> 433 us
  waiting for transfers between devices: 199 us -> 10.1 us
  Pallas kernels: 118 us -> 283 us
  local copies, waits for them, and re-layouts: 82.1 us -> 54.8 us
  starting transfers between devices: 23.6 us -> 8.23 us
  matrix products: 40.9 us -> 30.7 us
  other arithmetic: 39.8 us -> 31 us
    pallas_call x1, Pallas kernels: 35.3 us -> 191 us  [moe(): pl.pallas_call(functools.partial(moe_kernel, experts), out_shape=[jax.Sha...]
    all_to_all x2 -> x0, waiting for transfers between devices: 116 us -> none  [the longest x1 58.1 us: local(): lax.all_to_all(back, 'dp', 1, 1, tiled=True)]
    all_gather x1 -> x0, waiting for transfers between devices: 25.4 us -> none  [local(): c_all = lax.all_gather(normed_two, 'tensor', axis=1, tiled=True)]
    ppermute x1 -> x0, waiting for transfers between devices: 24.2 us -> none  [local(): lax.ppermute(piece(k), 'tensor', [(j, (j + k) % n_t) for j in range(n_t)])]
    all_gather x1, waiting for transfers between devices: 24 us -> 0.01 us  [local(): cot_all = lax.all_gather(cotangent, 'tensor', axis=1, tiled=True)]
    all_to_all x2 -> x0, starting transfers between devices: 14.5 us -> none  [the longest x1 8.84 us: local(): lax.all_to_all(back, 'dp', 1, 1, tiled=True)]
    dot_general x4 -> x0, matrix products: 10.6 us -> none  [the longest x1 3.98 us: local(): jnp.einsum('mqr,mqd->mrd', pick_one.astype(BF16), back[..., :d], preferre...]
    pallas_call x1, Pallas kernels: 31.9 us -> 41.4 us  [gather_weights(): pl.pallas_call(functools.partial(gather_kernel, ny, nz, n_t), out_shape=[...]
  transfers between devices with their start and end apart: 12 -> 6, of which waited for: 6 -> 1; matrix products, arithmetic and copies ran while one was open for 14% -> 15% of each run, Pallas kernels for 16% -> 21%
where the time goes in v3:
time: 434 us; the launch traced here: 433 us
  Pallas kernels  283 us (65%)
  local copies, waits for them, and re-layouts  54.8 us (13%)
  other arithmetic  31 us (7%)
  matrix products  30.7 us (7%)
  between operations  14.8 us (3%)
  waiting for transfers between devices  10.1 us (2%)
  starting transfers between devices  8.23 us (2%)
    pallas_call x1, Pallas kernels, moe(): pl.pallas_call(functools.partial(moe_kernel, experts), out_shape=[jax.Sha...  191 us
    pallas_call x1, Pallas kernels, scatter_grads(): pl.pallas_call(functools.partial(scatter_kernel, ny, nz, n_t), out_shape=...  50.9 us
    pallas_call x1, Pallas kernels, gather_weights(): pl.pallas_call(functools.partial(gather_kernel, ny, nz, n_t), out_shape=[...  41.4 us
    dot_general x6, matrix products, dot(): return lax.dot_general(a, b, (dims, ((), ())), preferred_element_type=F32)  11.3 us
    unnamed x171, local copies, waits for them, and re-layouts  9.77 us
    all_gather x1, waiting for transfers between devices, local(): wout = lax.all_gather(w_out[0], 'tensor', axis=0, tiled=True)  8.72 us
  transfers between devices with their start and end apart: 6, of which 1 were waited for; matrix products, arithmetic and copies ran while one was open for 15% of the time, Pallas kernels for 21%

profile of v3, /device:TPU:0, one launch (start us, length us, event | category | flops | bytes accessed | tf_op | source)
XLA Modules:
  0.0 432.7 jit_solution(8232100248539849684)
XLA Ops:
  9.5 5.6 %collective-permute-start = (bf16[3,59,512]{2,1,0:T(8,128)(2,1)}, bf16[3,59,512]{2,1,0:T(8,128)(2,1)}, u32[]{:S(2)}, u32[]{:S(2)}) collective-permute-start(bf16[3,59,512]{2,1,0:T(8,128)(2,1)} %slice.106), channel_id=1, source_target_pairs={{0,1},{2,3},{4,5},{6,7},{8,9},{10,11},{12,13},{14,15},{16,17},{18,... | collective-permute-start | bytes 543752 | tf_op jit(solution)/shard_map/ppermute | solution.py:699
  22.4 2.1 slice_convert_fusion
  28.0 41.4 %shard_map.221 = (bf16[4,2,2,32,1536]{4,3,2,1,0:T(8,128)(2,1)}, bf16[4,2,2,2,16,512]{5,4,3,2,1,0:T(8,128)(2,1)}, bf16[4,2,2,2,16,128]{5,4,3,2,1,0:T(8,128)(2,1)}) custom-call(bf16[32,768]{1,0:T(8,128)(2,1)} %reshape.259.qkv, bf16[16,512]{1,0:T(8,128)(2,1)} %reshape.260.proj, bf16[16,128]{1,0:T(8,128)(2,1)} %pad.33.small), custom_call_target="tpu_custom_call" | custom-call | tf_op jit(solution)/shard_map/pallas_call | solution.py:203
  69.4 2.2 convert_reduce_fusion.2
  81.1 3.0 fusion.56
  89.1 3.8 fusion.57
  92.9 3.1 convolution_convert_fusion.3
  102.6 2.5 pad.35
  105.1 8.7 %all-gather.10.cloned.1.call-done = bf16[1,2048,512]{2,1,0:T(8,128)(2,1)} async-done(((bf16[1,1024,512]{2,1,0:T(8,128)(2,1)}), bf16[1,2048,512]{2,1,0:T(8,128)(2,1)}) %all-gather.10.cloned.1.call-update) | async-done | bytes 2097168 | tf_op jit(solution)/shard_map/all_gather | solution.py:687
  113.8 190.6 %shard_map.222 = (f32[3,208,512]{2,1,0:T(8,128)}, f32[3,208,512]{2,1,0:T(8,128)}, f32[3,208,128]{2,1,0:T(8,128)}, f32[512,1024]{1,0:T(8,128)}, f32[1024,512]{1,0:T(8,128)}) custom-call(bf16[3,208,512]{2,1,0:T(8,128)(2,1)} %pad.34.c_own, bf16[3,416,512]{2,1,0:T(8,128)(2,1)} %bitcast.134, bf16[512,128]{1,0:T(8,128)(2,1)} %broadcast_select_fusion.router, ...), custom_call_target="tpu_custom_call" | custom-call | tf_op jit(solution)/shard_map/pallas_call | solution.py:584
  306.8 3.4 multiply_reduce_fusion.1
  314.9 3.8 multiply_reduce_fusion
  322.3 1.8 convolution_convert_fusion
  325.6 2.3 copy.143
  327.8 2.2 copy.144
  330.0 2.2 copy.145
  332.2 5.8 %pad_maximum_fusion = bf16[3,197,2,3,256]{4,3,2,1,0:T(4,128)(2,1)S(1)} fusion(bf16[3,197,2,1,256]{4,3,2,1,0:T(2,128)(2,1)} %copy.145, bf16[3,197,2,1,256]{4,3,2,1,0:T(2,128)(2,1)} %copy.144, bf16[3,197,2,1,256]{4,3,2,1,0:T(2,128)(2,1)} %copy.143), kind=kLoop, calls=%fused_computation.11 | loop fusion | flops 5446656 | bytes 3631104 | tf_op jit(solution)/shard_map/stack | solution.py:867
  338.0 3.3 reshape.271
  341.4 4.4 %fusion.3 = bf16[512,1536]{1,0:T(8,128)(2,1)} fusion(bf16[3,197,1536]{2,1,0:T(8,128)(2,1)} %reshape.271, bf16[3,197,512]{2,1,0:T(8,128)(2,1)S(1)} %get-tuple-element.91, f32[512]{0:T(512)S(1)} %copy-done.60, f32[512]{0:T(512)S(1)} %copy-done.40, f32[3,197]{1,0:T(4,128)S(1)} %fusion.46, f32[3,197]{1,0:T(4,128)S(1)} %broadcast_multiply_fusion.1), kind=kOutput, calls=%fused_computation.7 | convolution fusion | flops 932164608 | bytes 4002424 | tf_op jit(solution)/shard_map/dot_general | solution.py:19
  357.1 50.9 %shard_map.223 = (f32[32,768]{1,0:T(8,128)}, f32[16,512]{1,0:T(8,128)}, f32[16,128]{1,0:T(8,128)}) custom-call(bf16[4,2,2,32,1536]{4,3,2,1,0:T(8,128)(2,1)} %bitcast.145, bf16[4,2,2,2,16,512]{5,4,3,2,1,0:T(8,128)(2,1)} %reshape.274.refs_1_, f32[4,2,2,2,16,128]{5,4,3,2,1,0:T(8,128)} %bitcast.146), custom_call_target="tpu_custom_call" | custom-call | tf_op jit(solution)/shard_map/pallas_call | solution.py:321
  408.0 1.8 reshape.276
  411.5 1.8 reshape.277
  417.1 2.1 maximum_select_fusion.1
  419.2 2.7 maximum_select_fusion
  (288 shorter events, 66.5 us)
Async XLA Ops:
  7.2 92.6 %all-gather.6.cloned.1.call-start = ((), (), s32[]{:S(2)}) async-start(), calls=%async_computation | async-start | bytes 2359296 | tf_op jit(solution)/shard_map/all_gather | solution.py:688
  7.9 97.1 %all-gather.8.cloned.1.call-start = ((), (), s32[]{:S(2)}) async-start(), calls=%async_computation.1 | async-start | bytes 3145728 | tf_op jit(solution)/shard_map/all_gather | solution.py:686
  8.7 6.4 %copy-start.67 = (s32[3,512,2]{1,2,0:T(2,128)S(1)}, s32[3,512,2]{1,2,0:T(2,128)}, u32[]{:S(2)}) copy-start(s32[3,512,2]{1,2,0:T(2,128)} %param.25) | copy-start | bytes 36868
  8.7 6.4 %copy-start.62 = (s32[3,512]{1,0:T(4,128)S(1)}, s32[3,512]{1,0:T(4,128)}, u32[]{:S(2)}) copy-start(s32[3,512]{1,0:T(4,128)} %param.24) | copy-start | bytes 18436
  8.7 6.4 %copy-start.71 = (s32[3,1,512]{2,1,0:T(1,128)S(1)}, s32[3,1,512]{2,1,0:T(1,128)}, u32[]{:S(2)}) copy-start(s32[3,1,512]{2,1,0:T(1,128)} %param.26) | copy-start | bytes 18436
  8.7 105.1 %all-gather.10.cloned.1.call-start = ((), (), s32[]{:S(2)}) async-start(), calls=%async_computation.2 | async-start | bytes 3145728 | tf_op jit(solution)/shard_map/all_gather | solution.py:687
  9.5 69.9 %collective-permute-start = (bf16[3,59,512]{2,1,0:T(8,128)(2,1)}, bf16[3,59,512]{2,1,0:T(8,128)(2,1)}, u32[]{:S(2)}, u32[]{:S(2)}) collective-permute-start(bf16[3,59,512]{2,1,0:T(8,128)(2,1)} %slice.106), channel_id=1, source_target_pairs={{0,1},{2,3},{4,5},{6,7},{8,9},{10,11},{12,13},{14,15},{16,17},{18,... | collective-permute-start | bytes 543752 | tf_op jit(solution)/shard_map/ppermute | solution.py:699
  18.7 6.6 %copy-start.41 = (bf16[32,4,192]{2,1,0:T(4,128)(2,1)S(1)}, bf16[32,4,192]{2,1,0:T(4,128)(2,1)}, u32[]{:S(2)}) copy-start(bf16[32,4,192]{2,1,0:T(4,128)(2,1)} %param.15) | copy-start | bytes 147460
  22.4 4.9 %copy-start.72 = (bf16[16,16]{1,0:T(8,128)(2,1)S(1)}, bf16[16,16]{1,0:T(8,128)(2,1)}, u32[]{:S(2)}) copy-start(bf16[16,16]{1,0:T(8,128)(2,1)} %param.19) | copy-start | bytes 1540
  71.6 9.5 %copy-start.39 = (f32[512]{0:T(512)}, f32[512]{0:T(512)S(1)}, u32[]{:S(2)}) copy-start(f32[512]{0:T(512)S(1)} %get-tuple-element.78) | copy-start | bytes 6148
  71.6 9.5 %copy-start.59 = (f32[512]{0:T(512)}, f32[512]{0:T(512)S(1)}, u32[]{:S(2)}) copy-start(f32[512]{0:T(512)S(1)} %get-tuple-element.77) | copy-start | bytes 6148
  71.6 25.7 %copy-start.57 = (f32[512]{0:T(512)}, f32[512]{0:T(512)S(1)}, u32[]{:S(2)}) copy-start(f32[512]{0:T(512)S(1)} %get-tuple-element.75) | copy-start | bytes 6148
  87.4 5.5 %copy-start.9 = (bf16[3,197,2,1,256]{1,4,2,0,3:T(8,128)(2,1)}, bf16[3,197,2,1,256]{1,4,2,0,3:T(8,128)(2,1)S(1)}, u32[]{:S(2)}) copy-start(bf16[3,197,2,1,256]{1,4,2,0,3:T(8,128)(2,1)S(1)} %copy.125) | copy-start | bytes 1815556
  348.4 4.9 %copy-start.44 = (f32[3,197]{1,0:T(4,128)S(1)}, f32[3,197]{1,0:T(4,128)}, u32[]{:S(2)}) copy-start(f32[3,197]{1,0:T(4,128)} %copy-done.43) | copy-start | bytes 7096
  348.4 4.9 %copy-start.46 = (f32[3,197]{1,0:T(4,128)S(1)}, f32[3,197]{1,0:T(4,128)}, u32[]{:S(2)}) copy-start(f32[3,197]{1,0:T(4,128)} %copy-done.45) | copy-start | bytes 7096
  348.4 4.9 %copy-start.49 = (f32[3,197]{1,0:T(4,128)S(1)}, f32[3,197]{1,0:T(4,128)}, u32[]{:S(2)}) copy-start(f32[3,197]{1,0:T(4,128)} %dynamic-slice_convert_fusion.1) | copy-start | bytes 7096
  348.4 4.9 %copy-start.50 = (f32[3,197]{1,0:T(4,128)S(1)}, f32[3,197]{1,0:T(4,128)}, u32[]{:S(2)}) copy-start(f32[3,197]{1,0:T(4,128)} %dynamic-slice_convert_fusion.2) | copy-start | bytes 7096
  348.4 4.9 %copy-start.56 = (f32[3,197]{1,0:T(4,128)S(1)}, f32[3,197]{1,0:T(4,128)}, u32[]{:S(2)}) copy-start(f32[3,197]{1,0:T(4,128)} %copy-done.55) | copy-start | bytes 7096
  349.9 69.3 %collective-permute-start.2 = (f32[3,59,512]{2,1,0:T(8,128)}, f32[3,59,512]{2,1,0:T(8,128)}, u32[]{:S(2)}, u32[]{:S(2)}) collective-permute-start(f32[3,59,512]{2,1,0:T(8,128)} %slice.151), channel_id=1, source_target_pairs={{1,0},{3,2},{5,4},{7,6},{9,8},{11,10},{13,12},{15,14},{17,16},{19,... | collective-permute-start | bytes 1087496 | tf_op jit(solution)/shard_map/ppermute | solution.py:878
  351.9 65.2 %collective-permute-start.1 = (bf16[3,59,512]{2,1,0:T(8,128)(2,1)}, bf16[3,59,512]{2,1,0:T(8,128)(2,1)}, u32[]{:S(2)}, u32[]{:S(2)}) collective-permute-start(bf16[3,59,512]{2,1,0:T(8,128)(2,1)} %slice.148), channel_id=1, source_target_pairs={{1,0},{3,2},{5,4},{7,6},{9,8},{11,10},{13,12},{15,14},{17,16},{19,... | collective-permute-start | bytes 543752 | tf_op jit(solution)/shard_map/ppermute | solution.py:877
  408.0 8.4 %copy-start.32 = (f32[16,128]{1,0:T(8,128)S(1)}, f32[16,128]{1,0:T(8,128)}, u32[]{:S(2)}) copy-start(f32[16,128]{1,0:T(8,128)} %get-tuple-element.32) | copy-start | bytes 24580
  408.0 9.1 %copy-start.13 = (bf16[3,197,512]{2,1,0:T(8,128)(2,1)S(1)}, bf16[3,197,512]{2,1,0:T(8,128)(2,1)}, u32[]{:S(2)}) copy-start(bf16[3,197,512]{2,1,0:T(8,128)(2,1)} %get-tuple-element.94) | copy-start | bytes 1815556
  408.0 9.1 %copy-start.22 = (bf16[3,138,512]{2,1,0:T(8,128)(2,1)S(1)}, bf16[3,138,512]{2,1,0:T(8,128)(2,1)}, u32[]{:S(2)}) copy-start(bf16[3,138,512]{2,1,0:T(8,128)(2,1)} %slice.149) | copy-start | bytes 1271812
  408.0 9.1 %copy-start.24 = (bf16[3,118,512]{2,1,0:T(8,128)(2,1)S(1)}, bf16[3,118,512]{2,1,0:T(8,128)(2,1)}, u32[]{:S(2)}) copy-start(bf16[3,118,512]{2,1,0:T(8,128)(2,1)} %slice.125) | copy-start | bytes 1087492
  (65 other events, 169.9 us)
Sparse Core Ops, SparseCore 0:
  9.5 29.8 all-gather.5
  41.0 37.5 all-gather.7
  80.2 33.5 all-gather.9

commit v4 on v3

--- a/solution.py
+++ b/solution.py
@@ -137,10 +137,28 @@
     pl.semaphore_wait(barrier, count)
 
 
-def gather_kernel(ny, nz, n_t, qkv, proj, small, qkv_out, proj_out, small_out, send, recv, copied):
-    _, t, c, y, z = position(ny)
+def gather_kernel(ny, nz, n_t, extras, *refs):
+    (qkv, proj, small), refs = refs[:3], refs[3:]
+    side, refs = refs[:extras], refs[extras:]
+    (qkv_out, proj_out, small_out), refs = refs[:3], refs[3:]
+    side_out, (send, recv, copied) = refs[:extras], refs[extras:]
+    dp, t, c, y, z = position(ny)
     stages = neighbours(ny, nz, n_t)
     greet(stages)
+    aside = []
+    for i in range(extras):
+        aside.append(
+            pltpu.make_async_remote_copy(
+                src_ref=side[i],
+                dst_ref=side_out[i].at[t] if i == 0 else side_out[i],
+                send_sem=send.at[send.shape[0] - 1 - i],
+                recv_sem=recv.at[recv.shape[0] - 1 - i],
+                device_id=(dp, 1 - t),
+                device_id_type=MESH,
+            )
+        )
+    for copy in aside:
+        copy.start()
     cols = qkv.shape[1]
 
     def views(zs, ys, cs, ts):
@@ -157,6 +175,8 @@
         pltpu.make_async_copy(src, dst, copied.at[i])
         for i, (src, dst) in enumerate(zip((qkv, proj, small), mine))
     ]
+    if extras:
+        local.append(pltpu.make_async_copy(side[0], side_out[0].at[t], copied.at[3]))
     for copy in local:
         copy.start()
     slot = 0
@@ -195,29 +215,35 @@
                 copy.wait()
         for copy in copies:
             copy.wait()
-
-
-def gather_weights(qkv, proj, small, n_dp, n_t):
+    for copy in aside:
+        copy.wait()
+
+
+def gather_weights(qkv, proj, small, n_dp, n_t, side=()):
     nz, ny = grid_sizes(n_dp)
-    slots = 3 * (1 + (n_t - 1) + (ny - 1) + (nz - 1))
+    slots = 3 * (1 + (n_t - 1) + (ny - 1) + (nz - 1)) + len(side)
+    side_shapes = [
+        jax.ShapeDtypeStruct(((n_t,) if i == 0 else ()) + v.shape, v.dtype) for i, v in enumerate(side)
+    ]
     outs = pl.pallas_call(
-        functools.partial(gather_kernel, ny, nz, n_t),
+        functools.partial(gather_kernel, ny, nz, n_t, len(side)),
         out_shape=[
             jax.ShapeDtypeStruct((nz, ny, 2, qkv.shape[0], n_t * qkv.shape[1]), BF16),
             jax.ShapeDtypeStruct((nz, ny, 2, n_t) + proj.shape, BF16),
             jax.ShapeDtypeStruct((nz, ny, 2, n_t) + small.shape, BF16),
-        ],
-        in_specs=[ANYWHERE] * 3,
-        out_specs=[ANYWHERE] * 3,
+        ]
+        + side_shapes,
+        in_specs=[ANYWHERE] * (3 + len(side)),
+        out_specs=[ANYWHERE] * (3 + len(side)),
         scratch_shapes=[
             pltpu.SemaphoreType.DMA((slots,)),
             pltpu.SemaphoreType.DMA((slots,)),
-            pltpu.SemaphoreType.DMA((3,)),
+            pltpu.SemaphoreType.DMA((4,)),
         ],
         compiler_params=pltpu.CompilerParams(collective_id=0, has_side_effects=True),
-    )(qkv, proj, small)
+    )(qkv, proj, small, *side)
     qkv_all = outs[0].reshape(n_dp * qkv.shape[0], n_t * qkv.shape[1])
-    return qkv_all, outs[1].reshape((n_dp, n_t) + proj.shape), outs[2].reshape(-1, small.shape[1])
+    return (qkv_all, outs[1].reshape((n_dp, n_t) + proj.shape), outs[2].reshape(-1, small.shape[1])) + tuple(outs[3:])
 
 
 def scatter_kernel(ny, nz, n_t, *refs):
@@ -355,12 +381,17 @@
     paid,
     y_acc,
     dx_acc,
+    win_got,
+    wout_got,
+    gin_mine,
+    gout_mine,
     gin,
     gout,
     gin_half,
     gout_half,
     gin_got,
     gout_got,
+    w_sems,
     c_sems,
     go_send,
     go_recv,
@@ -374,7 +405,6 @@
     dp, t = lax.axis_index("dp"), lax.axis_index("tensor")
     share = sent.shape[1] // n_dp
     hidden = win.shape[1]
-    half = hidden // 2
     other = 1 - t
     partner = (dp, other)
 
@@ -433,15 +463,28 @@
         )
 
     def grad_copy(i):
+        src, dst = ((gin_half, gin_got), (gout_half, gout_got))[i // 2]
+        size = src.shape[0] // 2
+        band = pl.ds(i % 2 * size, size)
         return pltpu.make_async_remote_copy(
-            src_ref=(gin_half, gout_half)[i],
-            dst_ref=(gin_got, gout_got)[i],
+            src_ref=src.at[band],
+            dst_ref=dst.at[band],
             send_sem=grad_sems.at[0, i],
             recv_sem=grad_sems.at[1, i],
             device_id=partner,
             device_id_type=MESH,
         )
 
+    def w_copy(i):
+        return pltpu.make_async_remote_copy(
+            src_ref=(win, wout)[i],
+            dst_ref=(win_got, wout_got)[i],
+            send_sem=w_sems.at[0, i],
+            recv_sem=w_sems.at[1, i],
+            device_id=partner,
+            device_id_type=MESH,
+        )
+
     def every(body):
         def step(k, carry):
             body(k)
@@ -452,6 +495,8 @@
     for m in range(batches):
         c_copy(m).start()
         c_all[m, image(t)] = c_own[m]
+    w_copy(0).start()
+    w_copy(1).start()
 
     lane = lax.broadcasted_iota(jnp.int32, (2 * rows, router.shape[1]), 1)
 
@@ -482,8 +527,10 @@
 
     def clear(i, carry):
         cols = pl.ds(pl.multiple_of(i * tile, tile), tile)
-        gin[:, cols] = jnp.zeros((d, tile), F32)
-        gout[cols, :] = jnp.zeros((tile, d), F32)
+        for into in (gin, gin_mine):
+            into[:, cols] = jnp.zeros((d, tile), F32)
+        for into in (gout, gout_mine):
+            into[cols, :] = jnp.zeros((tile, d), F32)
         return carry
 
     lax.fori_loop(0, hidden // tile, clear, 0)
@@ -493,7 +540,7 @@
         y_acc[...] = jnp.zeros_like(y_acc)
         dx_acc[...] = jnp.zeros_like(dx_acc)
 
-        def chunk(i, inner):
+        def chunk(win, wout, gin, gout, i, inner):
             cols = pl.ds(pl.multiple_of(i * tile, tile), tile)
             x = got[m, :, :d]
             dprod = got[m, :, d:]
@@ -511,7 +558,18 @@
             dx_acc[...] += dot(dpre, w1, ((1,), (1,)))
             return inner
 
-        lax.fori_loop(0, hidden // tile, chunk, 0)
+        lax.fori_loop(
+            0, hidden // tile, functools.partial(chunk, win, wout, gin_mine, gout_mine), 0
+        )
+
+        @pl.when(m == 0)
+        def _():
+            w_copy(0).wait_recv()
+            w_copy(1).wait_recv()
+
+        lax.fori_loop(
+            0, hidden // tile, functools.partial(chunk, win_got, wout_got, gin, gout), 0
+        )
         back[m, :, :d] = y_acc[...].astype(BF16)
         back[m, :, d:] = dx_acc[...].astype(BF16)
         every(lambda k: back_copy(m, k).start())
@@ -520,10 +578,8 @@
 
     lax.fori_loop(0, batches, expert_step, 0)
 
-    gin_half[...] = gin[:, pl.ds(pl.multiple_of(other * half, 128), half)].astype(BF16)
-    gout_half[...] = gout[pl.ds(pl.multiple_of(other * half, 128), half), :].astype(BF16)
-    grad_copy(0).start()
-    grad_copy(1).start()
+    gin_half[...] = gin[...].astype(BF16)
+    gout_half[...] = gout[...].astype(BF16)
 
     def combine(m, carry):
         every(lambda k: back_copy(m, k).wait_recv())
@@ -550,7 +606,13 @@
                 dgate[m] = dg
         return carry
 
-    lax.fori_loop(0, batches, combine, 0)
+    pieces = 4
+    for m in range(batches):
+        if m < pieces:
+            grad_copy(m).start()
+        combine(m, 0)
+    for i in range(batches, pieces):
+        grad_copy(i).start()
 
     def settle(m, carry):
         pay_copy(m).wait_recv()
@@ -560,10 +622,12 @@
         return carry
 
     lax.fori_loop(0, batches, settle, 0)
-    grad_copy(0).wait()
-    grad_copy(1).wait()
-    gin_out[...] = gin[:, pl.ds(pl.multiple_of(t * half, 128), half)] + gin_got[...].astype(F32)
-    gout_out[...] = gout[pl.ds(pl.multiple_of(t * half, 128), half), :] + gout_got[...].astype(F32)
+    for i in range(pieces):
+        grad_copy(i).wait()
+    gin_out[...] = gin_mine[...] + gin_got[...].astype(F32)
+    gout_out[...] = gout_mine[...] + gout_got[...].astype(F32)
+    w_copy(0).wait_send()
+    w_copy(1).wait_send()
 
     def drain(m, carry):
         c_copy(m).wait_send()
@@ -578,8 +642,7 @@
 def moe(c_own, cot_all, router, flat, expert_of, codes, win, wout, experts, n_dp):
     batches, rows, d = c_own.shape
     slots = codes.shape[0]
-    hidden = win.shape[1]
-    half = hidden // 2
+    half = win.shape[1]
     dma = pltpu.SemaphoreType.DMA
     return pl.pallas_call(
         functools.partial(moe_kernel, experts),
@@ -603,19 +666,24 @@
             pltpu.VMEM((batches, rows, 2 * d + 128), BF16),
             pltpu.VMEM((slots, d), F32),
             pltpu.VMEM((slots, d), F32),
-            pltpu.VMEM((d, hidden), F32),
-            pltpu.VMEM((hidden, d), F32),
+            pltpu.VMEM((d, half), BF16),
+            pltpu.VMEM((half, d), BF16),
+            pltpu.VMEM((d, half), F32),
+            pltpu.VMEM((half, d), F32),
+            pltpu.VMEM((d, half), F32),
+            pltpu.VMEM((half, d), F32),
             pltpu.VMEM((d, half), BF16),
             pltpu.VMEM((half, d), BF16),
             pltpu.VMEM((d, half), BF16),
             pltpu.VMEM((half, d), BF16),
+            dma((2, 2)),
             dma((2, batches)),
             dma((batches, n_dp - 1)),
             dma((batches, n_dp - 1)),
             dma((batches, n_dp - 1)),
             dma((batches, n_dp - 1)),
             dma((2, batches)),
-            dma((2, 2)),
+            dma((2, 4)),
         ],
         compiler_params=pltpu.CompilerParams(
             collective_id=2, has_side_effects=True, vmem_limit_bytes=62 * 1024 * 1024
@@ -634,7 +702,7 @@
     )
 
 
-def local(
+def general(
     tokens,
     w_qkv,
     w_proj,
@@ -758,98 +826,67 @@
     hidden = x + live_own * attn
     normed_two = layer_norm(hidden, gain_two, shift_two).astype(BF16)
 
-    padded = -(-SEQ // 16) * 16
-    if direct:
-        def lay(v, fill=0):
-            v = v.reshape((batches, n_t, work) + v.shape[2:])
-            v = jnp.pad(v, ((0, 0), (0, 0), (0, padded - work)) + ((0, 0),) * (v.ndim - 3), constant_values=fill)
-            return v.reshape((batches, n_t * padded) + v.shape[3:])
-
-        flat = jnp.stack([lay(flat_one, -1), lay(flat_two, -1)], axis=1)
-        expert_of = jnp.stack(
-            [lay(jnp.where(keep_one, first, -1), -1), lay(jnp.where(keep_two, second, -1), -1)], axis=1
-        )
-        mixture, d_rows, dgates, grad_in, grad_out = moe(
-            jnp.pad(normed_two, ((0, 0), (0, padded - work), (0, 0))),
-            lay(cot_all),
-            jnp.pad(router, ((0, 0), (0, 128 - experts))),
-            flat,
-            expert_of,
-            codes,
-            win,
-            wout,
-            experts,
-            n_dp,
-        )
-        output = (hidden + mixture[:, :work]).astype(BF16)
-        d_rows = d_rows[:, :work]
-        dgates = dgates[:, :work, :2]
-        own_probs = jax.nn.softmax(dot(normed_two, router, ((2,), (0,))), axis=-1)
-        hits_one = (first[:, :, None] == labels).astype(F32)
-        hits_two = (second[:, :, None] == labels).astype(F32)
-    else:
-        c_all = lax.all_gather(normed_two, "tensor", axis=1, tiled=True)
-        gate_probs = jax.nn.softmax(dot(c_all, router, ((2,), (0,))), axis=-1)
-        hits_one = (first[:, :, None] == labels).astype(F32)
-        hits_two = (second[:, :, None] == labels).astype(F32)
-        gate_one = jnp.sum(gate_probs * hits_one, axis=-1) * keep_one
-        gate_two = jnp.sum(gate_probs * hits_two, axis=-1) * keep_two
-        picked = (pick_one | pick_two).astype(BF16)
-        sent = jnp.einsum(
-            "mqr,mrd->mqd",
-            picked,
-            jnp.concatenate([c_all, cot_all], axis=-1),
-            preferred_element_type=F32,
-        )
-        gate_slot = jnp.sum(
-            jnp.where(pick_one, gate_one[:, None, :], 0.0) + jnp.where(pick_two, gate_two[:, None, :], 0.0),
-            axis=-1,
-            keepdims=True,
-        )
-        sent = jnp.concatenate(
-            [sent[..., :d].astype(BF16), (sent[..., d:] * gate_slot).astype(BF16)], axis=-1
-        )
-        sent = sent.reshape(batches, experts, share, 2 * d)
-        got = lax.all_to_all(sent, "dp", 1, 1, tiled=True).reshape(-1, 2 * d)
-        produced, d_in, grad_in, grad_out = expert(got[:, :d], got[:, d:], win, wout)
-        back = jnp.concatenate([produced, d_in], axis=-1).reshape(batches, n_dp, share, 2 * d)
-        back = lax.all_to_all(back, "dp", 1, 1, tiled=True).reshape(batches, experts * share, 2 * d)
-        grad_in = lax.psum_scatter(grad_in, "tensor", scatter_dimension=1, tiled=True).astype(F32)
-        grad_out = lax.psum_scatter(grad_out, "tensor", scatter_dimension=0, tiled=True).astype(F32)
-
-        part_one = jnp.einsum("mqr,mqd->mrd", pick_one.astype(BF16), back[..., :d], preferred_element_type=F32)
-        part_two = jnp.einsum("mqr,mqd->mrd", pick_two.astype(BF16), back[..., :d], preferred_element_type=F32)
-        d_rows = jnp.einsum("mqr,mqd->mrd", picked, back[..., d:], preferred_element_type=F32)
-        mixture = gate_one[:, :, None] * part_one + gate_two[:, :, None] * part_two
-        cot_wide = cot_all.astype(F32)
-        dgate_one = jnp.sum(part_one * cot_wide, axis=-1, keepdims=True)
-        dgate_two = jnp.sum(part_two * cot_wide, axis=-1, keepdims=True)
-        dgates = jnp.concatenate([dgate_one, dgate_two], axis=-1)
-        payload = jnp.concatenate(
-            [mixture, d_rows, jnp.pad(dgates, ((0, 0), (0, 0), (0, 126)))], axis=-1
-        ).astype(BF16)
-        pieces = payload.reshape(batches, n_t, work, payload.shape[-1])
-
-        def piece(k):
-            return lax.dynamic_index_in_dim(pieces, (t + k) % n_t, 1, keepdims=False)
-
-        payload = piece(0).astype(F32)
-        for k in range(1, n_t):
-            payload = payload + lax.ppermute(
-                piece(k), "tensor", [(j, (j + k) % n_t) for j in range(n_t)]
-            ).astype(F32)
-        output = (hidden + payload[..., :d]).astype(BF16)
-        dgates = payload[..., 2 * d : 2 * d + 2]
-        d_rows = payload[..., d : 2 * d]
-        own_probs = own(gate_probs)
-
+    c_all = lax.all_gather(normed_two, "tensor", axis=1, tiled=True)
+    gate_probs = jax.nn.softmax(dot(c_all, router, ((2,), (0,))), axis=-1)
+    hits_one = (first[:, :, None] == labels).astype(F32)
+    hits_two = (second[:, :, None] == labels).astype(F32)
+    gate_one = jnp.sum(gate_probs * hits_one, axis=-1) * keep_one
+    gate_two = jnp.sum(gate_probs * hits_two, axis=-1) * keep_two
+    picked = (pick_one | pick_two).astype(BF16)
+    sent = jnp.einsum(
+        "mqr,mrd->mqd",
+        picked,
+        jnp.concatenate([c_all, cot_all], axis=-1),
+        preferred_element_type=F32,
+    )
+    gate_slot = jnp.sum(
+        jnp.where(pick_one, gate_one[:, None, :], 0.0) + jnp.where(pick_two, gate_two[:, None, :], 0.0),
+        axis=-1,
+        keepdims=True,
+    )
+    sent = jnp.concatenate(
+        [sent[..., :d].astype(BF16), (sent[..., d:] * gate_slot).astype(BF16)], axis=-1
+    )
+    sent = sent.reshape(batches, experts, share, 2 * d)
+    got = lax.all_to_all(sent, "dp", 1, 1, tiled=True).reshape(-1, 2 * d)
+    produced, d_in, grad_in, grad_out = expert(got[:, :d], got[:, d:], win, wout)
+    back = jnp.concatenate([produced, d_in], axis=-1).reshape(batches, n_dp, share, 2 * d)
+    back = lax.all_to_all(back, "dp", 1, 1, tiled=True).reshape(batches, experts * share, 2 * d)
+    grad_in = lax.psum_scatter(grad_in, "tensor", scatter_dimension=1, tiled=True).astype(F32)
+    grad_out = lax.psum_scatter(grad_out, "tensor", scatter_dimension=0, tiled=True).astype(F32)
+
+    part_one = jnp.einsum("mqr,mqd->mrd", pick_one.astype(BF16), back[..., :d], preferred_element_type=F32)
+    part_two = jnp.einsum("mqr,mqd->mrd", pick_two.astype(BF16), back[..., :d], preferred_element_type=F32)
+    d_rows = jnp.einsum("mqr,mqd->mrd", picked, back[..., d:], preferred_element_type=F32)
+    mixture = gate_one[:, :, None] * part_one + gate_two[:, :, None] * part_two
+    cot_wide = cot_all.astype(F32)
+    dgate_one = jnp.sum(part_one * cot_wide, axis=-1, keepdims=True)
+    dgate_two = jnp.sum(part_two * cot_wide, axis=-1, keepdims=True)
+    dgates = jnp.concatenate([dgate_one, dgate_two], axis=-1)
+    payload = jnp.concatenate(
+        [mixture, d_rows, jnp.pad(dgates, ((0, 0), (0, 0), (0, 126)))], axis=-1
+    ).astype(BF16)
+    pieces = payload.reshape(batches, n_t, work, payload.shape[-1])
+
+    def piece(k):
+        return lax.dynamic_index_in_dim(pieces, (t + k) % n_t, 1, keepdims=False)
+
+    payload = piece(0).astype(F32)
+    for k in range(1, n_t):
+        payload = payload + lax.ppermute(
+            piece(k), "tensor", [(j, (j + k) % n_t) for j in range(n_t)]
+        ).astype(F32)
+    output = (hidden + payload[..., :d]).astype(BF16)
+    dgates = payload[..., 2 * d : 2 * d + 2]
+
+    own_probs = own(gate_probs)
     dprobs = own(hits_one) * dgates[..., 0:1] * own(keep_one)[:, :, None]
     dprobs = dprobs + own(hits_two) * dgates[..., 1:2] * own(keep_two)[:, :, None]
     dlogits = own_probs * (dprobs - jnp.sum(dprobs * own_probs, axis=-1, keepdims=True))
     grad_router = lax.dot_general(
         normed_two.astype(F32), dlogits, (((0, 1), (0, 1)), ((), ())), precision=highest
     )
-    dc = d_rows + lax.dot_general(
+    dc = payload[..., d : 2 * d] + lax.dot_general(
         dlogits, router.astype(F32), (((2,), (1,)), ((), ())), precision=highest
     )
     _, back_two = jax.vjp(layer_norm, hidden, gain_two, shift_two)
@@ -921,6 +958,383 @@
         smalls[:, experts + 2],
         smalls[:, experts + 3],
     )
+
+
+def standardise(v):
+    centre = jnp.mean(v, axis=-1, keepdims=True)
+    centered = v - centre
+    inverse = lax.rsqrt(jnp.mean(centered * centered, axis=-1, keepdims=True) + EPS)
+    return centered * inverse, inverse
+
+
+def norm_back(grad, unit, inverse):
+    return inverse * (
+        grad
+        - jnp.mean(grad, axis=-1, keepdims=True)
+        - unit * jnp.mean(grad * unit, axis=-1, keepdims=True)
+    )
+
+
+def two_parts(v):
+    high = v.astype(BF16)
+    return high, (v - high.astype(F32)).astype(BF16)
+
+
+def gate_softmax(c, router, experts):
+    lane = lax.broadcasted_iota(jnp.int32, (c.shape[0], router.shape[1]), 1)
+    logits = jnp.where(lane < experts, dot(c, router, ((1,), (0,))), -1e30)
+    raised = jnp.exp(logits - jnp.max(logits, axis=-1, keepdims=True))
+    return raised / jnp.sum(raised, axis=-1, keepdims=True), lane
+
+
+def key_softmax(query, keys, count):
+    scores = dot(query, keys, ((1,), (1,)))
+    col = lax.broadcasted_iota(jnp.int32, scores.shape, 1)
+    scores = jnp.where(col < count, scores, -1e30)
+    raised = jnp.exp(scores - jnp.max(scores, axis=-1, keepdims=True))
+    return raised * (1.0 / jnp.sum(raised, axis=-1, keepdims=True))
+
+
+def pairs(n_t, block):
+    return [
+        (3 * block * s + 128 * i, block * s + 128 * i) for s in range(n_t) for i in range(block // 128)
+    ]
+
+
+def attend_kernel(n_t, block, count, factor, x, live, norms, qkv, proj, c_out, hidden_out, mixed_out, context_out):
+    xf = x[0].astype(F32)
+    unit, _ = standardise(xf)
+    a = (unit * norms[0:1] + norms[1:2]).astype(BF16)
+    for s in range(n_t):
+        for i in range(3):
+            cols = slice((3 * s + i) * block, (3 * s + i + 1) * block)
+            part = dot(a, qkv[:, cols], ((1,), (0,)))
+            mixed_out[0, :, cols] = (part * factor if i == 0 else part).astype(BF16)
+    low = lax.broadcasted_iota(jnp.int32, (x.shape[1], 128), 1) < 64
+    for col, dest in pairs(n_t, block):
+        query = mixed_out[0, :, col : col + 128]
+        keys = mixed_out[0, :, col + block : col + block + 128]
+        values = mixed_out[0, :, col + 2 * block : col + 2 * block + 128]
+        zero = jnp.zeros_like(query)
+        parts = []
+        for own in (low, ~low):
+            probs = key_softmax(jnp.where(own, query, zero), keys, count)
+            parts.append(dot(probs.astype(BF16), values, ((1,), (0,))))
+        context_out[0, :, dest : dest + 128] = jnp.where(low, parts[0], parts[1]).astype(BF16)
+    hidden = xf + live[0] * dot(context_out[0], proj[...], ((1,), (0,)))
+    hidden_out[0] = hidden
+    unit, _ = standardise(hidden)
+    c_out[0] = (unit * norms[2:3] + norms[3:4]).astype(BF16)
+
+
+def attend(x, live, norms, qkv, proj, n_t, block, count, factor):
+    batches, rows, d = x.shape
+    wide = qkv.shape[1]
+
+    def each(n):
+        return pl.BlockSpec((1, rows, n), lambda m: (m, 0, 0))
+
+    def fixed(shape):
+        return pl.BlockSpec(shape, lambda m: (0, 0))
+
+    return pl.pallas_call(
+        functools.partial(attend_kernel, n_t, block, count, factor),
+        grid=(batches,),
+        in_specs=[each(d), each(1), fixed(norms.shape), fixed(qkv.shape), fixed(proj.shape)],
+        out_specs=[each(d), each(d), each(wide), each(d)],
+        out_shape=[
+            jax.ShapeDtypeStruct((batches, rows, d), BF16),
+            jax.ShapeDtypeStruct((batches, rows, d), F32),
+            jax.ShapeDtypeStruct((batches, rows, wide), BF16),
+            jax.ShapeDtypeStruct((batches, rows, d), BF16),
+        ],
+        compiler_params=pltpu.CompilerParams(vmem_limit_bytes=32 * 1024 * 1024),
+        cost_estimate=pl.CostEstimate(
+            flops=2 * batches * rows * d * (wide + d), transcendentals=0, bytes_accessed=8 * batches * rows * d
+        ),
+    )(x, live, norms, qkv, proj)
+
+
+def retreat_kernel(
+    n_t,
+    block,
+    count,
+    factor,
+    experts,
+    x,
+    hidden_in,
+    mixed,
+    context,
+    mix,
+    d_rows,
+    dgate,
+    dy,
+    live,
+    expert_own,
+    norms,
+    qkv,
+    proj,
+    router,
+    out,
+    grad_x,
+    gqkv_out,
+    gproj_out,
+    grouter,
+    gnorms,
+    dmixed,
+    gqkv,
+    gproj,
+):
+    step = pl.program_id(0)
+
+    @pl.when(step == 0)
+    def _():
+        gqkv[...] = jnp.zeros_like(gqkv)
+        gproj[...] = jnp.zeros_like(gproj)
+        grouter[...] = jnp.zeros_like(grouter)
+        gnorms[...] = jnp.zeros_like(gnorms)
+
+    hidden = hidden_in[0]
+    out[0] = (hidden + mix[0]).astype(BF16)
+    unit, inverse = standardise(hidden)
+    c = (unit * norms[2:3] + norms[3:4]).astype(BF16)
+    probs, lane = gate_softmax(c, router[...], experts)
+    dprobs = jnp.where(lane == expert_own[0, :, 0:1], dgate[0, :, 0:1], 0.0)
+    dprobs = dprobs + jnp.where(lane == expert_own[0, :, 1:2], dgate[0, :, 1:2], 0.0)
+    dlogits = probs * (dprobs - jnp.sum(dprobs * probs, axis=-1, keepdims=True))
+    dc = d_rows[0]
+    for piece in two_parts(dlogits):
+        grouter[...] += dot(c, piece, ((0,), (0,)))
+        dc = dc + dot(piece, router[...], ((1,), (1,)))
+    gnorms[2:3] += jnp.sum(dc * unit, axis=0, keepdims=True)
+    gnorms[3:4] += jnp.sum(dc, axis=0, keepdims=True)
+    dhidden = dy[0].astype(F32) + norm_back(dc * norms[2:3], unit, inverse)
+    dattn = (live[0] * dhidden).astype(BF16)
+    gproj[...] += dot(context[0], dattn, ((0,), (0,)))
+    dcontext = dot(dattn, proj[...], ((1,), (1,))).astype(BF16)
+    low = lax.broadcasted_iota(jnp.int32, (x.shape[1], 128), 1) < 64
+    for col, dest in pairs(n_t, block):
+        query = mixed[0, :, col : col + 128]
+        keys = mixed[0, :, col + block : col + block + 128]
+        values = mixed[0, :, col + 2 * block : col + 2 * block + 128]
+        grads = dcontext[:, dest : dest + 128]
+        zero = jnp.zeros_like(query)
+        parts = []
+        for own in (low, ~low):
+            probs = key_softmax(jnp.where(own, query, zero), keys, count)
+            dvalues = dot(probs.astype(BF16), grads, ((0,), (0,)))
+            dweights = dot(jnp.where(own, grads, zero), values, ((1,), (1,)))
+            dscores = probs * (dweights - jnp.sum(dweights * probs, axis=-1, keepdims=True))
+            dscores = dscores.astype(BF16)
+            parts.append(
+                (dot(dscores, keys, ((1,), (0,))), dot(dscores, query, ((0,), (0,))), dvalues)
+            )
+        for i in range(3):
+            both = jnp.where(low, parts[0][i], parts[1][i]).astype(BF16)
+            if i == 0:
+                both = both * BF16(factor)
+            dmixed[:, col + i * block : col + i * block + 128] = both
+    xf = x[0].astype(F32)
+    unit, inverse = standardise(xf)
+    a = (unit * norms[0:1] + norms[1:2]).astype(BF16)
+    gqkv[...] += dot(a, dmixed[...], ((0,), (0,)))
+    da = dot(dmixed[...], qkv[...], ((1,), (1,)))
+    gnorms[0:1] += jnp.sum(da * unit, axis=0, keepdims=True)
+    gnorms[1:2] += jnp.sum(da, axis=0, keepdims=True)
+    grad_x[0] = dhidden + norm_back(da * norms[0:1], unit, inverse)
+
+    @pl.when(step == pl.num_programs(0) - 1)
+    def _():
+        gqkv_out[...] = gqkv[...].astype(BF16)
+        gproj_out[...] = gproj[...].astype(BF16)
+
+
+def retreat(x, saved, arrived, dy, live, expert_own, norms, qkv, proj, router, n_t, block, count, factor, experts):
+    batches, rows, d = x.shape
+    wide = qkv.shape[1]
+
+    def each(n):
+        return pl.BlockSpec((1, rows, n), lambda m: (m, 0, 0))
+
+    def fixed(v):
+        return pl.BlockSpec(v.shape, lambda m: (0, 0))
+
+    whole = [
+        jax.ShapeDtypeStruct((d, wide), BF16),
+        jax.ShapeDtypeStruct((d, d), BF16),
+        jax.ShapeDtypeStruct((d, router.shape[1]), F32),
+        jax.ShapeDtypeStruct((8, d), F32),
+    ]
+    return pl.pallas_call(
+        functools.partial(retreat_kernel, n_t, block, count, factor, experts),
+        grid=(batches,),
+        in_specs=[each(d), each(d), each(wide), each(d), each(d), each(d), each(128), each(d), each(1), each(2)]
+        + [fixed(v) for v in (norms, qkv, proj, router)],
+        out_specs=[each(d), each(d)] + [fixed(v) for v in whole],
+        out_shape=[
+            jax.ShapeDtypeStruct((batches, rows, d), BF16),
+            jax.ShapeDtypeStruct((batches, rows, d), F32),
+        ]
+        + whole,
+        scratch_shapes=[
+            pltpu.VMEM((rows, wide), BF16),
+            pltpu.VMEM((d, wide), F32),
+            pltpu.VMEM((d, d), F32),
+        ],
+        compiler_params=pltpu.CompilerParams(vmem_limit_bytes=48 * 1024 * 1024),
+        cost_estimate=pl.CostEstimate(
+            flops=6 * batches * rows * d * (wide + d), transcendentals=0, bytes_accessed=16 * batches * rows * d
+        ),
+    )(x, *saved, *arrived, dy, live, expert_own, norms, qkv, proj, router)
+
+
+def fast(
+    tokens,
+    w_qkv,
+    w_proj,
+    w_in,
+    w_out,
+    w_router,
+    gain_attn,
+    shift_attn,
+    gain_moe,
+    shift_moe,
+    live_rows,
+    chosen,
+    priority,
+    cotangent,
+):
+    batches, own_rows, d = tokens.shape
+    rows = live_rows.shape[1]
+    n_dp = lax.axis_size("dp")
+    n_t = lax.axis_size("tensor")
+    t = lax.axis_index("tensor")
+    heads_here = w_qkv.shape[1]
+    width = w_qkv.shape[2] // 3
+    block = heads_here * width
+    experts = n_dp
+    cap = 2 * rows // experts
+    share = cap // n_t
+    span = n_t * SEQ
+    padded = -(-SEQ // 16) * 16
+    edge = own_rows - SEQ
+    factor = width ** (-0.5)
+
+    small = jnp.concatenate(
+        [w_router] + [v[:, None] for v in (gain_attn, shift_attn, gain_moe, shift_moe)], axis=1
+    )
+    small = jnp.pad(small, ((0, 0), (0, 128 - small.shape[1])))
+    qkv_block = w_qkv.reshape(-1, heads_here, 3, width).transpose(0, 2, 1, 3).reshape(-1, 3 * block)
+    qkv, proj, small, cot_all, moved = gather_weights(
+        qkv_block, w_proj.reshape(-1, d), small, n_dp, n_t, (cotangent, tokens[:, SEQ:])
+    )
+    cot_all = cot_all.transpose(1, 0, 2, 3).reshape(batches, rows, d)
+    router = jnp.where(jnp.arange(128) < experts, small, 0)
+    norms = jnp.pad(small[:, experts : experts + 4].astype(F32).T, ((0, 4), (0, 0)))
+    proj = proj.reshape(n_dp, n_t, heads_here, w_proj.shape[1], d)
+    proj = proj.transpose(1, 2, 0, 3, 4).reshape(n_t * block, d)
+
+    def pad_rows(v, axis, fill=0):
+        spec = [(0, 0)] * v.ndim
+        spec[axis] = (0, padded - SEQ)
+        return jnp.pad(v, spec, constant_values=fill)
+
+    def lay(v, axis, fill=0):
+        shape = v.shape
+        v = v.reshape(shape[:axis] + (n_t, SEQ) + shape[axis + 1 :])
+        v = pad_rows(v, axis + 1, fill)
+        return v.reshape(shape[:axis] + (n_t * padded,) + shape[axis + 1 :])
+
+    def own(v, axis):
+        return lax.dynamic_slice_in_dim(v, t * padded, padded, axis)
+
+    x = jnp.where(t == 0, tokens[:, :SEQ], jnp.concatenate([moved, tokens[:, : SEQ - edge]], axis=1))
+    x = pad_rows(x, 1)
+    cot_all = lay(cot_all[:, :span], 1)
+
+    live = live_rows[:, :span]
+    rank = priority[:, 0, :span]
+    picks = chosen[:, :span].transpose(0, 2, 1)
+    labels = jnp.arange(experts, dtype=jnp.int32)
+    earlier = (rank[:, None, :] < rank[:, :, None]).astype(BF16)
+    hits = (picks[..., None] == labels).astype(F32)
+    live_hits = hits * live[:, None, :, None].astype(F32)
+    ahead = jnp.einsum("mrs,mkse->mkre", earlier, live_hits.astype(BF16), preferred_element_type=F32)
+    firsts = jnp.sum(live_hits[:, :1], axis=2, keepdims=True)
+    ahead = ahead + jnp.concatenate([jnp.zeros_like(firsts), firsts], axis=1)
+    slot = jnp.sum(ahead * hits, axis=-1).astype(jnp.int32)
+    keep = (live[:, None, :] > 0) & (slot < cap)
+    flat = lay(jnp.where(keep, picks * cap + slot, -1), 2, -1)
+    expert_of = lay(jnp.where(keep, picks, -1), 2, -1)
+    codes = (jnp.arange(experts)[:, None] * cap + t * share + jnp.arange(share)[None, :]).reshape(-1)
+    live_own = own(lay(live.astype(F32)[:, :, None], 1), 1)
+
+    c, hidden, mixed, context = attend(x, live_own, norms, qkv, proj, n_t, block, SEQ, factor)
+    mixture, d_rows, dgates, grad_in, grad_out = moe(
+        c, cot_all, router, flat, expert_of, codes, w_in[0], w_out[0], experts, n_dp
+    )
+    output, grad_x, grad_qkv, grad_proj, grad_router, grad_norms = retreat(
+        x,
+        (hidden, mixed, context),
+        (mixture, d_rows, dgates),
+        own(cot_all, 1),
+        live_own,
+        own(expert_of, 2).transpose(0, 2, 1),
+        norms,
+        qkv,
+        proj,
+        router,
+        n_t,
+        block,
+        SEQ,
+        factor,
+        experts,
+    )
+
+    out_edge = lax.ppermute(output[:, :edge], "tensor", [(1, 0)])
+    grad_edge = lax.ppermute(grad_x[:, :edge], "tensor", [(1, 0)])
+    rest = SEQ - edge
+
+    def home(v, moved_rows, other):
+        return jnp.where(
+            t == 0,
+            jnp.concatenate([v[:, :SEQ], moved_rows], axis=1),
+            jnp.concatenate([v[:, edge:SEQ], other[:, rest:].astype(v.dtype)], axis=1),
+        )
+
+    nz, ny = grid_sizes(n_dp)
+    grad_proj = grad_proj.reshape(n_t, heads_here, n_dp, -1, d)
+    grad_proj = grad_proj.transpose(2, 0, 1, 3, 4).reshape(nz, ny, 2, n_t, -1, d)
+    lane = jnp.arange(128)
+    smalls = jnp.where(lane < experts, grad_router, 0.0)
+    smalls = smalls + jnp.pad(grad_norms[:4].T, ((0, 0), (experts, 124 - experts)))
+    grad_qkv, grad_proj, smalls = scatter_grads(
+        grad_qkv.reshape(nz, ny, 2, d // n_dp, -1), grad_proj, smalls.reshape(nz, ny, 2, n_t, -1, 128), n_dp, n_t
+    )
+    grad_qkv = grad_qkv.reshape(-1, 3, heads_here, width).transpose(0, 2, 1, 3)
+    return (
+        home(output, out_edge, tokens),
+        home(grad_x, grad_edge, cotangent),
+        grad_qkv.reshape(w_qkv.shape),
+        grad_proj.reshape(w_proj.shape),
+        grad_in[None],
+        grad_out[None],
+        smalls[:, :experts],
+        smalls[:, experts],
+        smalls[:, experts + 1],
+        smalls[:, experts + 2],
+        smalls[:, experts + 3],
+    )
+
+
+def local(*args):
+    tokens, w_qkv, live_rows = args[0], args[1], args[10]
+    n_t = lax.axis_size("tensor")
+    images = live_rows.shape[1] // SEQ
+    block = w_qkv.shape[1] * (w_qkv.shape[2] // 3)
+    if n_t == 2 and images == 2 and tokens.shape[1] >= SEQ and block % 128 == 0 and w_qkv.shape[2] == 192:
+        return fast(*args)
+    return general(*args)
 
 
 def solution(mesh):

time: 434 us -> 377 us (0.87)
  Pallas kernels: 283 us -> 317 us
  matrix products: 30.7 us -> 0.65 us
  other arithmetic: 31 us -> 11.6 us
  between operations: 14.8 us -> 1.16 us
  local copies, waits for them, and re-layouts: 54.8 us -> 43.3 us
  waiting for transfers between devices: 10.1 us -> 0.01 us
  starting transfers between devices: 8.23 us -> 2.56 us
    pallas_call x1 -> x3, Pallas kernels: 41.4 us -> 77.3 us  [the longest x1 45.9 us: gather_weights(): pl.pallas_call(functools.partial(gather_kernel, ny, nz, n_t, len(side)),...]
    dot_general x14 -> x1, matrix products: 26 us -> 0.65 us  [fast(): jnp.einsum('mrs,mkse->mkre', earlier, live_hits.astype(BF16), preferred_e...]
    another operation x10 -> x3, local copies, waits for them, and re-layouts: 10.6 us -> 0.4 us  [the longest x2 0.31 us: fast(): proj = proj.reshape(n_dp, n_t, heads_here, w_proj.shape[1], d)]
    pallas_call x1, Pallas kernels: 191 us -> 182 us  [moe(): pl.pallas_call(functools.partial(moe_kernel, experts), out_shape=[jax.Sha...]
    all_gather x3 -> x0, waiting for transfers between devices: 8.72 us -> none  [the longest x1 8.72 us: local(): wout = lax.all_gather(w_out[0], 'tensor', axis=0, tiled=True)]
    pallas_call x1, Pallas kernels: 50.9 us -> 58.2 us  [scatter_grads(): pl.pallas_call(functools.partial(scatter_kernel, ny, nz, n_t), out_shape=...]
    convert_element_type x10 -> x2, other arithmetic: 9.55 us -> 2.76 us  [the longest x1 1.96 us: home(): other[:, rest:].astype(v.dtype)]
    another operation x3 -> x0, other arithmetic: 6.09 us -> none  [the longest x1 5.83 us: local(): jnp.stack([v.reshape(batches, work, n_t, block) for v in (dquery * BF16(f...]
  transfers between devices with their start and end apart: 6 -> 2, of which waited for: 1 -> 0; matrix products, arithmetic and copies ran while one was open for 15% -> 5% of each run, Pallas kernels for 21% -> 15%
where the time goes in v4:
time: 377 us; the launch traced here: 376 us
  Pallas kernels  317 us (84%)
  local copies, waits for them, and re-layouts  43.3 us (11%)
  other arithmetic  11.6 us (3%)
    pallas_call x1, Pallas kernels, moe(): pl.pallas_call(functools.partial(moe_kernel, experts), out_shape=[jax.Sha...  182 us
    pallas_call x1, Pallas kernels, scatter_grads(): pl.pallas_call(functools.partial(scatter_kernel, ny, nz, n_t), out_shape=...  58.2 us
    pallas_call x1, Pallas kernels, gather_weights(): pl.pallas_call(functools.partial(gather_kernel, ny, nz, n_t, len(side)),...  45.9 us
    pallas_call x1, Pallas kernels, retreat(): pl.pallas_call(functools.partial(retreat_kernel, n_t, block, count, facto...  25 us
    unnamed x77, local copies, waits for them, and re-layouts  14.2 us
  transfers between devices with their start and end apart: 2, of which 0 were waited for; matrix products, arithmetic and copies ran while one was open for 5% of the time, Pallas kernels for 15%

profile of v4, /device:TPU:0, one launch (start us, length us, event | category | flops | bytes accessed | tf_op | source)
XLA Modules:
  0.0 376.4 jit_solution(12074272036297643471)
XLA Ops:
  0.7 1.7 slice.70.refs_4_
  9.5 45.9 %shard_map.221 = (bf16[4,2,2,32,1536]{4,3,2,1,0:T(8,128)(2,1)}, bf16[4,2,2,2,16,512]{5,4,3,2,1,0:T(8,128)(2,1)}, bf16[4,2,2,2,16,128]{5,4,3,2,1,0:T(8,128)(2,1)}...) custom-call(bf16[32,768]{1,0:T(8,128)(2,1)} %reshape.145.refs_0_, bf16[16,512]{1,0:T(8,128)(2,1)} %reshape.146.refs_1_, ...), custom_call_target="tpu_custom_call" | custom-call | tf_op jit(solution)/shard_map/pallas_call | solution.py:228
  55.5 1.2 maximum_select_fusion.2
  61.0 1.5 copy.71
  62.6 1.2 reshape.152
  63.8 1.4 pad.39
  65.3 1.4 constant_dynamic-slice_fusion.1.live
  67.5 6.4 %shard_map.222 = (bf16[3,208,512]{2,1,0:T(8,128)(2,1)S(1)}, f32[3,208,512]{2,1,0:T(8,128)S(1)}, bf16[3,208,1536]{2,1,0:T(8,128)(2,1)S(1)}, bf16[3,208,512]{2,1,0:T(8,128)(2,1)S(1)}) custom-call(bf16[3,208,512]{2,1,0:T(8,128)(2,1)S(1)} %pad.35.x, f32[3,208,1]{2,1,0:T(8,128)S(1)} %constant_dynamic-slice_fusion.1.live, f32[8,512]{1,0:T(8,128)S(1)} %copy.70.norms, ...), custom_call_target="tpu_custom_call" | custom-call | flops 1308622848 | bytes 2555904 | tf_op jit(solution)/shard_map/pallas_call | solution.py:1040
  74.8 1.3 copy-done.9
  77.9 181.6 %shard_map.223 = (f32[3,208,512]{2,1,0:T(8,128)}, f32[3,208,512]{2,1,0:T(8,128)}, f32[3,208,128]{2,1,0:T(8,128)}, f32[512,1024]{1,0:T(8,128)}, f32[1024,512]{1,0:T(8,128)}) custom-call(bf16[3,208,512]{2,1,0:T(8,128)(2,1)} %copy-done, bf16[3,416,512]{2,1,0:T(8,128)(2,1)} %bitcast.82, bf16[512,128]{1,0:T(8,128)(2,1)} %broadcast_select_fusion.router, ...), custom_call_target="tpu_custom_call" | custom-call | tf_op jit(solution)/shard_map/pallas_call | solution.py:647
  263.5 25.0 %shard_map.224 = (bf16[3,208,512]{2,1,0:T(8,128)(2,1)S(1)}, f32[3,208,512]{2,1,0:T(8,128)}, bf16[512,1536]{1,0:T(8,128)(2,1)}, bf16[512,512]{1,0:T(8,128)(2,1)S(...) custom-call(bf16[3,208,512]{2,1,0:T(8,128)(2,1)S(1)} %pad.35.x, f32[3,208,512]{2,1,0:T(8,128)} %copy-done.10, ...), custom_call_target="tpu_custom_call" | custom-call | flops 3925868544 | bytes 5111808 | tf_op jit(solution)/shard_map/pallas_call | solution.py:1168
  289.2 1.9 slice.83
  291.1 1.3 collective-permute-start.1
  293.1 1.3 collective-permute-start
  294.4 2.0 slice_convert_fusion
  297.3 1.1 slice.82
  301.9 58.2 %shard_map.225 = (f32[32,768]{1,0:T(8,128)}, f32[16,512]{1,0:T(8,128)}, f32[16,128]{1,0:T(8,128)}) custom-call(bf16[4,2,2,32,1536]{4,3,2,1,0:T(8,128)(2,1)} %bitcast.93, bf16[4,2,2,2,16,512]{5,4,3,2,1,0:T(8,128)(2,1)} %reshape.160.refs_1_, f32[4,2,2,2,16,128]{5,4,3,2,1,0:T(8,128)} %bitcast.95), custom_call_target="tpu_custom_call" | custom-call | tf_op jit(solution)/shard_map/pallas_call | solution.py:347
  362.0 1.3 reshape.163
  364.0 1.4 reshape.164
  365.4 1.6 slice_reduce_fusion.1
  367.0 2.4 maximum_select_fusion.1
  369.4 2.7 maximum_select_fusion
  372.1 1.3 copy.96
  374.4 1.3 copy.97
  (135 shorter events, 28.9 us)
Async XLA Ops:
  0.6 6.2 %copy-start.26 = (bf16[32,4,192]{2,1,0:T(4,128)(2,1)S(1)}, bf16[32,4,192]{2,1,0:T(4,128)(2,1)}, u32[]{:S(2)}) copy-start(bf16[32,4,192]{2,1,0:T(4,128)(2,1)} %param.15) | copy-start | bytes 147460
  0.7 7.2 %copy-start.31 = (bf16[16]{0:T(256)(128)(2,1)S(1)}, bf16[16]{0:T(256)(128)(2,1)}, u32[]{:S(2)}) copy-start(bf16[16]{0:T(256)(128)(2,1)} %param.20) | copy-start | bytes 100
  0.7 7.3 %copy-start.32 = (bf16[16]{0:T(256)(128)(2,1)S(1)}, bf16[16]{0:T(256)(128)(2,1)}, u32[]{:S(2)}) copy-start(bf16[16]{0:T(256)(128)(2,1)} %param.21) | copy-start | bytes 100
  0.7 7.3 %copy-start.33 = (bf16[16]{0:T(256)(128)(2,1)S(1)}, bf16[16]{0:T(256)(128)(2,1)}, u32[]{:S(2)}) copy-start(bf16[16]{0:T(256)(128)(2,1)} %param.22) | copy-start | bytes 100
  0.7 7.4 %copy-start.34 = (bf16[16]{0:T(256)(128)(2,1)S(1)}, bf16[16]{0:T(256)(128)(2,1)}, u32[]{:S(2)}) copy-start(bf16[16]{0:T(256)(128)(2,1)} %param.23) | copy-start | bytes 100
  0.7 7.5 %copy-start.28 = (bf16[4,4,512]{2,1,0:T(4,128)(2,1)S(1)}, bf16[4,4,512]{2,1,0:T(4,128)(2,1)}, u32[]{:S(2)}) copy-start(bf16[4,4,512]{2,1,0:T(4,128)(2,1)} %param.16) | copy-start | bytes 49156
  0.7 8.1 %copy-start.30 = (bf16[16,16]{1,0:T(8,128)(2,1)S(1)}, bf16[16,16]{1,0:T(8,128)(2,1)}, u32[]{:S(2)}) copy-start(bf16[16,16]{1,0:T(8,128)(2,1)} %param.19) | copy-start | bytes 1540
  2.4 53.0 %copy-start.18 = (bf16[3,256,512]{2,1,0:T(8,128)(2,1)S(1)}, bf16[3,256,512]{2,1,0:T(8,128)(2,1)}, u32[]{:S(2)}) copy-start(bf16[3,256,512]{2,1,0:T(8,128)(2,1)} %param.14) | copy-start | bytes 2359300
  2.4 53.0 %slice-start = ((bf16[3,256,512]{2,1,0:T(8,128)(2,1)}), bf16[3,138,512]{2,1,0:T(8,128)(2,1)S(1)}, s32[]{:S(2)}) async-start(bf16[3,256,512]{2,1,0:T(8,128)(2,1)} %param.14), calls=%async_computation | async-start | bytes 884736 | tf_op jit(solution)/shard_map/slice | solution.py:1251
  55.5 1.5 copy-start.23
  58.9 3.5 copy-start.14
  60.2 6.4 %copy-start.17 = (s32[3,2,2,208]{1,3,2,0:T(8,128)}, s32[3,2,2,208]{1,3,2,0:T(8,128)S(1)}, u32[]{:S(2)}) copy-start(s32[3,2,2,208]{1,3,2,0:T(8,128)S(1)} %pad.41) | copy-start | bytes 29956
  65.2 8.7 %copy-start.13 = (bf16[3,2,208,512]{3,2,1,0:T(8,128)(2,1)}, bf16[3,2,208,512]{3,2,1,0:T(8,128)(2,1)S(1)}, u32[]{:S(2)}) copy-start(bf16[3,2,208,512]{3,2,1,0:T(8,128)(2,1)S(1)} %pad.39) | copy-start | bytes 3833860
  65.2 2.3 copy-start.7
  66.6 7.3 %copy-start.2 = (f32[3,208,1]{2,1,0:T(8,128)}, f32[3,208,1]{2,1,0:T(8,128)S(1)}, u32[]{:S(2)}) copy-start(f32[3,208,1]{2,1,0:T(8,128)S(1)} %constant_dynamic-slice_fusion.1.live) | copy-start | bytes 7492
  77.9 181.6 %copy-start.1 = (bf16[512,128]{1,0:T(8,128)(2,1)S(1)}, bf16[512,128]{1,0:T(8,128)(2,1)}, u32[]{:S(2)}) copy-start(bf16[512,128]{1,0:T(8,128)(2,1)} %broadcast_select_fusion.router) | copy-start | bytes 393220
  289.2 7.3 %copy-start.6 = (f32[512,128]{1,0:T(8,128)S(1)}, f32[512,128]{1,0:T(8,128)}, u32[]{:S(2)}) copy-start(f32[512,128]{1,0:T(8,128)} %copy-done.5) | copy-start | bytes 786436
  289.2 8.1 %copy-start.15 = (f32[3,208,512]{2,1,0:T(8,128)S(1)}, f32[3,208,512]{2,1,0:T(8,128)}, u32[]{:S(2)}) copy-start(f32[3,208,512]{2,1,0:T(8,128)} %get-tuple-element.47) | copy-start | bytes 3833860
  291.1 78.3 %collective-permute-start.1 = (f32[3,59,512]{2,1,0:T(8,128)}, f32[3,59,512]{2,1,0:T(8,128)}, u32[]{:S(2)}, u32[]{:S(2)}) collective-permute-start(f32[3,59,512]{2,1,0:T(8,128)} %slice.83), channel_id=1, source_target_pairs={{1,0},{3,2},{5,4},{7,6},{9,8},{11,10},{13,12},{15,14},{17,16},{19,... | collective-permute-start | bytes 1087496 | tf_op jit(solution)/shard_map/ppermute | solution.py:1295
  293.1 73.9 %collective-permute-start = (bf16[3,59,512]{2,1,0:T(8,128)(2,1)}, bf16[3,59,512]{2,1,0:T(8,128)(2,1)}, u32[]{:S(2)}, u32[]{:S(2)}) collective-permute-start(bf16[3,59,512]{2,1,0:T(8,128)(2,1)} %slice.79), channel_id=1, source_target_pairs={{1,0},{3,2},{5,4},{7,6},{9,8},{11,10},{13,12},{15,14},{17,16},{19,... | collective-permute-start | bytes 543752 | tf_op jit(solution)/shard_map/ppermute | solution.py:1294
  362.0 7.4 %copy-start.16 = (f32[3,197,512]{2,1,0:T(8,128)S(1)}, f32[3,197,512]{2,1,0:T(8,128)}, u32[]{:S(2)}) copy-start(f32[3,197,512]{2,1,0:T(8,128)} %slice.82) | copy-start | bytes 3631108
  362.0 7.4 %copy-start.20 = (f32[3,118,512]{2,1,0:T(8,128)S(1)}, f32[3,118,512]{2,1,0:T(8,128)}, u32[]{:S(2)}) copy-start(f32[3,118,512]{2,1,0:T(8,128)} %slice_convert_fusion) | copy-start | bytes 2174980
  369.4 2.7 copy-start.22
  372.1 2.3 copy-start.21
  (14 other events, 14.2 us)

commit v5 on v4

--- a/solution.py
+++ b/solution.py
@@ -354,8 +354,53 @@
     )(qkv, proj, small)
 
 
+def standardise(v):
+    centre = jnp.mean(v, axis=-1, keepdims=True)
+    centered = v - centre
+    inverse = lax.rsqrt(jnp.mean(centered * centered, axis=-1, keepdims=True) + EPS)
+    return centered * inverse, inverse
+
+
+def norm_back(grad, unit, inverse):
+    return inverse * (
+        grad
+        - jnp.mean(grad, axis=-1, keepdims=True)
+        - unit * jnp.mean(grad * unit, axis=-1, keepdims=True)
+    )
+
+
+def two_parts(v):
+    high = v.astype(BF16)
+    return high, (v - high.astype(F32)).astype(BF16)
+
+
+def gate_softmax(c, router, experts):
+    lane = lax.broadcasted_iota(jnp.int32, (c.shape[0], router.shape[1]), 1)
+    logits = jnp.where(lane < experts, dot(c, router, ((1,), (0,))), -1e30)
+    raised = jnp.exp(logits - jnp.max(logits, axis=-1, keepdims=True))
+    return raised / jnp.sum(raised, axis=-1, keepdims=True), lane
+
+
+def key_softmax(query, keys, count):
+    scores = dot(query, keys, ((1,), (1,)))
+    col = lax.broadcasted_iota(jnp.int32, scores.shape, 1)
+    scores = jnp.where(col < count, scores, -1e30)
+    raised = jnp.exp(scores - jnp.max(scores, axis=-1, keepdims=True))
+    return raised * (1.0 / jnp.sum(raised, axis=-1, keepdims=True))
+
+
+def pairs(n_t, block):
+    return [
+        (3 * block * s + 128 * i, block * s + 128 * i) for s in range(n_t) for i in range(block // 128)
+    ]
+
+
 def moe_kernel(
     experts,
+    n_t,
+    block,
+    count,
+    factor,
     c_own,
     cot_all,
     router,
@@ -366,25 +411,39 @@
     code_col,
     win,
     wout,
-    mix,
-    dx,
-    dgate,
-    gin_out,
-    gout_out,
+    x_in,
+    hidden_in,
+    mixed,
+    context,
+    live,
+    norms,
+    qkv,
+    proj,
+    out,
+    grad_x,
+    gqkv_out,
+    gproj_out,
+    grouter,
+    gnorms,
+    gin_mine,
+    gout_mine,
     c_all,
     gates,
     sent,
     got,
-    back,
     ret,
     pay,
     paid,
+    mix,
+    dx,
+    dgate,
+    dmixed,
+    gqkv,
+    gproj,
     y_acc,
     dx_acc,
     win_got,
     wout_got,
-    gin_mine,
-    gout_mine,
     gin,
     gout,
     gin_half,
@@ -450,7 +509,7 @@
 
     def back_copy(m, k):
         to = (dp + k) % n_dp
-        return remote(back.at[m, part(to)], ret.at[m, part(dp)], (back_send, back_recv), m, k - 1, (to, t))
+        return remote(got.at[m, part(to)], ret.at[m, part(dp)], (back_send, back_recv), m, k - 1, (to, t))
 
     def pay_copy(m):
         return pltpu.make_async_remote_copy(
@@ -570,10 +629,10 @@
         lax.fori_loop(
             0, hidden // tile, functools.partial(chunk, win_got, wout_got, gin, gout), 0
         )
-        back[m, :, :d] = y_acc[...].astype(BF16)
-        back[m, :, d:] = dx_acc[...].astype(BF16)
+        got[m, :, :d] = y_acc[...].astype(BF16)
+        got[m, :, d:] = dx_acc[...].astype(BF16)
         every(lambda k: back_copy(m, k).start())
-        ret[m, part(dp)] = back[m, part(dp)]
+        ret[m, part(dp)] = got[m, part(dp)]
         return carry
 
     lax.fori_loop(0, batches, expert_step, 0)
@@ -606,26 +665,92 @@
                 dgate[m] = dg
         return carry
 
+    gqkv[...] = jnp.zeros_like(gqkv)
+    gproj[...] = jnp.zeros_like(gproj)
+    grouter[...] = jnp.zeros_like(grouter)
+    gnorms[...] = jnp.zeros_like(gnorms)
+    low = lax.broadcasted_iota(jnp.int32, (rows, 128), 1) < 64
+
+    def retreat(m):
+        pay_copy(m).wait_recv()
+        hidden = hidden_in[m]
+        out[m] = (hidden + mix[m] + paid[m, :, :d].astype(F32)).astype(BF16)
+        unit, inverse = standardise(hidden)
+        c = (unit * norms[2:3] + norms[3:4]).astype(BF16)
+        probs, lane = gate_softmax(c, router[...], experts)
+        dg = dgate[m] + paid[m, :, 2 * d :].astype(F32)
+        dprobs = jnp.zeros_like(probs)
+        for k in range(2):
+            dprobs = dprobs + jnp.where(lane == expert_col[m, image(t), k : k + 1], dg[:, k : k + 1], 0.0)
+        dlogits = probs * (dprobs - jnp.sum(dprobs * probs, axis=-1, keepdims=True))
+        dc = dx[m] + paid[m, :, d : 2 * d].astype(F32)
+        for piece in two_parts(dlogits):
+            grouter[...] += dot(c, piece, ((0,), (0,)))
+            dc = dc + dot(piece, router[...], ((1,), (1,)))
+        gnorms[2:3] += jnp.sum(dc * unit, axis=0, keepdims=True)
+        gnorms[3:4] += jnp.sum(dc, axis=0, keepdims=True)
+        dhidden = cot_all[m, image(t)].astype(F32) + norm_back(dc * norms[2:3], unit, inverse)
+        grad_x[m] = dhidden
+        dattn = (live[m] * dhidden).astype(BF16)
+        gproj[...] += dot(context[m], dattn, ((0,), (0,)))
+        dcontext = dot(dattn, proj[...], ((1,), (1,))).astype(BF16)
+        for col, dest in pairs(n_t, block):
+            query = mixed[m, :, col : col + 128]
+            keys = mixed[m, :, col + block : col + block + 128]
+            values = mixed[m, :, col + 2 * block : col + 2 * block + 128]
+            grads = dcontext[:, dest : dest + 128]
+            zero = jnp.zeros_like(query)
+            parts = []
+            for own in (low, ~low):
+                probs = key_softmax(jnp.where(own, query, zero), keys, count)
+                dvalues = dot(probs.astype(BF16), grads, ((0,), (0,)))
+                dweights = dot(jnp.where(own, grads, zero), values, ((1,), (1,)))
+                dscores = probs * (dweights - jnp.sum(dweights * probs, axis=-1, keepdims=True))
+                dscores = dscores.astype(BF16)
+                parts.append(
+                    (dot(dscores, keys, ((1,), (0,))), dot(dscores, query, ((0,), (0,))), dvalues)
+                )
+            for i in range(3):
+                both = jnp.where(low, parts[0][i], parts[1][i]).astype(BF16)
+                if i == 0:
+                    both = both * BF16(factor)
+                dmixed[:, col + i * block : col + i * block + 128] = both
+        unit, inverse = standardise(x_in[m].astype(F32))
+        a = (unit * norms[0:1] + norms[1:2]).astype(BF16)
+        gqkv[...] += dot(a, dmixed[...], ((0,), (0,)))
+        da = dot(dmixed[...], qkv[...], ((1,), (1,)))
+        gnorms[0:1] += jnp.sum(da * unit, axis=0, keepdims=True)
+        gnorms[1:2] += jnp.sum(da, axis=0, keepdims=True)
+        grad_x[m] += norm_back(da * norms[0:1], unit, inverse)
+
     pieces = 4
-    for m in range(batches):
-        if m < pieces:
-            grad_copy(m).start()
-        combine(m, 0)
-    for i in range(batches, pieces):
+
+    def finish(m, carry):
+        for i in range(pieces):
+
+            @pl.when(m == i)
+            def _(i=i):
+                grad_copy(i).start()
+
+        @pl.when(m < batches)
+        def _():
+            combine(m, 0)
+
+        @pl.when(m > 0)
+        def _():
+            retreat(m - 1)
+
+        return carry
+
+    lax.fori_loop(0, batches + 1, finish, 0)
+    for i in range(batches + 1, pieces):
         grad_copy(i).start()
-
-    def settle(m, carry):
-        pay_copy(m).wait_recv()
-        mix[m] += paid[m, :, :d].astype(F32)
-        dx[m] += paid[m, :, d : 2 * d].astype(F32)
-        dgate[m] += paid[m, :, 2 * d :].astype(F32)
-        return carry
-
-    lax.fori_loop(0, batches, settle, 0)
+    gqkv_out[...] = gqkv[...].astype(BF16)
+    gproj_out[...] = gproj[...].astype(BF16)
     for i in range(pieces):
         grad_copy(i).wait()
-    gin_out[...] = gin_mine[...] + gin_got[...].astype(F32)
-    gout_out[...] = gout_mine[...] + gout_got[...].astype(F32)
+    gin_mine[...] += gin_got[...].astype(F32)
+    gout_mine[...] += gout_got[...].astype(F32)
     w_copy(0).wait_send()
     w_copy(1).wait_send()
 
@@ -639,37 +764,44 @@
     lax.fori_loop(0, batches, drain, 0)
 
 
-def moe(c_own, cot_all, router, flat, expert_of, codes, win, wout, experts, n_dp):
+def moe(c_own, cot_all, router, flat, expert_of, codes, win, wout, saved, experts, n_dp, n_t, block, count, factor):
     batches, rows, d = c_own.shape
     slots = codes.shape[0]
     half = win.shape[1]
+    wide = saved[2].shape[2]
     dma = pltpu.SemaphoreType.DMA
     return pl.pallas_call(
-        functools.partial(moe_kernel, experts),
+        functools.partial(moe_kernel, experts, n_t, block, count, factor),
         out_shape=[
+            jax.ShapeDtypeStruct((batches, rows, d), BF16),
             jax.ShapeDtypeStruct((batches, rows, d), F32),
-            jax.ShapeDtypeStruct((batches, rows, d), F32),
-            jax.ShapeDtypeStruct((batches, rows, 128), F32),
+            jax.ShapeDtypeStruct((d, wide), BF16),
+            jax.ShapeDtypeStruct((d, d), BF16),
+            jax.ShapeDtypeStruct((d, router.shape[1]), F32),
+            jax.ShapeDtypeStruct((8, d), F32),
             jax.ShapeDtypeStruct((d, half), F32),
             jax.ShapeDtypeStruct((half, d), F32),
         ],
-        in_specs=[ANYWHERE] * 10,
-        out_specs=[ANYWHERE] * 5,
+        in_specs=[ANYWHERE] * 18,
+        out_specs=[ANYWHERE] * 8,
         scratch_shapes=[
             pltpu.VMEM((batches, 2 * rows, d), BF16),
             pltpu.VMEM((batches, 2 * rows, 128), F32),
             pltpu.VMEM((batches, slots, 2 * d), BF16),
             pltpu.VMEM((batches, slots, 2 * d), BF16),
             pltpu.VMEM((batches, slots, 2 * d), BF16),
-            pltpu.VMEM((batches, slots, 2 * d), BF16),
             pltpu.VMEM((batches, rows, 2 * d + 128), BF16),
             pltpu.VMEM((batches, rows, 2 * d + 128), BF16),
+            pltpu.VMEM((batches, rows, d), F32),
+            pltpu.VMEM((batches, rows, d), F32),
+            pltpu.VMEM((batches, rows, 128), F32),
+            pltpu.VMEM((rows, wide), BF16),
+            pltpu.VMEM((d, wide), F32),
+            pltpu.VMEM((d, d), F32),
             pltpu.VMEM((slots, d), F32),
             pltpu.VMEM((slots, d), F32),
             pltpu.VMEM((d, half), BF16),
             pltpu.VMEM((half, d), BF16),
-            pltpu.VMEM((d, half), F32),
-            pltpu.VMEM((half, d), F32),
             pltpu.VMEM((d, half), F32),
             pltpu.VMEM((half, d), F32),
             pltpu.VMEM((d, half), BF16),
@@ -686,7 +818,7 @@
             dma((2, 4)),
         ],
         compiler_params=pltpu.CompilerParams(
-            collective_id=2, has_side_effects=True, vmem_limit_bytes=62 * 1024 * 1024
+            collective_id=2, has_side_effects=True, vmem_limit_bytes=67043328
         ),
     )(
         c_own,
@@ -699,6 +831,7 @@
         codes[:, None],
         win,
         wout,
+        *saved,
     )
 
 
@@ -960,47 +1093,6 @@
     )
 
 
-def standardise(v):
-    centre = jnp.mean(v, axis=-1, keepdims=True)
-    centered = v - centre
-    inverse = lax.rsqrt(jnp.mean(centered * centered, axis=-1, keepdims=True) + EPS)
-    return centered * inverse, inverse
-
-
-def norm_back(grad, unit, inverse):
-    return inverse * (
-        grad
-        - jnp.mean(grad, axis=-1, keepdims=True)
-        - unit * jnp.mean(grad * unit, axis=-1, keepdims=True)
-    )
-
-
-def two_parts(v):
-    high = v.astype(BF16)
-    return high, (v - high.astype(F32)).astype(BF16)
-
-
-def gate_softmax(c, router, experts):
-    lane = lax.broadcasted_iota(jnp.int32, (c.shape[0], router.shape[1]), 1)
-    logits = jnp.where(lane < experts, dot(c, router, ((1,), (0,))), -1e30)
-    raised = jnp.exp(logits - jnp.max(logits, axis=-1, keepdims=True))
-    return raised / jnp.sum(raised, axis=-1, keepdims=True), lane
-
-
-def key_softmax(query, keys, count):
-    scores = dot(query, keys, ((1,), (1,)))
-    col = lax.broadcasted_iota(jnp.int32, scores.shape, 1)
-    scores = jnp.where(col < count, scores, -1e30)
-    raised = jnp.exp(scores - jnp.max(scores, axis=-1, keepdims=True))
-    return raised * (1.0 / jnp.sum(raised, axis=-1, keepdims=True))
-
-
-def pairs(n_t, block):
-    return [
-        (3 * block * s + 128 * i, block * s + 128 * i) for s in range(n_t) for i in range(block // 128)
-    ]
-
-
 def attend_kernel(n_t, block, count, factor, x, live, norms, qkv, proj, c_out, hidden_out, mixed_out, context_out):
     xf = x[0].astype(F32)
     unit, _ = standardise(xf)
@@ -1053,139 +1145,6 @@
             flops=2 * batches * rows * d * (wide + d), transcendentals=0, bytes_accessed=8 * batches * rows * d
         ),
     )(x, live, norms, qkv, proj)
-
-
-def retreat_kernel(
-    n_t,
-    block,
-    count,
-    factor,
-    experts,
-    x,
-    hidden_in,
-    mixed,
-    context,
-    mix,
-    d_rows,
-    dgate,
-    dy,
-    live,
-    expert_own,
-    norms,
-    qkv,
-    proj,
-    router,
-    out,
-    grad_x,
-    gqkv_out,
-    gproj_out,
-    grouter,
-    gnorms,
-    dmixed,
-    gqkv,
-    gproj,
-):
-    step = pl.program_id(0)
-
-    @pl.when(step == 0)
-    def _():
-        gqkv[...] = jnp.zeros_like(gqkv)
-        gproj[...] = jnp.zeros_like(gproj)
-        grouter[...] = jnp.zeros_like(grouter)
-        gnorms[...] = jnp.zeros_like(gnorms)
-
-    hidden = hidden_in[0]
-    out[0] = (hidden + mix[0]).astype(BF16)
-    unit, inverse = standardise(hidden)
-    c = (unit * norms[2:3] + norms[3:4]).astype(BF16)
-    probs, lane = gate_softmax(c, router[...], experts)
-    dprobs = jnp.where(lane == expert_own[0, :, 0:1], dgate[0, :, 0:1], 0.0)
-    dprobs = dprobs + jnp.where(lane == expert_own[0, :, 1:2], dgate[0, :, 1:2], 0.0)
-    dlogits = probs * (dprobs - jnp.sum(dprobs * probs, axis=-1, keepdims=True))
-    dc = d_rows[0]
-    for piece in two_parts(dlogits):
-        grouter[...] += dot(c, piece, ((0,), (0,)))
-        dc = dc + dot(piece, router[...], ((1,), (1,)))
-    gnorms[2:3] += jnp.sum(dc * unit, axis=0, keepdims=True)
-    gnorms[3:4] += jnp.sum(dc, axis=0, keepdims=True)
-    dhidden = dy[0].astype(F32) + norm_back(dc * norms[2:3], unit, inverse)
-    dattn = (live[0] * dhidden).astype(BF16)
-    gproj[...] += dot(context[0], dattn, ((0,), (0,)))
-    dcontext = dot(dattn, proj[...], ((1,), (1,))).astype(BF16)
-    low = lax.broadcasted_iota(jnp.int32, (x.shape[1], 128), 1) < 64
-    for col, dest in pairs(n_t, block):
-        query = mixed[0, :, col : col + 128]
-        keys = mixed[0, :, col + block : col + block + 128]
-        values = mixed[0, :, col + 2 * block : col + 2 * block + 128]
-        grads = dcontext[:, dest : dest + 128]
-        zero = jnp.zeros_like(query)
-        parts = []
-        for own in (low, ~low):
-            probs = key_softmax(jnp.where(own, query, zero), keys, count)
-            dvalues = dot(probs.astype(BF16), grads, ((0,), (0,)))
-            dweights = dot(jnp.where(own, grads, zero), values, ((1,), (1,)))
-            dscores = probs * (dweights - jnp.sum(dweights * probs, axis=-1, keepdims=True))
-            dscores = dscores.astype(BF16)
-            parts.append(
-                (dot(dscores, keys, ((1,), (0,))), dot(dscores, query, ((0,), (0,))), dvalues)
-            )
-        for i in range(3):
-            both = jnp.where(low, parts[0][i], parts[1][i]).astype(BF16)
-            if i == 0:
-                both = both * BF16(factor)
-            dmixed[:, col + i * block : col + i * block + 128] = both
-    xf = x[0].astype(F32)
-    unit, inverse = standardise(xf)
-    a = (unit * norms[0:1] + norms[1:2]).astype(BF16)
-    gqkv[...] += dot(a, dmixed[...], ((0,), (0,)))
-    da = dot(dmixed[...], qkv[...], ((1,), (1,)))
-    gnorms[0:1] += jnp.sum(da * unit, axis=0, keepdims=True)
-    gnorms[1:2] += jnp.sum(da, axis=0, keepdims=True)
-    grad_x[0] = dhidden + norm_back(da * norms[0:1], unit, inverse)
-
-    @pl.when(step == pl.num_programs(0) - 1)
-    def _():
-        gqkv_out[...] = gqkv[...].astype(BF16)
-        gproj_out[...] = gproj[...].astype(BF16)
-
-
-def retreat(x, saved, arrived, dy, live, expert_own, norms, qkv, proj, router, n_t, block, count, factor, experts):
-    batches, rows, d = x.shape
-    wide = qkv.shape[1]
-
-    def each(n):
-        return pl.BlockSpec((1, rows, n), lambda m: (m, 0, 0))
-
-    def fixed(v):
-        return pl.BlockSpec(v.shape, lambda m: (0, 0))
-
-    whole = [
-        jax.ShapeDtypeStruct((d, wide), BF16),
-        jax.ShapeDtypeStruct((d, d), BF16),
-        jax.ShapeDtypeStruct((d, router.shape[1]), F32),
-        jax.ShapeDtypeStruct((8, d), F32),
-    ]
-    return pl.pallas_call(
-        functools.partial(retreat_kernel, n_t, block, count, factor, experts),
-        grid=(batches,),
-        in_specs=[each(d), each(d), each(wide), each(d), each(d), each(d), each(128), each(d), each(1), each(2)]
-        + [fixed(v) for v in (norms, qkv, proj, router)],
-        out_specs=[each(d), each(d)] + [fixed(v) for v in whole],
-        out_shape=[
-            jax.ShapeDtypeStruct((batches, rows, d), BF16),
-            jax.ShapeDtypeStruct((batches, rows, d), F32),
-        ]
-        + whole,
-        scratch_shapes=[
-            pltpu.VMEM((rows, wide), BF16),
-            pltpu.VMEM((d, wide), F32),
-            pltpu.VMEM((d, d), F32),
-        ],
-        compiler_params=pltpu.CompilerParams(vmem_limit_bytes=48 * 1024 * 1024),
-        cost_estimate=pl.CostEstimate(
-            flops=6 * batches * rows * d * (wide + d), transcendentals=0, bytes_accessed=16 * batches * rows * d
-        ),
-    )(x, *saved, *arrived, dy, live, expert_own, norms, qkv, proj, router)
 
 
 def fast(
@@ -1270,25 +1229,22 @@
     live_own = own(lay(live.astype(F32)[:, :, None], 1), 1)
 
     c, hidden, mixed, context = attend(x, live_own, norms, qkv, proj, n_t, block, SEQ, factor)
-    mixture, d_rows, dgates, grad_in, grad_out = moe(
-        c, cot_all, router, flat, expert_of, codes, w_in[0], w_out[0], experts, n_dp
-    )
-    output, grad_x, grad_qkv, grad_proj, grad_router, grad_norms = retreat(
-        x,
-        (hidden, mixed, context),
-        (mixture, d_rows, dgates),
-        own(cot_all, 1),
-        live_own,
-        own(expert_of, 2).transpose(0, 2, 1),
-        norms,
-        qkv,
-        proj,
+    output, grad_x, grad_qkv, grad_proj, grad_router, grad_norms, grad_in, grad_out = moe(
+        c,
+        cot_all,
         router,
+        flat,
+        expert_of,
+        codes,
+        w_in[0],
+        w_out[0],
+        (x, hidden, mixed, context, live_own, norms, qkv, proj),
+        experts,
+        n_dp,
         n_t,
         block,
         SEQ,
         factor,
-        experts,
     )
 
     out_edge = lax.ppermute(output[:, :edge], "tensor", [(1, 0)])

time: 377 us -> 350 us (0.928)
  Pallas kernels: 317 us -> 294 us
  local copies, waits for them, and re-layouts: 43.3 us -> 38.9 us
    pallas_call x2 -> x1, Pallas kernels: 207 us -> 184 us  [moe(): pl.pallas_call(functools.partial(moe_kernel, experts, n_t, block, count,...]
    unnamed x77 -> x78, local copies, waits for them, and re-layouts: 14.2 us -> 10.3 us
  transfers between devices with their start and end apart: 2 -> 2, of which waited for: 0 -> 0; matrix products, arithmetic and copies ran while one was open for 5% -> 5% of each run, Pallas kernels for 15% -> 17%
where the time goes in v5:
time: 350 us; the launch traced here: 349 us
  Pallas kernels  294 us (84%)
  local copies, waits for them, and re-layouts  38.9 us (11%)
  other arithmetic  11.5 us (3%)
    pallas_call x1, Pallas kernels, moe(): pl.pallas_call(functools.partial(moe_kernel, experts, n_t, block, count,...  184 us
    pallas_call x1, Pallas kernels, scatter_grads(): pl.pallas_call(functools.partial(scatter_kernel, ny, nz, n_t), out_shape=...  58.2 us
    pallas_call x1, Pallas kernels, gather_weights(): pl.pallas_call(functools.partial(gather_kernel, ny, nz, n_t, len(side)),...  45.9 us
    unnamed x78, local copies, waits for them, and re-layouts  10.3 us
  transfers between devices with their start and end apart: 2, of which 0 were waited for; matrix products, arithmetic and copies ran while one was open for 5% of the time, Pallas kernels for 17%

profile of v5, /device:TPU:0, one launch (start us, length us, event | category | flops | bytes accessed | tf_op | source)
XLA Modules:
  0.0 349.3 jit_solution(7896431534825556284)
XLA Ops:
  0.7 1.7 slice.70.refs_4_
  8.7 45.9 %shard_map.221 = (bf16[4,2,2,32,1536]{4,3,2,1,0:T(8,128)(2,1)}, bf16[4,2,2,2,16,512]{5,4,3,2,1,0:T(8,128)(2,1)}, bf16[4,2,2,2,16,128]{5,4,3,2,1,0:T(8,128)(2,1)}...) custom-call(bf16[32,768]{1,0:T(8,128)(2,1)} %reshape.145.refs_0_, bf16[16,512]{1,0:T(8,128)(2,1)} %reshape.146.refs_1_, ...), custom_call_target="tpu_custom_call" | custom-call | tf_op jit(solution)/shard_map/pallas_call | solution.py:228
  54.7 1.2 maximum_select_fusion.2
  60.9 1.5 copy.51
  62.5 1.2 reshape.152
  63.8 2.6 pad.39
  66.4 6.4 %shard_map.222 = (bf16[3,208,512]{2,1,0:T(8,128)(2,1)S(1)}, f32[3,208,512]{2,1,0:T(8,128)S(1)}, bf16[3,208,1536]{2,1,0:T(8,128)(2,1)S(1)}, bf16[3,208,512]{2,1,0:T(8,128)(2,1)S(1)}) custom-call(bf16[3,208,512]{2,1,0:T(8,128)(2,1)S(1)} %pad.35.x.x_in, f32[3,208,1]{2,1,0:T(8,128)S(1)} %constant_dynamic-slice_fusion.live, f32[8,512]{1,0:T(8,128)S(1)} %pad_convert_fusion.norms, ...), custom_call_target="tpu_custom_call" | custom-call | flops 1308622848 | bytes 2555904 | tf_op jit(solution)/shard_map/pallas_call | solution.py:1132
  72.9 1.2 copy-done.2
  74.1 1.0 copy-done.5
  76.8 184.1 %shard_map.223 = (bf16[3,208,512]{2,1,0:T(8,128)(2,1)}, f32[3,208,512]{2,1,0:T(8,128)}, bf16[512,1536]{1,0:T(8,128)(2,1)}, bf16[512,512]{1,0:T(8,128)(2,1)}, f32...) custom-call(bf16[3,208,512]{2,1,0:T(8,128)(2,1)} %copy-done.6, ...), custom_call_target="tpu_custom_call" | custom-call | tf_op jit(solution)/shard_map/pallas_call | solution.py:773
  260.9 1.9 slice.83
  262.8 1.3 collective-permute-start.1
  264.1 1.6 slice.79
  265.8 1.3 collective-permute-start
  267.0 2.0 slice_convert_fusion
  275.0 58.2 %shard_map.224 = (f32[32,768]{1,0:T(8,128)}, f32[16,512]{1,0:T(8,128)}, f32[16,128]{1,0:T(8,128)}) custom-call(bf16[4,2,2,32,1536]{4,3,2,1,0:T(8,128)(2,1)} %bitcast.88, bf16[4,2,2,2,16,512]{5,4,3,2,1,0:T(8,128)(2,1)} %reshape.160.refs_1_, f32[4,2,2,2,16,128]{5,4,3,2,1,0:T(8,128)} %bitcast.92), custom_call_target="tpu_custom_call" | custom-call | tf_op jit(solution)/shard_map/pallas_call | solution.py:347
  335.0 1.2 reshape.163
  336.9 1.4 reshape.164
  338.3 1.6 slice_reduce_fusion.1
  339.9 2.4 maximum_select_fusion.1
  342.4 2.7 maximum_select_fusion
  345.1 1.3 copy.76
  346.4 1.0 copy-done.15
  347.4 1.3 copy.77
  (132 shorter events, 22.1 us)
Async XLA Ops:
  0.6 5.4 %copy-start.23 = (bf16[32,4,192]{2,1,0:T(4,128)(2,1)S(1)}, bf16[32,4,192]{2,1,0:T(4,128)(2,1)}, u32[]{:S(2)}) copy-start(bf16[32,4,192]{2,1,0:T(4,128)(2,1)} %param.15) | copy-start | bytes 147460
  0.7 6.4 %copy-start.31 = (bf16[16]{0:T(256)(128)(2,1)S(1)}, bf16[16]{0:T(256)(128)(2,1)}, u32[]{:S(2)}) copy-start(bf16[16]{0:T(256)(128)(2,1)} %param.20) | copy-start | bytes 100
  0.7 6.4 %copy-start.32 = (bf16[16]{0:T(256)(128)(2,1)S(1)}, bf16[16]{0:T(256)(128)(2,1)}, u32[]{:S(2)}) copy-start(bf16[16]{0:T(256)(128)(2,1)} %param.21) | copy-start | bytes 100
  0.7 6.5 %copy-start.33 = (bf16[16]{0:T(256)(128)(2,1)S(1)}, bf16[16]{0:T(256)(128)(2,1)}, u32[]{:S(2)}) copy-start(bf16[16]{0:T(256)(128)(2,1)} %param.22) | copy-start | bytes 100
  0.7 6.6 %copy-start.34 = (bf16[16]{0:T(256)(128)(2,1)S(1)}, bf16[16]{0:T(256)(128)(2,1)}, u32[]{:S(2)}) copy-start(bf16[16]{0:T(256)(128)(2,1)} %param.23) | copy-start | bytes 100
  0.7 6.7 %copy-start.25 = (bf16[4,4,512]{2,1,0:T(4,128)(2,1)S(1)}, bf16[4,4,512]{2,1,0:T(4,128)(2,1)}, u32[]{:S(2)}) copy-start(bf16[4,4,512]{2,1,0:T(4,128)(2,1)} %param.16) | copy-start | bytes 49156
  0.7 7.3 %copy-start.28 = (bf16[16,16]{1,0:T(8,128)(2,1)S(1)}, bf16[16,16]{1,0:T(8,128)(2,1)}, u32[]{:S(2)}) copy-start(bf16[16,16]{1,0:T(8,128)(2,1)} %param.19) | copy-start | bytes 1540
  2.4 52.2 %copy-start.11 = (bf16[3,256,512]{2,1,0:T(8,128)(2,1)S(1)}, bf16[3,256,512]{2,1,0:T(8,128)(2,1)}, u32[]{:S(2)}) copy-start(bf16[3,256,512]{2,1,0:T(8,128)(2,1)} %param.14) | copy-start | bytes 2359300
  2.4 52.2 %slice-start = ((bf16[3,256,512]{2,1,0:T(8,128)(2,1)}), bf16[3,138,512]{2,1,0:T(8,128)(2,1)S(1)}, s32[]{:S(2)}) async-start(bf16[3,256,512]{2,1,0:T(8,128)(2,1)} %param.14), calls=%async_computation | async-start | bytes 884736 | tf_op jit(solution)/shard_map/slice | solution.py:1210
  3.9 56.3 %copy-start.29 = (pred[128]{0:T(512)(128)(4,1)}, pred[128]{0:T(512)(128)(4,1)S(1)}, u32[]{:S(2)}) copy-start(pred[128]{0:T(512)(128)(4,1)S(1)} %iota_compare_fusion.1) | copy-start | bytes 388
  55.9 10.5 %copy-start = (bf16[3,208,512]{2,1,0:T(8,128)(2,1)}, bf16[3,208,512]{2,1,0:T(8,128)(2,1)S(1)}, u32[]{:S(2)}) copy-start(bf16[3,208,512]{2,1,0:T(8,128)(2,1)S(1)} %pad.35.x.x_in) | copy-start | bytes 1916932
  56.2 10.3 %copy-start.8 = (f32[8,512]{1,0:T(8,128)}, f32[8,512]{1,0:T(8,128)S(1)}, u32[]{:S(2)}) copy-start(f32[8,512]{1,0:T(8,128)S(1)} %pad_convert_fusion.norms) | copy-start | bytes 49156
  56.9 9.5 %copy-start.1 = (bf16[512,512]{1,0:T(8,128)(2,1)}, bf16[512,512]{1,0:T(8,128)(2,1)S(1)}, u32[]{:S(2)}) copy-start(bf16[512,512]{1,0:T(8,128)(2,1)S(1)} %reshape.150.proj) | copy-start | bytes 1572868
  58.1 4.3 %copy-start.9 = (s32[3,2,2,208]{1,3,2,0:T(8,128)}, s32[3,2,2,208]{1,3,2,0:T(8,128)S(1)}, u32[]{:S(2)}) copy-start(s32[3,2,2,208]{1,3,2,0:T(8,128)S(1)} %pad.40) | copy-start | bytes 29956
  66.4 6.4 %copy-start.4 = (f32[3,208,1]{2,1,0:T(8,128)}, f32[3,208,1]{2,1,0:T(8,128)S(1)}, u32[]{:S(2)}) copy-start(f32[3,208,1]{2,1,0:T(8,128)S(1)} %constant_dynamic-slice_fusion.live) | copy-start | bytes 7492
  260.9 8.1 %copy-start.27 = (f32[8,512]{1,0:T(8,128)S(1)}, f32[8,512]{1,0:T(8,128)}, u32[]{:S(2)}) copy-start(f32[8,512]{1,0:T(8,128)} %get-tuple-element.45) | copy-start | bytes 49156
  260.9 8.3 %copy-start.21 = (f32[512,128]{1,0:T(8,128)S(1)}, f32[512,128]{1,0:T(8,128)}, u32[]{:S(2)}) copy-start(f32[512,128]{1,0:T(8,128)} %get-tuple-element.44) | copy-start | bytes 786436
  260.9 8.3 %copy-start.30 = (pred[128]{0:T(512)(128)(4,1)S(1)}, pred[128]{0:T(512)(128)(4,1)}, u32[]{:S(2)}) copy-start(pred[128]{0:T(512)(128)(4,1)} %copy-done.29) | copy-start | bytes 388
  260.9 9.1 %copy-start.10 = (f32[3,208,512]{2,1,0:T(8,128)S(1)}, f32[3,208,512]{2,1,0:T(8,128)}, u32[]{:S(2)}) copy-start(f32[3,208,512]{2,1,0:T(8,128)} %get-tuple-element.41) | copy-start | bytes 3833860
  262.8 79.5 %collective-permute-start.1 = (f32[3,59,512]{2,1,0:T(8,128)}, f32[3,59,512]{2,1,0:T(8,128)}, u32[]{:S(2)}, u32[]{:S(2)}) collective-permute-start(f32[3,59,512]{2,1,0:T(8,128)} %slice.83), channel_id=1, source_target_pairs={{1,0},{3,2},{5,4},{7,6},{9,8},{11,10},{13,12},{15,14},{17,16},{19,... | collective-permute-start | bytes 1087496 | tf_op jit(solution)/shard_map/ppermute | solution.py:1251
  265.8 74.2 %collective-permute-start = (bf16[3,59,512]{2,1,0:T(8,128)(2,1)}, bf16[3,59,512]{2,1,0:T(8,128)(2,1)}, u32[]{:S(2)}, u32[]{:S(2)}) collective-permute-start(bf16[3,59,512]{2,1,0:T(8,128)(2,1)} %slice.79), channel_id=1, source_target_pairs={{1,0},{3,2},{5,4},{7,6},{9,8},{11,10},{13,12},{15,14},{17,16},{19,... | collective-permute-start | bytes 543752 | tf_op jit(solution)/shard_map/ppermute | solution.py:1250
  270.2 2.7 copy-start.12
  275.0 64.9 %copy-start.17 = (bf16[3,138,512]{2,1,0:T(8,128)(2,1)S(1)}, bf16[3,138,512]{2,1,0:T(8,128)(2,1)}, u32[]{:S(2)}) copy-start(bf16[3,138,512]{2,1,0:T(8,128)(2,1)} %slice.80) | copy-start | bytes 1271812
  335.0 7.4 %copy-start.13 = (f32[3,118,512]{2,1,0:T(8,128)S(1)}, f32[3,118,512]{2,1,0:T(8,128)}, u32[]{:S(2)}) copy-start(f32[3,118,512]{2,1,0:T(8,128)} %slice_convert_fusion) | copy-start | bytes 2174980
  (14 other events, 21.0 us)

commit v6 on v5

--- a/solution.py
+++ b/solution.py
@@ -145,86 +145,77 @@
     dp, t, c, y, z = position(ny)
     stages = neighbours(ny, nz, n_t)
     greet(stages)
-    aside = []
-    for i in range(extras):
-        aside.append(
-            pltpu.make_async_remote_copy(
-                src_ref=side[i],
-                dst_ref=side_out[i].at[t] if i == 0 else side_out[i],
-                send_sem=send.at[send.shape[0] - 1 - i],
-                recv_sem=recv.at[recv.shape[0] - 1 - i],
-                device_id=(dp, 1 - t),
-                device_id_type=MESH,
+    cols, wide = qkv.shape[1], proj.shape[1]
+    whole = slice(None)
+    slot = 0
+
+    def start(pieces, device):
+        nonlocal slot
+        copies = []
+        for src, dst in pieces:
+            copies.append(
+                pltpu.make_async_remote_copy(
+                    src_ref=src,
+                    dst_ref=dst,
+                    send_sem=send.at[slot],
+                    recv_sem=recv.at[slot],
+                    device_id=device,
+                    device_id_type=MESH,
+                )
             )
-        )
-    for copy in aside:
-        copy.start()
-    cols = qkv.shape[1]
-
-    def views(zs, ys, cs, ts):
-        lanes = pl.ds(pl.multiple_of(ts * cols, 128), cols)
-        return (
-            qkv_out.at[zs, ys, cs, :, lanes],
-            proj_out.at[zs, ys, cs, ts],
-            small_out.at[zs, ys, cs, ts],
-        )
-
-    whole = slice(None)
-    mine = views(z, y, c, t)
-    local = [
-        pltpu.make_async_copy(src, dst, copied.at[i])
-        for i, (src, dst) in enumerate(zip((qkv, proj, small), mine))
-    ]
-    if extras:
-        local.append(pltpu.make_async_copy(side[0], side_out[0].at[t], copied.at[3]))
+            copies[-1].start()
+            slot += 1
+        return copies
+
+    def along(name, pieces):
+        size, device = stages[name]
+        return [copy for k in range(1, size) for copy in start(pieces, device(k))]
+
+    def lanes(ts, half):
+        return pl.ds(pl.multiple_of(ts * cols + half * (cols // 2), 128), cols // 2)
+
+    def views(zs, ys, ts, half):
+        band = slice(half * (wide // 2), (half + 1) * (wide // 2))
+        parts = [qkv_out.at[zs, ys, c, :, lanes(i, half)] for i in ts]
+        if len(ts) == 1:
+            parts.append(proj_out.at[zs, ys, c, ts[0], :, band])
+            if half == 0:
+                parts.append(small_out.at[zs, ys, c, ts[0]])
+        else:
+            parts.append(proj_out.at[zs, ys, c, :, :, band])
+        return [(part, part) for part in parts]
+
+    aside = start([(side[i], side_out[i]) for i in range(extras)], (dp, 1 - t)) if extras else []
+    mine = (
+        qkv_out.at[z, y, c, :, pl.ds(pl.multiple_of(t * cols, 128), cols)],
+        proj_out.at[z, y, c, t],
+        small_out.at[z, y, c, t],
+    )
+    inputs = list(zip((qkv, proj, small), mine))
+    local = [pltpu.make_async_copy(src, dst, copied.at[i]) for i, (src, dst) in enumerate(inputs)]
     for copy in local:
         copy.start()
-    slot = 0
-    for name in ("z", "y", "tensor", "core"):
-        size, device = stages[name]
-        if name == "z":
-            sources, targets = (qkv, proj, small), mine
-        elif name == "y":
-            sources = targets = views(whole, y, c, t)
-        elif name == "tensor":
-            sources = targets = views(whole, whole, c, t)
-        else:
-            sources = targets = (
-                qkv_out.at[:, :, c],
-                proj_out.at[:, :, c],
-                small_out.at[:, :, c],
-            )
-        copies = []
-        for k in range(1, size):
-            for src, dst in zip(sources, targets):
-                copies.append(
-                    pltpu.make_async_remote_copy(
-                        src_ref=src,
-                        dst_ref=dst,
-                        send_sem=send.at[slot],
-                        recv_sem=recv.at[slot],
-                        device_id=device(k),
-                        device_id_type=MESH,
-                    )
-                )
-                slot += 1
-        for copy in copies:
-            copy.start()
-        if name == "z":
-            for copy in local:
-                copy.wait()
-        for copy in copies:
-            copy.wait()
-    for copy in aside:
+    for copy in along("z", inputs) + local:
+        copy.wait()
+    one = along("y", views(whole, y, [t], 0))
+    two = along("tensor", views(whole, y, [t], 1))
+    for copy in one:
+        copy.wait()
+    one = along("tensor", views(whole, whole, [t], 0))
+    for copy in two:
+        copy.wait()
+    two = along("y", views(whole, y, list(range(n_t)), 1))
+    for copy in one + two:
+        copy.wait()
+    rest = [ref.at[:, :, c] for ref in (qkv_out, proj_out, small_out)]
+    for copy in along("core", [(part, part) for part in rest]) + aside:
         copy.wait()
 
 
 def gather_weights(qkv, proj, small, n_dp, n_t, side=()):
     nz, ny = grid_sizes(n_dp)
-    slots = 3 * (1 + (n_t - 1) + (ny - 1) + (nz - 1)) + len(side)
-    side_shapes = [
-        jax.ShapeDtypeStruct(((n_t,) if i == 0 else ()) + v.shape, v.dtype) for i, v in enumerate(side)
-    ]
+    slots = 3 * (nz - 1) + 5 * (n_t - 1) + (4 + n_t) * (ny - 1) + 3 + len(side)
+    side_shapes = [jax.ShapeDtypeStruct(v.shape, v.dtype) for v in side]
     outs = pl.pallas_call(
         functools.partial(gather_kernel, ny, nz, n_t, len(side)),
         out_shape=[
@@ -238,7 +229,7 @@
         scratch_shapes=[
             pltpu.SemaphoreType.DMA((slots,)),
             pltpu.SemaphoreType.DMA((slots,)),
-            pltpu.SemaphoreType.DMA((4,)),
+            pltpu.SemaphoreType.DMA((3,)),
         ],
         compiler_params=pltpu.CompilerParams(collective_id=0, has_side_effects=True),
     )(qkv, proj, small, *side)
@@ -249,84 +240,129 @@
 def scatter_kernel(ny, nz, n_t, *refs):
     ins, refs = refs[:3], refs[3:]
     outs, refs = refs[:3], refs[3:]
-    got = [refs[3 * i : 3 * i + 3] for i in range(4)]
-    held = [refs[12 + 3 * i : 15 + 3 * i] for i in range(3)]
-    send, recv = refs[21], refs[22]
+    got_core, refs = refs[:3], refs[3:]
+    held, refs = refs[:3], refs[3:]
+    one_got, one_held, one_last, refs = refs[:3], refs[3:6], refs[6:9], refs[9:]
+    two_got, two_held, two_last, refs = refs[:2], refs[2:4], refs[4:6], refs[6:]
+    end, end_got, (send, recv) = refs[:3], refs[3:6], refs[6:]
     _, t, c, y, z = position(ny)
     stages = neighbours(ny, nz, n_t)
     greet(stages)
-    cols = outs[0].shape[1]
+    cols, wide = outs[0].shape[1], outs[1].shape[1]
     slot = 0
 
-    def lanes(ts):
-        return pl.ds(pl.multiple_of(ts * cols, 128), cols)
-
-    def exchange(name, me, piece):
+    def lanes(ts, half):
+        return pl.ds(pl.multiple_of(ts * cols + half * (cols // 2), 128), cols // 2)
+
+    def band(half):
+        return slice(half * (wide // 2), (half + 1) * (wide // 2))
+
+    def along(name, me, pieces):
         nonlocal slot
         size, device = stages[name]
-        level = ("core", "tensor", "y", "z").index(name)
         copies = []
         for k in range(1, size):
-            for i, src in enumerate(piece((me + k) % size)):
+            for src, dst in pieces((me + k) % size, k - 1):
                 copies.append(
                     pltpu.make_async_remote_copy(
                         src_ref=src,
-                        dst_ref=got[level][i].at[k - 1],
+                        dst_ref=dst,
                         send_sem=send.at[slot],
                         recv_sem=recv.at[slot],
                         device_id=device(k),
                         device_id_type=MESH,
                     )
                 )
+                copies[-1].start()
                 slot += 1
-        for copy in copies:
-            copy.start()
+        return copies
+
+    def finish(copies):
         for copy in copies:
             copy.wait()
 
-    def total(own, level, index, i):
+    def total(own, got, index):
         value = own.astype(F32)
-        for k in range(got[level][i].shape[0]):
-            value = value + got[level][i][(k,) + index].astype(F32)
+        for k in range(got.shape[0]):
+            value = value + got[(k,) + index].astype(F32)
         return value
 
-    def over_zy(body):
+    def loop(count, body):
         def step(n, carry):
-            body(n // ny, n % ny)
+            body(n)
             return carry
 
-        lax.fori_loop(0, nz * ny, step, 0)
-
-    exchange("core", c, lambda j: [ref.at[:, :, j] for ref in ins])
-
-    def add_core(zi, yi):
+        lax.fori_loop(0, count, step, 0)
+
+    finish(
+        along("core", c, lambda j, k: [(ins[i].at[:, :, j], got_core[i].at[k]) for i in range(3)])
+    )
+
+    def add_core(n):
+        zi, yi = n // ny, n % ny
         for i in range(3):
-            held[0][i][zi, yi] = total(ins[i][zi, yi, c], 0, (zi, yi), i).astype(held[0][i].dtype)
-
-    over_zy(add_core)
-    exchange(
+            held[i][zi, yi] = total(ins[i][zi, yi, c], got_core[i], (zi, yi)).astype(held[i].dtype)
+
+    loop(nz * ny, add_core)
+    one = along(
         "tensor",
         t,
-        lambda j: [held[0][0].at[:, :, :, lanes(j)], held[0][1].at[:, :, j], held[0][2].at[:, :, j]],
-    )
-
-    def add_tensor(zi, yi):
-        owns = (held[0][0][zi, yi, :, lanes(t)], held[0][1][zi, yi, t], held[0][2][zi, yi, t])
+        lambda j, k: [
+            (held[0].at[:, :, :, lanes(j, 0)], one_got[0].at[k]),
+            (held[1].at[:, :, j, :, band(0)], one_got[1].at[k]),
+            (held[2].at[:, :, j], one_got[2].at[k]),
+        ],
+    )
+    two = along(
+        "y",
+        y,
+        lambda j, k: [(held[0].at[:, j, :, lanes(i, 1)], two_got[0].at[k, i]) for i in range(n_t)]
+        + [(held[1].at[:, j, i, :, band(1)], two_got[1].at[k, i]) for i in range(n_t)],
+    )
+    finish(one)
+
+    def add_one(n):
+        zi, yi = n // ny, n % ny
+        owns = (held[0][zi, yi, :, lanes(t, 0)], held[1][zi, yi, t, :, band(0)], held[2][zi, yi, t])
         for i in range(3):
-            held[1][i][zi, yi] = total(owns[i], 1, (zi, yi), i).astype(held[1][i].dtype)
-
-    over_zy(add_tensor)
-    exchange("y", y, lambda j: [ref.at[:, j] for ref in held[1]])
-
-    def add_y(zi, carry):
+            one_held[i][zi, yi] = total(owns[i], one_got[i], (zi, yi)).astype(one_held[i].dtype)
+
+    loop(nz * ny, add_one)
+    one = along("y", y, lambda j, k: [(one_held[i].at[:, j], one_last[i].at[k]) for i in range(3)])
+    finish(two)
+
+    def add_two(zi):
+        for i in range(n_t):
+            owns = (held[0][zi, y, :, lanes(i, 1)], held[1][zi, y, i, :, band(1)])
+            for j in range(2):
+                two_held[j][i, zi] = total(owns[j], two_got[j], (i, zi)).astype(two_held[j].dtype)
+
+    loop(nz, add_two)
+    two = along("tensor", t, lambda j, k: [(two_held[i].at[j], two_last[i].at[k]) for i in range(2)])
+    finish(one)
+    halves = [
+        (slice(0, cols // 2), slice(cols // 2, cols)),
+        (band(0), band(1)),
+        (slice(None),),
+    ]
+
+    def end_one(zi):
         for i in range(3):
-            held[2][i][zi] = total(held[1][i][zi, y], 2, (zi,), i).astype(held[2][i].dtype)
-        return carry
-
-    lax.fori_loop(0, nz, add_y, 0)
-    exchange("z", z, lambda j: [ref.at[j] for ref in held[2]])
+            value = total(one_held[i][zi, y], one_last[i], (zi,))
+            end[i][zi, :, halves[i][0]] = value.astype(end[i].dtype)
+
+    loop(nz, end_one)
+    finish(two)
+
+    def end_two(zi):
+        for i in range(2):
+            value = total(two_held[i][t, zi], two_last[i], (zi,))
+            end[i][zi, :, halves[i][1]] = value.astype(end[i].dtype)
+
+    loop(nz, end_two)
+    finish(along("z", z, lambda j, k: [(end[i].at[j], end_got[i].at[k]) for i in range(3)]))
     for i in range(3):
-        outs[i][...] = total(held[2][i][z], 3, (), i)
+        outs[i][...] = total(end[i][z], end_got[i], ())
 
 
 def scatter_grads(qkv, proj, small, n_dp, n_t):
@@ -334,15 +370,17 @@
     rows, cols = qkv.shape[3], qkv.shape[4] // n_t
     tails = [(rows, cols), proj.shape[4:], small.shape[4:]]
     kinds = [BF16, BF16, F32]
+    parts = [(rows, cols // 2), (proj.shape[4], proj.shape[5] // 2), small.shape[4:]]
     wide = [(rows, n_t * cols), (n_t,) + proj.shape[4:], (n_t,) + small.shape[4:]]
-    scratch = [pltpu.VMEM((1, nz, ny) + wide[i], kinds[i]) for i in range(3)]
-    scratch += [pltpu.VMEM((n_t - 1, nz, ny) + tails[i], kinds[i]) for i in range(3)]
-    scratch += [pltpu.VMEM((ny - 1, nz) + tails[i], kinds[i]) for i in range(3)]
-    scratch += [pltpu.VMEM((nz - 1,) + tails[i], kinds[i]) for i in range(3)]
-    scratch += [pltpu.VMEM((nz, ny) + wide[i], kinds[i]) for i in range(3)]
-    scratch += [pltpu.VMEM((nz, ny) + tails[i], kinds[i]) for i in range(3)]
-    scratch += [pltpu.VMEM((nz,) + tails[i], kinds[i]) for i in range(3)]
-    slots = 3 * (1 + (n_t - 1) + (ny - 1) + (nz - 1))
+
+    def room(lead, shapes):
+        return [pltpu.VMEM(lead + shape, kind) for shape, kind in zip(shapes, kinds)]
+
+    scratch = room((1, nz, ny), wide) + room((nz, ny), wide)
+    scratch += room((n_t - 1, nz, ny), parts) + room((nz, ny), parts) + room((ny - 1, nz), parts)
+    scratch += room((ny - 1, n_t, nz), parts[:2]) + room((n_t, nz), parts[:2]) + room((n_t - 1, nz), parts[:2])
+    scratch += room((nz,), tails) + room((nz - 1,), tails)
+    slots = 3 + 5 * (n_t - 1) + (3 + 2 * n_t) * (ny - 1) + 3 * (nz - 1)
     scratch += [pltpu.SemaphoreType.DMA((slots,)), pltpu.SemaphoreType.DMA((slots,))]
     return pl.pallas_call(
         functools.partial(scatter_kernel, ny, nz, n_t),
@@ -395,14 +433,13 @@
     ]
 
 
-def moe_kernel(
+def layer_kernel(
     experts,
     n_t,
     block,
     count,
     factor,
-    c_own,
-    cot_all,
+    cot_own,
     router,
     flat_row,
     flat_col,
@@ -412,9 +449,6 @@
     win,
     wout,
     x_in,
-    hidden_in,
-    mixed,
-    context,
     live,
     norms,
     qkv,
@@ -427,7 +461,12 @@
     gnorms,
     gin_mine,
     gout_mine,
+    c_own,
+    hidden_in,
+    mixed,
+    context,
     c_all,
+    cot_all,
     gates,
     sent,
     got,
@@ -452,6 +491,7 @@
     gout_got,
     w_sems,
     c_sems,
+    cot_sems,
     go_send,
     go_recv,
     back_send,
@@ -459,7 +499,7 @@
     pay_sems,
     grad_sems,
 ):
-    batches, rows, d = c_own.shape
+    batches, rows, d = cot_own.shape
     n_dp = lax.axis_size("dp")
     dp, t = lax.axis_index("dp"), lax.axis_index("tensor")
     share = sent.shape[1] // n_dp
@@ -499,6 +539,16 @@
             dst_ref=c_all.at[m, image(t)],
             send_sem=c_sems.at[0, m],
             recv_sem=c_sems.at[1, m],
+            device_id=partner,
+            device_id_type=MESH,
+        )
+
+    def cot_copy(m):
+        return pltpu.make_async_remote_copy(
+            src_ref=cot_own.at[m],
+            dst_ref=cot_all.at[m, image(t)],
+            send_sem=cot_sems.at[0, m],
+            recv_sem=cot_sems.at[1, m],
             device_id=partner,
             device_id_type=MESH,
         )
@@ -551,9 +601,39 @@
 
         lax.fori_loop(1, n_dp, step, 0)
 
-    for m in range(batches):
+    low = lax.broadcasted_iota(jnp.int32, (rows, 128), 1) < 64
+
+    def attend(m, carry):
+        cot_copy(m).start()
+        cot_all[m, image(t)] = cot_own[m]
+        xf = x_in[m].astype(F32)
+        unit, _ = standardise(xf)
+        a = (unit * norms[0:1] + norms[1:2]).astype(BF16)
+        for s in range(n_t):
+            for i in range(3):
+                cols = slice((3 * s + i) * block, (3 * s + i + 1) * block)
+                projected = dot(a, qkv[:, cols], ((1,), (0,)))
+                mixed[m, :, cols] = (projected * factor if i == 0 else projected).astype(BF16)
+        for col, dest in pairs(n_t, block):
+            query = mixed[m, :, col : col + 128]
+            keys = mixed[m, :, col + block : col + block + 128]
+            values = mixed[m, :, col + 2 * block : col + 2 * block + 128]
+            zero = jnp.zeros_like(query)
+            parts = []
+            for own in (low, ~low):
+                probs = key_softmax(jnp.where(own, query, zero), keys, count)
+                parts.append(dot(probs.astype(BF16), values, ((1,), (0,))))
+            context[m, :, dest : dest + 128] = jnp.where(low, parts[0], parts[1]).astype(BF16)
+        hidden = xf + live[m] * dot(context[m], proj[...], ((1,), (0,)))
+        hidden_in[m] = hidden
+        unit, _ = standardise(hidden)
+        c = (unit * norms[2:3] + norms[3:4]).astype(BF16)
+        c_own[m] = c
+        c_all[m, image(t)] = c
         c_copy(m).start()
-        c_all[m, image(t)] = c_own[m]
+        return carry
+
+    lax.fori_loop(0, batches, attend, 0)
     w_copy(0).start()
     w_copy(1).start()
 
@@ -561,6 +641,7 @@
 
     def dispatch(m, carry):
         c_copy(m).wait_recv()
+        cot_copy(m).wait_recv()
         c = c_all[m]
         logits = jnp.where(lane < experts, dot(c, router[...], ((1,), (0,))), -1e30)
         raised = jnp.exp(logits - jnp.max(logits, axis=-1, keepdims=True))
@@ -669,7 +750,6 @@
     gproj[...] = jnp.zeros_like(gproj)
     grouter[...] = jnp.zeros_like(grouter)
     gnorms[...] = jnp.zeros_like(gnorms)
-    low = lax.broadcasted_iota(jnp.int32, (rows, 128), 1) < 64
 
     def retreat(m):
         pay_copy(m).wait_recv()
@@ -756,6 +836,7 @@
 
     def drain(m, carry):
         c_copy(m).wait_send()
+        cot_copy(m).wait_send()
         pay_copy(m).wait_send()
         every(lambda k: go_copy(m, k).wait_send())
         every(lambda k: back_copy(m, k).wait_send())
@@ -764,14 +845,14 @@
     lax.fori_loop(0, batches, drain, 0)
 
 
-def moe(c_own, cot_all, router, flat, expert_of, codes, win, wout, saved, experts, n_dp, n_t, block, count, factor):
-    batches, rows, d = c_own.shape
+def layer(cot_own, router, flat, expert_of, codes, win, wout, saved, experts, n_dp, n_t, block, count, factor):
+    batches, rows, d = cot_own.shape
     slots = codes.shape[0]
     half = win.shape[1]
-    wide = saved[2].shape[2]
+    wide = 3 * n_t * block
     dma = pltpu.SemaphoreType.DMA
     return pl.pallas_call(
-        functools.partial(moe_kernel, experts, n_t, block, count, factor),
+        functools.partial(layer_kernel, experts, n_t, block, count, factor),
         out_shape=[
             jax.ShapeDtypeStruct((batches, rows, d), BF16),
             jax.ShapeDtypeStruct((batches, rows, d), F32),
@@ -782,9 +863,14 @@
             jax.ShapeDtypeStruct((d, half), F32),
             jax.ShapeDtypeStruct((half, d), F32),
         ],
-        in_specs=[ANYWHERE] * 18,
+        in_specs=[ANYWHERE] * 14,
         out_specs=[ANYWHERE] * 8,
         scratch_shapes=[
+            pltpu.VMEM((batches, rows, d), BF16),
+            pltpu.VMEM((batches, rows, d), F32),
+            pltpu.VMEM((batches, rows, wide), BF16),
+            pltpu.VMEM((batches, rows, d), BF16),
+            pltpu.VMEM((batches, 2 * rows, d), BF16),
             pltpu.VMEM((batches, 2 * rows, d), BF16),
             pltpu.VMEM((batches, 2 * rows, 128), F32),
             pltpu.VMEM((batches, slots, 2 * d), BF16),
@@ -810,6 +896,7 @@
             pltpu.VMEM((half, d), BF16),
             dma((2, 2)),
             dma((2, batches)),
+            dma((2, batches)),
             dma((batches, n_dp - 1)),
             dma((batches, n_dp - 1)),
             dma((batches, n_dp - 1)),
@@ -821,8 +908,7 @@
             collective_id=2, has_side_effects=True, vmem_limit_bytes=67043328
         ),
     )(
-        c_own,
-        cot_all,
+        cot_own,
         router,
         flat,
         flat.transpose(0, 2, 1),
@@ -1093,60 +1179,6 @@
     )
 
 
-def attend_kernel(n_t, block, count, factor, x, live, norms, qkv, proj, c_out, hidden_out, mixed_out, context_out):
-    xf = x[0].astype(F32)
-    unit, _ = standardise(xf)
-    a = (unit * norms[0:1] + norms[1:2]).astype(BF16)
-    for s in range(n_t):
-        for i in range(3):
-            cols = slice((3 * s + i) * block, (3 * s + i + 1) * block)
-            part = dot(a, qkv[:, cols], ((1,), (0,)))
-            mixed_out[0, :, cols] = (part * factor if i == 0 else part).astype(BF16)
-    low = lax.broadcasted_iota(jnp.int32, (x.shape[1], 128), 1) < 64
-    for col, dest in pairs(n_t, block):
-        query = mixed_out[0, :, col : col + 128]
-        keys = mixed_out[0, :, col + block : col + block + 128]
-        values = mixed_out[0, :, col + 2 * block : col + 2 * block + 128]
-        zero = jnp.zeros_like(query)
-        parts = []
-        for own in (low, ~low):
-            probs = key_softmax(jnp.where(own, query, zero), keys, count)
-            parts.append(dot(probs.astype(BF16), values, ((1,), (0,))))
-        context_out[0, :, dest : dest + 128] = jnp.where(low, parts[0], parts[1]).astype(BF16)
-    hidden = xf + live[0] * dot(context_out[0], proj[...], ((1,), (0,)))
-    hidden_out[0] = hidden
-    unit, _ = standardise(hidden)
-    c_out[0] = (unit * norms[2:3] + norms[3:4]).astype(BF16)
-
-
-def attend(x, live, norms, qkv, proj, n_t, block, count, factor):
-    batches, rows, d = x.shape
-    wide = qkv.shape[1]
-
-    def each(n):
-        return pl.BlockSpec((1, rows, n), lambda m: (m, 0, 0))
-
-    def fixed(shape):
-        return pl.BlockSpec(shape, lambda m: (0, 0))
-
-    return pl.pallas_call(
-        functools.partial(attend_kernel, n_t, block, count, factor),
-        grid=(batches,),
-        in_specs=[each(d), each(1), fixed(norms.shape), fixed(qkv.shape), fixed(proj.shape)],
-        out_specs=[each(d), each(d), each(wide), each(d)],
-        out_shape=[
-            jax.ShapeDtypeStruct((batches, rows, d), BF16),
-            jax.ShapeDtypeStruct((batches, rows, d), F32),
-            jax.ShapeDtypeStruct((batches, rows, wide), BF16),
-            jax.ShapeDtypeStruct((batches, rows, d), BF16),
-        ],
-        compiler_params=pltpu.CompilerParams(vmem_limit_bytes=32 * 1024 * 1024),
-        cost_estimate=pl.CostEstimate(
-            flops=2 * batches * rows * d * (wide + d), transcendentals=0, bytes_accessed=8 * batches * rows * d
-        ),
-    )(x, live, norms, qkv, proj)
-
-
 def fast(
     tokens,
     w_qkv,
@@ -1184,10 +1216,10 @@
     )
     small = jnp.pad(small, ((0, 0), (0, 128 - small.shape[1])))
     qkv_block = w_qkv.reshape(-1, heads_here, 3, width).transpose(0, 2, 1, 3).reshape(-1, 3 * block)
-    qkv, proj, small, cot_all, moved = gather_weights(
-        qkv_block, w_proj.reshape(-1, d), small, n_dp, n_t, (cotangent, tokens[:, SEQ:])
-    )
-    cot_all = cot_all.transpose(1, 0, 2, 3).reshape(batches, rows, d)
+    held = jnp.concatenate([tokens, cotangent], axis=0)
+    qkv, proj, small, moved = gather_weights(
+        qkv_block, w_proj.reshape(-1, d), small, n_dp, n_t, (held[:, SEQ:],)
+    )
     router = jnp.where(jnp.arange(128) < experts, small, 0)
     norms = jnp.pad(small[:, experts : experts + 4].astype(F32).T, ((0, 4), (0, 0)))
     proj = proj.reshape(n_dp, n_t, heads_here, w_proj.shape[1], d)
@@ -1207,9 +1239,9 @@
     def own(v, axis):
         return lax.dynamic_slice_in_dim(v, t * padded, padded, axis)
 
-    x = jnp.where(t == 0, tokens[:, :SEQ], jnp.concatenate([moved, tokens[:, : SEQ - edge]], axis=1))
-    x = pad_rows(x, 1)
-    cot_all = lay(cot_all[:, :span], 1)
+    laid = jnp.where(t == 0, held[:, :SEQ], jnp.concatenate([moved, held[:, : SEQ - edge]], axis=1))
+    laid = pad_rows(laid, 1)
+    x, cot_own = laid[:batches], laid[batches:]
 
     live = live_rows[:, :span]
     rank = priority[:, 0, :span]
@@ -1228,17 +1260,15 @@
     codes = (jnp.arange(experts)[:, None] * cap + t * share + jnp.arange(share)[None, :]).reshape(-1)
     live_own = own(lay(live.astype(F32)[:, :, None], 1), 1)
 
-    c, hidden, mixed, context = attend(x, live_own, norms, qkv, proj, n_t, block, SEQ, factor)
-    output, grad_x, grad_qkv, grad_proj, grad_router, grad_norms, grad_in, grad_out = moe(
-        c,
-        cot_all,
+    output, grad_x, grad_qkv, grad_proj, grad_router, grad_norms, grad_in, grad_out = layer(
+        cot_own,
         router,
         flat,
         expert_of,
         codes,
         w_in[0],
         w_out[0],
-        (x, hidden, mixed, context, live_own, norms, qkv, proj),
+        (x, live_own, norms, qkv, proj),
         experts,
         n_dp,
         n_t,

time: 350 us -> 309 us (0.88)
  Pallas kernels: 294 us -> 256 us
    pallas_call x1, Pallas kernels: 58.2 us -> 34.5 us  [scatter_grads(): pl.pallas_call(functools.partial(scatter_kernel, ny, nz, n_t), out_shape=...]
    pallas_call x1, Pallas kernels: 45.9 us -> 30.6 us  [gather_weights(): pl.pallas_call(functools.partial(gather_kernel, ny, nz, n_t, len(side)),...]
    unnamed x78 -> x57, local copies, waits for them, and re-layouts: 10.3 us -> 8.35 us
    pallas_call x2 -> x1, Pallas kernels: 190 us -> 191 us  [layer(): pl.pallas_call(functools.partial(layer_kernel, experts, n_t, block, count...]
  transfers between devices with their start and end apart: 2 -> 2, of which waited for: 0 -> 0; matrix products, arithmetic and copies ran while one was open for 5% -> 7% of each run, Pallas kernels for 17% -> 11%
where the time goes in v6:
time: 309 us
  Pallas kernels  256 us (83%)
  local copies, waits for them, and re-layouts  37.1 us (12%)
  other arithmetic  10.8 us (3%)
    pallas_call x1, Pallas kernels, layer(): pl.pallas_call(functools.partial(layer_kernel, experts, n_t, block, count...  191 us
    pallas_call x1, Pallas kernels, scatter_grads(): pl.pallas_call(functools.partial(scatter_kernel, ny, nz, n_t), out_shape=...  34.5 us
    pallas_call x1, Pallas kernels, gather_weights(): pl.pallas_call(functools.partial(gather_kernel, ny, nz, n_t, len(side)),...  30.6 us
    unnamed x57, local copies, waits for them, and re-layouts  8.35 us
  transfers between devices with their start and end apart: 2, of which 0 were waited for; matrix products, arithmetic and copies ran while one was open for 7% of the time, Pallas kernels for 11%

profile of v6, /device:TPU:0, one launch (start us, length us, event | category | flops | bytes accessed | tf_op | source)
XLA Modules:
  0.0 308.7 jit_solution(15894253269600087029)
XLA Ops:
  0.7 1.3 constant_dynamic-update-slice_fusion.1
  7.5 30.6 %shard_map.221 = (bf16[4,2,2,32,1536]{4,3,2,1,0:T(8,128)(2,1)}, bf16[4,2,2,2,16,512]{5,4,3,2,1,0:T(8,128)(2,1)}, bf16[4,2,2,2,16,128]{5,4,3,2,1,0:T(8,128)(2,1)}, bf16[6,59,512]{2,1,0:T(8,128)(2,1)}) custom-call(bf16[32,768]{1,0:T(8,128)(2,1)} %reshape.136.refs_0_, bf16[16,512]{1,0:T(8,128)(2,1)} %reshape.137.refs_1_, bf16[16,128]{1,0:T(8,128)(2,1)} %pad.30.refs_2_, ...), custom_call_target="tpu_custom_call" | custom-call | tf_op jit(solution)/shard_map/pallas_call | solution.py:219
  38.2 1.4 slice_select_fusion
  39.6 1.2 pad_slice_fusion
  48.1 191.3 %shard_map.222 = (bf16[3,208,512]{2,1,0:T(8,128)(2,1)}, f32[3,208,512]{2,1,0:T(8,128)}, bf16[512,1536]{1,0:T(8,128)(2,1)}, bf16[512,512]{1,0:T(8,128)(2,1)}, f32...) custom-call(bf16[3,208,512]{2,1,0:T(8,128)(2,1)} %get-tuple-element.57.cot_own, ...), custom_call_target="tpu_custom_call" | custom-call | tf_op jit(solution)/shard_map/pallas_call | solution.py:854
  239.4 1.9 slice.87
  241.3 1.3 collective-permute-start.1
  242.6 1.6 slice.83
  244.2 1.3 collective-permute-start
  245.5 2.0 slice_convert_fusion
  250.5 1.8 slice.85
  252.3 1.2 reshape.147
  253.5 1.1 copy.68
  254.6 2.0 reshape.148.refs_1_
  256.5 34.5 %shard_map.223 = (f32[32,768]{1,0:T(8,128)}, f32[16,512]{1,0:T(8,128)}, f32[16,128]{1,0:T(8,128)}) custom-call(bf16[4,2,2,32,1536]{4,3,2,1,0:T(8,128)(2,1)} %bitcast.80, bf16[4,2,2,2,16,512]{5,4,3,2,1,0:T(8,128)(2,1)} %reshape.148.refs_1_, f32[4,2,2,2,16,128]{5,4,3,2,1,0:T(8,128)} %bitcast.83), custom_call_target="tpu_custom_call" | custom-call | tf_op jit(solution)/shard_map/pallas_call | solution.py:385
  292.8 1.9 reshape.151
  294.7 1.6 copy.59
  296.3 1.4 reshape.152
  297.7 1.6 slice_reduce_fusion.1
  299.3 2.4 maximum_select_fusion.1
  301.7 2.7 maximum_select_fusion
  304.4 1.3 copy.76
  305.7 1.0 copy-done.4
  306.7 1.3 copy.77
  (106 shorter events, 18.1 us)
Async XLA Ops:
  0.6 1.4 copy-start.6
  2.1 2.8 copy-start.11
  2.9 2.9 copy-start.20
  2.9 3.0 copy-start.21
  2.9 3.1 copy-start.22
  2.9 3.2 %copy-start.23 = (bf16[16]{0:T(256)(128)(2,1)S(1)}, bf16[16]{0:T(256)(128)(2,1)}, u32[]{:S(2)}) copy-start(bf16[16]{0:T(256)(128)(2,1)} %param.23) | copy-start | bytes 100
  2.9 3.2 %copy-start.14 = (bf16[4,4,512]{2,1,0:T(4,128)(2,1)S(1)}, bf16[4,4,512]{2,1,0:T(4,128)(2,1)}, u32[]{:S(2)}) copy-start(bf16[4,4,512]{2,1,0:T(4,128)(2,1)} %param.16) | copy-start | bytes 49156
  3.0 3.9 %copy-start.17 = (bf16[16,16]{1,0:T(8,128)(2,1)S(1)}, bf16[16,16]{1,0:T(8,128)(2,1)}, u32[]{:S(2)}) copy-start(bf16[16,16]{1,0:T(8,128)(2,1)} %param.19) | copy-start | bytes 1540
  3.1 41.5 %copy-start.18 = (pred[128]{0:T(512)(128)(4,1)}, pred[128]{0:T(512)(128)(4,1)S(1)}, u32[]{:S(2)}) copy-start(pred[128]{0:T(512)(128)(4,1)S(1)} %iota_compare_fusion.1) | copy-start | bytes 388
  39.6 1.6 copy-start.12
  39.6 1.7 copy-start.15
  42.4 3.0 copy-start
  42.5 2.1 copy-start.8
  42.5 3.6 %copy-start.7 = (bf16[4,2,2,2,16,512]{5,4,3,2,1,0:T(8,128)(2,1)S(1)}, bf16[4,2,2,2,16,512]{5,4,3,2,1,0:T(8,128)(2,1)}, u32[]{:S(2)}) copy-start(bf16[4,2,2,2,16,512]{5,4,3,2,1,0:T(8,128)(2,1)} %get-tuple-element.29) | copy-start | bytes 1572868
  239.4 8.1 %copy-start.16 = (f32[8,512]{1,0:T(8,128)S(1)}, f32[8,512]{1,0:T(8,128)}, u32[]{:S(2)}) copy-start(f32[8,512]{1,0:T(8,128)} %get-tuple-element.35) | copy-start | bytes 49156
  239.4 8.3 %copy-start.9 = (f32[512,128]{1,0:T(8,128)S(1)}, f32[512,128]{1,0:T(8,128)}, u32[]{:S(2)}) copy-start(f32[512,128]{1,0:T(8,128)} %get-tuple-element.34) | copy-start | bytes 786436
  239.4 8.3 %copy-start.19 = (pred[128]{0:T(512)(128)(4,1)S(1)}, pred[128]{0:T(512)(128)(4,1)}, u32[]{:S(2)}) copy-start(pred[128]{0:T(512)(128)(4,1)} %copy-done.18) | copy-start | bytes 388
  239.4 9.1 %copy-start.1 = (f32[3,208,512]{2,1,0:T(8,128)S(1)}, f32[3,208,512]{2,1,0:T(8,128)}, u32[]{:S(2)}) copy-start(f32[3,208,512]{2,1,0:T(8,128)} %get-tuple-element.31) | copy-start | bytes 3833860
  241.3 60.4 %collective-permute-start.1 = (f32[3,59,512]{2,1,0:T(8,128)}, f32[3,59,512]{2,1,0:T(8,128)}, u32[]{:S(2)}, u32[]{:S(2)}) collective-permute-start(f32[3,59,512]{2,1,0:T(8,128)} %slice.87), channel_id=1, source_target_pairs={{1,0},{3,2},{5,4},{7,6},{9,8},{11,10},{13,12},{15,14},{17,16},{19,... | collective-permute-start | bytes 1087496 | tf_op jit(solution)/shard_map/ppermute | solution.py:1281
  244.2 55.1 %collective-permute-start = (bf16[3,59,512]{2,1,0:T(8,128)(2,1)}, bf16[3,59,512]{2,1,0:T(8,128)(2,1)}, u32[]{:S(2)}, u32[]{:S(2)}) collective-permute-start(bf16[3,59,512]{2,1,0:T(8,128)(2,1)} %slice.83), channel_id=1, source_target_pairs={{1,0},{3,2},{5,4},{7,6},{9,8},{11,10},{13,12},{15,14},{17,16},{19,... | collective-permute-start | bytes 543752 | tf_op jit(solution)/shard_map/ppermute | solution.py:1280
  292.8 8.9 %copy-start.2 = (f32[3,118,512]{2,1,0:T(8,128)S(1)}, f32[3,118,512]{2,1,0:T(8,128)}, u32[]{:S(2)}) copy-start(f32[3,118,512]{2,1,0:T(8,128)} %slice_convert_fusion) | copy-start | bytes 2174980
  301.7 2.7 copy-start.5
  304.4 2.3 copy-start.4
  306.7 1.3 copy-start.10
  (2 other events, 2.1 us)

commit v7 on v6

--- a/solution.py
+++ b/solution.py
@@ -185,7 +185,10 @@
             parts.append(proj_out.at[zs, ys, c, :, :, band])
         return [(part, part) for part in parts]
 
-    aside = start([(side[i], side_out[i]) for i in range(extras)], (dp, 1 - t)) if extras else []
+    aside = []
+    for i in range(extras):
+        strip = side_out[i].shape[1]
+        aside += start([(side[i].at[:, side[i].shape[1] - strip :], side_out[i])], (dp, 1 - t))
     mine = (
         qkv_out.at[z, y, c, :, pl.ds(pl.multiple_of(t * cols, 128), cols)],
         proj_out.at[z, y, c, t],
@@ -212,10 +215,10 @@
         copy.wait()
 
 
-def gather_weights(qkv, proj, small, n_dp, n_t, side=()):
+def gather_weights(qkv, proj, small, n_dp, n_t, side=(), strip=0):
     nz, ny = grid_sizes(n_dp)
     slots = 3 * (nz - 1) + 5 * (n_t - 1) + (4 + n_t) * (ny - 1) + 3 + len(side)
-    side_shapes = [jax.ShapeDtypeStruct(v.shape, v.dtype) for v in side]
+    side_shapes = [jax.ShapeDtypeStruct((v.shape[0], strip) + v.shape[2:], v.dtype) for v in side]
     outs = pl.pallas_call(
         functools.partial(gather_kernel, ny, nz, n_t, len(side)),
         out_shape=[
@@ -237,7 +240,7 @@
     return (qkv_all, outs[1].reshape((n_dp, n_t) + proj.shape), outs[2].reshape(-1, small.shape[1])) + tuple(outs[3:])
 
 
-def scatter_kernel(ny, nz, n_t, *refs):
+def scatter_kernel(ny, nz, n_t, heads, *refs):
     ins, refs = refs[:3], refs[3:]
     outs, refs = refs[:3], refs[3:]
     got_core, refs = refs[:3], refs[3:]
@@ -248,7 +251,7 @@
     _, t, c, y, z = position(ny)
     stages = neighbours(ny, nz, n_t)
     greet(stages)
-    cols, wide = outs[0].shape[1], outs[1].shape[1]
+    cols, wide = ins[0].shape[4] // n_t, ins[1].shape[5]
     slot = 0
 
     def lanes(ts, half):
@@ -361,11 +364,22 @@
 
     loop(nz, end_two)
     finish(along("z", z, lambda j, k: [(end[i].at[j], end_got[i].at[k]) for i in range(3)]))
-    for i in range(3):
-        outs[i][...] = total(end[i][z], end_got[i], ())
-
-
-def scatter_grads(qkv, proj, small, n_dp, n_t):
+    results = [total(end[i][z], end_got[i], ()) for i in range(3)]
+    outs[2][...] = results[2]
+    if heads == 0:
+        outs[0][...] = results[0]
+        outs[1][...] = results[1]
+        return
+    width = cols // (3 * heads)
+    jump = outs[1].shape[1]
+    for h in range(heads):
+        outs[1][h] = results[1][h * jump : (h + 1) * jump]
+        for i in range(3):
+            at = (i * heads + h) * width
+            outs[0][:, h, i * width : (i + 1) * width] = results[0][:, at : at + width]
+
+
+def scatter_grads(qkv, proj, small, n_dp, n_t, heads=0):
     nz, ny = qkv.shape[:2]
     rows, cols = qkv.shape[3], qkv.shape[4] // n_t
     tails = [(rows, cols), proj.shape[4:], small.shape[4:]]
@@ -381,10 +395,13 @@
     scratch += room((ny - 1, n_t, nz), parts[:2]) + room((n_t, nz), parts[:2]) + room((n_t - 1, nz), parts[:2])
     scratch += room((nz,), tails) + room((nz - 1,), tails)
     slots = 3 + 5 * (n_t - 1) + (3 + 2 * n_t) * (ny - 1) + 3 * (nz - 1)
+    shapes = list(tails)
+    if heads:
+        shapes[:2] = [(rows, heads, cols // heads), (heads, proj.shape[4] // heads, proj.shape[5])]
     scratch += [pltpu.SemaphoreType.DMA((slots,)), pltpu.SemaphoreType.DMA((slots,))]
     return pl.pallas_call(
-        functools.partial(scatter_kernel, ny, nz, n_t),
-        out_shape=[jax.ShapeDtypeStruct(tail, F32) for tail in tails],
+        functools.partial(scatter_kernel, ny, nz, n_t, heads),
+        out_shape=[jax.ShapeDtypeStruct(shape, F32) for shape in shapes],
         in_specs=[ANYWHERE] * 3,
         out_specs=[ANYWHERE] * 3,
         scratch_shapes=scratch,
@@ -419,10 +436,10 @@
     return raised / jnp.sum(raised, axis=-1, keepdims=True), lane
 
 
-def key_softmax(query, keys, count):
+def key_softmax(query, keys, gap):
     scores = dot(query, keys, ((1,), (1,)))
     col = lax.broadcasted_iota(jnp.int32, scores.shape, 1)
-    scores = jnp.where(col < count, scores, -1e30)
+    scores = jnp.where((col < gap[0]) | (col >= gap[1]), scores, -1e30)
     raised = jnp.exp(scores - jnp.max(scores, axis=-1, keepdims=True))
     return raised * (1.0 / jnp.sum(raised, axis=-1, keepdims=True))
 
@@ -439,20 +456,21 @@
     block,
     count,
     factor,
-    cot_own,
+    tokens,
+    cotangent,
+    moved_x,
+    moved_cot,
     router,
     flat_row,
     flat_col,
     expert_col,
-    code_row,
-    code_col,
+    order,
     win,
     wout,
-    x_in,
     live,
     norms,
     qkv,
-    proj,
+    proj_in,
     out,
     grad_x,
     gqkv_out,
@@ -461,6 +479,15 @@
     gnorms,
     gin_mine,
     gout_mine,
+    x_in,
+    cot_own,
+    proj,
+    dhidden_in,
+    edge_o,
+    edge_g,
+    edge_sent,
+    edge_o_got,
+    edge_g_got,
     c_own,
     hidden_in,
     mixed,
@@ -492,6 +519,7 @@
     w_sems,
     c_sems,
     cot_sems,
+    edge_sems,
     go_send,
     go_recv,
     back_send,
@@ -506,6 +534,9 @@
     hidden = win.shape[1]
     other = 1 - t
     partner = (dp, other)
+    own_rows, strip = tokens.shape[1], edge_o.shape[1]
+    head, edge = rows - strip, own_rows - count
+    gap = (jnp.where(t == 0, count, count - edge), jnp.where(t == 0, rows, rows - edge))
 
     barrier = pltpu.get_barrier_semaphore()
     pl.semaphore_signal(barrier, inc=1, device_id=partner, device_id_type=MESH)
@@ -516,6 +547,10 @@
 
     lax.fori_loop(1, n_dp, hello, 0)
     pl.semaphore_wait(barrier, n_dp)
+
+    def slot_codes(shape, axis):
+        q = lax.broadcasted_iota(jnp.int32, shape, axis)
+        return q + (q >> (share.bit_length() - 1)) * share * (n_t - 1) + t * share
 
     def image(i):
         return pl.ds(pl.multiple_of(i * rows, 16), rows)
@@ -602,6 +637,32 @@
         lax.fori_loop(1, n_dp, step, 0)
 
     low = lax.broadcasted_iota(jnp.int32, (rows, 128), 1) < 64
+
+    def edge_copy(i, m):
+        return pltpu.make_async_remote_copy(
+            src_ref=(edge_o, edge_sent)[i].at[m],
+            dst_ref=(edge_o_got, edge_g_got)[i].at[m],
+            send_sem=edge_sems.at[2 * i, m],
+            recv_sem=edge_sems.at[2 * i + 1, m],
+            device_id=partner,
+            device_id_type=MESH,
+        )
+
+    for own_ref, ref, moved in ((cot_own, cotangent, moved_cot), (x_in, tokens, moved_x)):
+        own_ref[:, :head] = ref[:, :head]
+
+        @pl.when(t == 0)
+        def _(own_ref=own_ref, ref=ref):
+            own_ref[:, head:] = ref[:, head:rows]
+
+        @pl.when(t != 0)
+        def _(own_ref=own_ref, moved=moved):
+            own_ref[:, head:] = moved[...]
+
+    def permutation():
+        return (order[...] == lax.broadcasted_iota(jnp.int32, (d, d), 1)).astype(F32).astype(BF16)
+
+    proj[...] = dot(permutation(), proj_in[...], ((0,), (0,))).astype(BF16)
 
     def attend(m, carry):
         cot_copy(m).start()
@@ -621,7 +682,7 @@
             zero = jnp.zeros_like(query)
             parts = []
             for own in (low, ~low):
-                probs = key_softmax(jnp.where(own, query, zero), keys, count)
+                probs = key_softmax(jnp.where(own, query, zero), keys, gap)
                 parts.append(dot(probs.astype(BF16), values, ((1,), (0,))))
             context[m, :, dest : dest + 128] = jnp.where(low, parts[0], parts[1]).astype(BF16)
         hidden = xf + live[m] * dot(context[m], proj[...], ((1,), (0,)))
@@ -652,7 +713,7 @@
             gate = jnp.sum(jnp.where(lane == expert_col[m, :, k : k + 1], probs, 0.0), axis=-1, keepdims=True)
             gates[m, :, k : k + 1] = gate
             scaled.append((gate * cot).astype(BF16))
-        codes = code_col[...]
+        codes = slot_codes((n_dp * share, 1), 0)
         picks = [(flat_row[m, k : k + 1, :] == codes).astype(F32).astype(BF16) for k in range(2)]
         sent[m, :, :d] = dot(picks[0] + picks[1], c, ((1,), (0,))).astype(BF16)
         moved = dot(picks[0], scaled[0], ((1,), (0,))) + dot(picks[1], scaled[1], ((1,), (0,)))
@@ -698,18 +759,32 @@
             dx_acc[...] += dot(dpre, w1, ((1,), (1,)))
             return inner
 
-        lax.fori_loop(
-            0, hidden // tile, functools.partial(chunk, win, wout, gin_mine, gout_mine), 0
-        )
-
-        @pl.when(m == 0)
+        def own_half():
+            lax.fori_loop(0, hidden // tile, functools.partial(chunk, win, wout, gin_mine, gout_mine), 0)
+
+        def other_half():
+            lax.fori_loop(0, hidden // tile, functools.partial(chunk, win_got, wout_got, gin, gout), 0)
+
+        @pl.when(m < batches - 1)
         def _():
-            w_copy(0).wait_recv()
-            w_copy(1).wait_recv()
-
-        lax.fori_loop(
-            0, hidden // tile, functools.partial(chunk, win_got, wout_got, gin, gout), 0
-        )
+            own_half()
+
+            @pl.when(m == 0)
+            def _():
+                w_copy(0).wait_recv()
+                w_copy(1).wait_recv()
+
+            other_half()
+
+        @pl.when(m == batches - 1)
+        def _():
+            other_half()
+            gin_half[...] = gin[...].astype(BF16)
+            gout_half[...] = gout[...].astype(BF16)
+            grad_copy(0).start()
+            grad_copy(1).start()
+            own_half()
+
         got[m, :, :d] = y_acc[...].astype(BF16)
         got[m, :, d:] = dx_acc[...].astype(BF16)
         every(lambda k: back_copy(m, k).start())
@@ -718,12 +793,9 @@
 
     lax.fori_loop(0, batches, expert_step, 0)
 
-    gin_half[...] = gin[...].astype(BF16)
-    gout_half[...] = gout[...].astype(BF16)
-
     def combine(m, carry):
         every(lambda k: back_copy(m, k).wait_recv())
-        codes = code_row[...]
+        codes = slot_codes((1, n_dp * share), 1)
         for i in (other, t):
             picks = [(flat_col[m, image(i), k : k + 1] == codes).astype(F32).astype(BF16) for k in range(2)]
             one = dot(picks[0], ret[m, :, :d], ((1,), (0,)))
@@ -754,7 +826,10 @@
     def retreat(m):
         pay_copy(m).wait_recv()
         hidden = hidden_in[m]
-        out[m] = (hidden + mix[m] + paid[m, :, :d].astype(F32)).astype(BF16)
+        result = (hidden + mix[m] + paid[m, :, :d].astype(F32)).astype(BF16)
+        out[m, :head] = result[:head]
+        edge_o[m] = result[head:]
+        edge_copy(0, m).start()
         unit, inverse = standardise(hidden)
         c = (unit * norms[2:3] + norms[3:4]).astype(BF16)
         probs, lane = gate_softmax(c, router[...], experts)
@@ -770,7 +845,7 @@
         gnorms[2:3] += jnp.sum(dc * unit, axis=0, keepdims=True)
         gnorms[3:4] += jnp.sum(dc, axis=0, keepdims=True)
         dhidden = cot_all[m, image(t)].astype(F32) + norm_back(dc * norms[2:3], unit, inverse)
-        grad_x[m] = dhidden
+        dhidden_in[...] = dhidden
         dattn = (live[m] * dhidden).astype(BF16)
         gproj[...] += dot(context[m], dattn, ((0,), (0,)))
         dcontext = dot(dattn, proj[...], ((1,), (1,))).astype(BF16)
@@ -782,7 +857,7 @@
             zero = jnp.zeros_like(query)
             parts = []
             for own in (low, ~low):
-                probs = key_softmax(jnp.where(own, query, zero), keys, count)
+                probs = key_softmax(jnp.where(own, query, zero), keys, gap)
                 dvalues = dot(probs.astype(BF16), grads, ((0,), (0,)))
                 dweights = dot(jnp.where(own, grads, zero), values, ((1,), (1,)))
                 dscores = probs * (dweights - jnp.sum(dweights * probs, axis=-1, keepdims=True))
@@ -801,21 +876,27 @@
         da = dot(dmixed[...], qkv[...], ((1,), (1,)))
         gnorms[0:1] += jnp.sum(da * unit, axis=0, keepdims=True)
         gnorms[1:2] += jnp.sum(da, axis=0, keepdims=True)
-        grad_x[m] += norm_back(da * norms[0:1], unit, inverse)
+        result = dhidden_in[...] + norm_back(da * norms[0:1], unit, inverse)
+        grad_x[m, :head] = result[:head]
+        edge_g[m] = result[head:]
+        edge_sent[m] = result[head:].astype(BF16)
+        edge_copy(1, m).start()
 
     pieces = 4
 
     def finish(m, carry):
-        for i in range(pieces):
-
-            @pl.when(m == i)
-            def _(i=i):
-                grad_copy(i).start()
-
         @pl.when(m < batches)
         def _():
             combine(m, 0)
 
+        @pl.when(m == 0)
+        def _():
+            grad_copy(2).start()
+
+        @pl.when(m == batches - 1)
+        def _():
+            grad_copy(3).start()
+
         @pl.when(m > 0)
         def _():
             retreat(m - 1)
@@ -823,10 +904,36 @@
         return carry
 
     lax.fori_loop(0, batches + 1, finish, 0)
-    for i in range(batches + 1, pieces):
-        grad_copy(i).start()
     gqkv_out[...] = gqkv[...].astype(BF16)
-    gproj_out[...] = gproj[...].astype(BF16)
+    gproj_out[...] = dot(permutation(), gproj[...].astype(BF16), ((1,), (0,))).astype(BF16)
+
+    @pl.when(t != 0)
+    def _():
+        out[:, head:] = tokens[:, head:]
+        grad_x[:, head:] = cotangent[:, head:].astype(F32)
+
+    first = own_rows - strip
+    near = lax.broadcasted_iota(jnp.int32, (16, d), 0) < strip - edge
+
+    def place(m, carry):
+        edge_copy(0, m).wait()
+        edge_copy(1, m).wait()
+
+        @pl.when(t == 0)
+        def _():
+            for ref, mine, theirs in ((out, edge_o, edge_o_got), (grad_x, edge_g, edge_g_got)):
+                ref[m, head:first] = mine[m, : first - head]
+                blend = jnp.where(
+                    near,
+                    mine[m, first - head : first - head + 16].astype(F32),
+                    theirs[m, :16].astype(F32),
+                )
+                ref[m, first : first + 16] = blend.astype(ref.dtype)
+                ref[m, first + 16 :] = theirs[m, 16:].astype(ref.dtype)
+
+        return carry
+
+    lax.fori_loop(0, batches, place, 0)
     for i in range(pieces):
         grad_copy(i).wait()
     gin_mine[...] += gin_got[...].astype(F32)
@@ -845,17 +952,19 @@
     lax.fori_loop(0, batches, drain, 0)
 
 
-def layer(cot_own, router, flat, expert_of, codes, win, wout, saved, experts, n_dp, n_t, block, count, factor):
-    batches, rows, d = cot_own.shape
-    slots = codes.shape[0]
+def layer(held, moved, router, flat, expert_of, order, win, wout, live, norms, qkv, proj, statics):
+    batches, own_rows, d = held[0].shape
+    experts, n_dp, n_t, block, count, factor, cap = statics
+    rows, strip = live.shape[1], moved[0].shape[1]
+    slots = n_dp * cap // n_t
     half = win.shape[1]
     wide = 3 * n_t * block
     dma = pltpu.SemaphoreType.DMA
     return pl.pallas_call(
         functools.partial(layer_kernel, experts, n_t, block, count, factor),
         out_shape=[
-            jax.ShapeDtypeStruct((batches, rows, d), BF16),
-            jax.ShapeDtypeStruct((batches, rows, d), F32),
+            jax.ShapeDtypeStruct((batches, own_rows, d), BF16),
+            jax.ShapeDtypeStruct((batches, own_rows, d), F32),
             jax.ShapeDtypeStruct((d, wide), BF16),
             jax.ShapeDtypeStruct((d, d), BF16),
             jax.ShapeDtypeStruct((d, router.shape[1]), F32),
@@ -863,9 +972,18 @@
             jax.ShapeDtypeStruct((d, half), F32),
             jax.ShapeDtypeStruct((half, d), F32),
         ],
-        in_specs=[ANYWHERE] * 14,
+        in_specs=[ANYWHERE] * 15,
         out_specs=[ANYWHERE] * 8,
         scratch_shapes=[
+            pltpu.VMEM((batches, rows, d), BF16),
+            pltpu.VMEM((batches, rows, d), BF16),
+            pltpu.VMEM((d, d), BF16),
+            pltpu.VMEM((rows, d), F32),
+            pltpu.VMEM((batches, strip, d), BF16),
+            pltpu.VMEM((batches, strip, d), F32),
+            pltpu.VMEM((batches, strip, d), BF16),
+            pltpu.VMEM((batches, strip, d), BF16),
+            pltpu.VMEM((batches, strip, d), BF16),
             pltpu.VMEM((batches, rows, d), BF16),
             pltpu.VMEM((batches, rows, d), F32),
             pltpu.VMEM((batches, rows, wide), BF16),
@@ -897,6 +1015,7 @@
             dma((2, 2)),
             dma((2, batches)),
             dma((2, batches)),
+            dma((4, batches)),
             dma((batches, n_dp - 1)),
             dma((batches, n_dp - 1)),
             dma((batches, n_dp - 1)),
@@ -908,16 +1027,19 @@
             collective_id=2, has_side_effects=True, vmem_limit_bytes=67043328
         ),
     )(
-        cot_own,
+        *held,
+        *moved,
         router,
         flat,
         flat.transpose(0, 2, 1),
         expert_of.transpose(0, 2, 1),
-        codes[None, :],
-        codes[:, None],
+        order,
         win,
         wout,
-        *saved,
+        live,
+        norms,
+        qkv,
+        proj,
     )
 
 
@@ -1216,32 +1338,27 @@
     )
     small = jnp.pad(small, ((0, 0), (0, 128 - small.shape[1])))
     qkv_block = w_qkv.reshape(-1, heads_here, 3, width).transpose(0, 2, 1, 3).reshape(-1, 3 * block)
-    held = jnp.concatenate([tokens, cotangent], axis=0)
-    qkv, proj, small, moved = gather_weights(
-        qkv_block, w_proj.reshape(-1, d), small, n_dp, n_t, (held[:, SEQ:],)
+    strip = -(-edge // 16) * 16
+    qkv, proj, small, *moved = gather_weights(
+        qkv_block, w_proj.reshape(-1, d), small, n_dp, n_t, (tokens, cotangent), strip
     )
     router = jnp.where(jnp.arange(128) < experts, small, 0)
     norms = jnp.pad(small[:, experts : experts + 4].astype(F32).T, ((0, 4), (0, 0)))
-    proj = proj.reshape(n_dp, n_t, heads_here, w_proj.shape[1], d)
-    proj = proj.transpose(1, 2, 0, 3, 4).reshape(n_t * block, d)
-
-    def pad_rows(v, axis, fill=0):
-        spec = [(0, 0)] * v.ndim
-        spec[axis] = (0, padded - SEQ)
-        return jnp.pad(v, spec, constant_values=fill)
+    order = jnp.arange(d, dtype=jnp.int32).reshape(n_t, heads_here, n_dp, -1)
+    order = order.transpose(2, 0, 1, 3).reshape(d, 1)
 
     def lay(v, axis, fill=0):
-        shape = v.shape
-        v = v.reshape(shape[:axis] + (n_t, SEQ) + shape[axis + 1 :])
-        v = pad_rows(v, axis + 1, fill)
-        return v.reshape(shape[:axis] + (n_t * padded,) + shape[axis + 1 :])
+        def rows_of(low, high):
+            return lax.slice_in_dim(v, low, high, axis=axis)
+
+        shape = v.shape[:axis] + (padded - SEQ,) + v.shape[axis + 1 :]
+        hole = jnp.full(shape, fill, v.dtype)
+        return jnp.concatenate(
+            [rows_of(0, SEQ), hole, rows_of(own_rows, span), hole, rows_of(SEQ, own_rows)], axis=axis
+        )
 
     def own(v, axis):
         return lax.dynamic_slice_in_dim(v, t * padded, padded, axis)
-
-    laid = jnp.where(t == 0, held[:, :SEQ], jnp.concatenate([moved, held[:, : SEQ - edge]], axis=1))
-    laid = pad_rows(laid, 1)
-    x, cot_own = laid[:batches], laid[batches:]
 
     live = live_rows[:, :span]
     rank = priority[:, 0, :span]
@@ -1257,52 +1374,40 @@
     keep = (live[:, None, :] > 0) & (slot < cap)
     flat = lay(jnp.where(keep, picks * cap + slot, -1), 2, -1)
     expert_of = lay(jnp.where(keep, picks, -1), 2, -1)
-    codes = (jnp.arange(experts)[:, None] * cap + t * share + jnp.arange(share)[None, :]).reshape(-1)
     live_own = own(lay(live.astype(F32)[:, :, None], 1), 1)
 
     output, grad_x, grad_qkv, grad_proj, grad_router, grad_norms, grad_in, grad_out = layer(
-        cot_own,
+        (tokens, cotangent),
+        moved,
         router,
         flat,
         expert_of,
-        codes,
+        order,
         w_in[0],
         w_out[0],
-        (x, live_own, norms, qkv, proj),
-        experts,
-        n_dp,
-        n_t,
-        block,
-        SEQ,
-        factor,
-    )
-
-    out_edge = lax.ppermute(output[:, :edge], "tensor", [(1, 0)])
-    grad_edge = lax.ppermute(grad_x[:, :edge], "tensor", [(1, 0)])
-    rest = SEQ - edge
-
-    def home(v, moved_rows, other):
-        return jnp.where(
-            t == 0,
-            jnp.concatenate([v[:, :SEQ], moved_rows], axis=1),
-            jnp.concatenate([v[:, edge:SEQ], other[:, rest:].astype(v.dtype)], axis=1),
-        )
-
+        live_own,
+        norms,
+        qkv,
+        proj.reshape(d, d),
+        (experts, n_dp, n_t, block, SEQ, factor, cap),
+    )
     nz, ny = grid_sizes(n_dp)
-    grad_proj = grad_proj.reshape(n_t, heads_here, n_dp, -1, d)
-    grad_proj = grad_proj.transpose(2, 0, 1, 3, 4).reshape(nz, ny, 2, n_t, -1, d)
     lane = jnp.arange(128)
     smalls = jnp.where(lane < experts, grad_router, 0.0)
     smalls = smalls + jnp.pad(grad_norms[:4].T, ((0, 0), (experts, 124 - experts)))
     grad_qkv, grad_proj, smalls = scatter_grads(
-        grad_qkv.reshape(nz, ny, 2, d // n_dp, -1), grad_proj, smalls.reshape(nz, ny, 2, n_t, -1, 128), n_dp, n_t
-    )
-    grad_qkv = grad_qkv.reshape(-1, 3, heads_here, width).transpose(0, 2, 1, 3)
+        grad_qkv.reshape(nz, ny, 2, d // n_dp, -1),
+        grad_proj.reshape(nz, ny, 2, n_t, -1, d),
+        smalls.reshape(nz, ny, 2, n_t, -1, 128),
+        n_dp,
+        n_t,
+        heads_here,
+    )
     return (
-        home(output, out_edge, tokens),
-        home(grad_x, grad_edge, cotangent),
-        grad_qkv.reshape(w_qkv.shape),
-        grad_proj.reshape(w_proj.shape),
+        output,
+        grad_x,
+        grad_qkv,
+        grad_proj,
         grad_in[None],
         grad_out[None],
         smalls[:, :experts],
@@ -1318,7 +1423,9 @@
     n_t = lax.axis_size("tensor")
     images = live_rows.shape[1] // SEQ
     block = w_qkv.shape[1] * (w_qkv.shape[2] // 3)
-    if n_t == 2 and images == 2 and tokens.shape[1] >= SEQ and block % 128 == 0 and w_qkv.shape[2] == 192:
+    edge = tokens.shape[1] - SEQ
+    fits = tokens.shape[1] % 16 == 0 and 0 < edge <= SEQ // 2 and args[3].shape[0] == 1
+    if n_t == 2 and images == 2 and fits and block % 128 == 0 and w_qkv.shape[2] == 192 and args[0].shape[0] > 1:
         return fast(*args)
     return general(*args)
 

time: 309 us -> 288 us (0.932)
  local copies, waits for them, and re-layouts: 37.1 us -> 25.6 us
  other arithmetic: 10.8 us -> 5.55 us
    reshape x14 -> x1, local copies, waits for them, and re-layouts: 12 us -> 0.84 us  [fast(): order = jnp.arange(d, dtype=jnp.int32).reshape(n_t, heads_here, n_dp, -1)]
    slice x10 -> x9, local copies, waits for them, and re-layouts: 8.52 us -> 0.23 us  [rows_of(): return lax.slice_in_dim(v, low, high, axis=axis)]
    select_n x3 -> x0, other arithmetic: 6.49 us -> none  [the longest x2 5.07 us: home(): jnp.where(t == 0, jnp.concatenate([v[:, :SEQ], moved_rows], axis=1), jnp....]
    pallas_call x1, Pallas kernels: 34.5 us -> 29.1 us  [scatter_grads(): pl.pallas_call(functools.partial(scatter_kernel, ny, nz, n_t, heads), out...]
    pallas_call x1, Pallas kernels: 191 us -> 195 us  [layer(): pl.pallas_call(functools.partial(layer_kernel, experts, n_t, block, count...]
    concatenate x1 -> x5, local copies, waits for them, and re-layouts: 0.05 us -> 3.21 us  [lay(): jnp.concatenate([rows_of(0, SEQ), hole, rows_of(own_rows, span), hole, ro...]
    unnamed x57 -> x34, local copies, waits for them, and re-layouts: 8.35 us -> 9.7 us
  transfers between devices with their start and end apart: 2 -> 0, of which waited for: 0 -> 0; matrix products, arithmetic and copies ran while one was open for 7% -> 0% of each run, Pallas kernels for 11% -> 0%
where the time goes in v7:
time: 288 us; the launch traced here: 287 us
  Pallas kernels  255 us (89%)
  local copies, waits for them, and re-layouts  25.6 us (9%)
  other arithmetic  5.55 us (2%)
    pallas_call x1, Pallas kernels, layer(): pl.pallas_call(functools.partial(layer_kernel, experts, n_t, block, count...  195 us
    pallas_call x1, Pallas kernels, gather_weights(): pl.pallas_call(functools.partial(gather_kernel, ny, nz, n_t, len(side)),...  31 us
    pallas_call x1, Pallas kernels, scatter_grads(): pl.pallas_call(functools.partial(scatter_kernel, ny, nz, n_t, heads), out...  29.1 us
    unnamed x34, local copies, waits for them, and re-layouts  9.7 us

profile of v7, /device:TPU:0, one launch (start us, length us, event | category | flops | bytes accessed | tf_op | source)
XLA Modules:
  0.0 287.4 jit_solution(17246528454938354354)
XLA Ops:
  2.1 0.7 copy.73
  2.9 0.7 copy.74
  3.6 0.7 copy.75
  4.4 0.8 concatenate.15
  7.1 1.3 reshape.141.refs_1_
  9.3 0.8 copy.70
  11.2 0.8 reshape.158.order
  13.6 0.8 concatenate.19
  14.4 0.8 constant_dynamic-slice_fusion.live
  15.2 1.1 copy.78
  16.3 1.1 copy.77
  17.4 31.0 %shard_map.221 = (bf16[4,2,2,32,1536]{4,3,2,1,0:T(8,128)(2,1)}, bf16[4,2,2,2,16,512]{5,4,3,2,1,0:T(8,128)(2,1)}, bf16[4,2,2,2,16,128]{5,4,3,2,1,0:T(8,128)(2,1)}...) custom-call(bf16[32,768]{1,0:T(8,128)(2,1)} %reshape.140.refs_0_, bf16[16,512]{1,0:T(8,128)(2,1)} %reshape.141.refs_1_, ...), custom_call_target="tpu_custom_call" | custom-call | tf_op jit(solution)/shard_map/pallas_call | solution.py:222
  48.4 1.0 slice.90
  50.2 1.6 broadcast_select_fusion.router
  51.8 194.6 %shard_map.222 = (bf16[3,256,512]{2,1,0:T(8,128)(2,1)}, f32[3,256,512]{2,1,0:T(8,128)}, bf16[512,1536]{1,0:T(8,128)(2,1)}, bf16[512,512]{1,0:T(8,128)(2,1)}, f32...) custom-call(bf16[3,256,512]{2,1,0:T(8,128)(2,1)} %tokens.1, ...), custom_call_target="tpu_custom_call" | custom-call | tf_op jit(solution)/shard_map/pallas_call | solution.py:963
  246.4 0.8 slice.74
  247.3 1.8 pad_add_fusion
  249.1 29.1 %shard_map.223 = (f32[32,4,192]{2,1,0:T(4,128)}, f32[4,4,512]{2,1,0:T(4,128)}, f32[16,128]{1,0:T(8,128)}) custom-call(bf16[4,2,2,32,1536]{4,3,2,1,0:T(8,128)(2,1)} %bitcast.62, bf16[4,2,2,2,16,512]{5,4,3,2,1,0:T(8,128)(2,1)} %bitcast.70, f32[4,2,2,2,16,128]{5,4,3,2,1,0:T(8,128)} %bitcast.65), custom_call_target="tpu_custom_call" | custom-call | tf_op jit(solution)/shard_map/pallas_call | solution.py:402
  278.3 1.6 slice_reduce_fusion.1
  279.8 0.9 copy.101
  280.7 1.1 copy.102
  283.2 1.3 copy.105
  284.5 1.0 copy-done
  285.5 1.3 copy.106
  (58 shorter events, 9.6 us)
Async XLA Ops:
  0.6 12.2 %copy-start.7 = (s32[3,512,2]{1,2,0:T(2,128)S(1)}, s32[3,512,2]{1,2,0:T(2,128)}, u32[]{:S(2)}) copy-start(s32[3,512,2]{1,2,0:T(2,128)} %param.25) | copy-start | bytes 36868
  0.7 49.5 %copy-start.9 = (pred[128]{0:T(512)(128)(4,1)}, pred[128]{0:T(512)(128)(4,1)S(1)}, u32[]{:S(2)}) copy-start(pred[128]{0:T(512)(128)(4,1)S(1)} %iota_compare_fusion.1) | copy-start | bytes 388
  13.3 35.2 %copy-start.6 = (s32[3,2,416]{2,1,0:T(2,128)}, s32[3,2,416]{2,1,0:T(2,128)S(1)}, u32[]{:S(2)}) copy-start(s32[3,2,416]{2,1,0:T(2,128)S(1)} %concatenate.17.flat_row) | copy-start | bytes 29956
  246.4 33.5 %copy-start.3 = (bf16[3,256,512]{2,1,0:T(8,128)(2,1)S(1)}, bf16[3,256,512]{2,1,0:T(8,128)(2,1)}, u32[]{:S(2)}) copy-start(bf16[3,256,512]{2,1,0:T(8,128)(2,1)} %get-tuple-element.62) | copy-start | bytes 2359300
  249.1 31.6 %copy-start.2 = (f32[3,256,512]{2,1,0:T(8,128)S(1)}, f32[3,256,512]{2,1,0:T(8,128)}, u32[]{:S(2)}) copy-start(f32[3,256,512]{2,1,0:T(8,128)} %get-tuple-element.63) | copy-start | bytes 4718596
  279.8 2.0 copy-start.5
  279.8 2.7 copy-start.8
  280.7 2.4 copy-start.1
  283.2 2.3 copy-start
  285.5 1.3 copy-start.4

commit v8 on v7

--- a/solution.py
+++ b/solution.py
@@ -2,6 +2,7 @@
 
 import jax
 import jax.numpy as jnp
+import numpy as np
 from jax import lax
 from jax.experimental import pallas as pl
 from jax.experimental.pallas import tpu as pltpu
@@ -463,10 +464,9 @@
     router,
     flat_row,
     flat_col,
-    expert_col,
     order,
-    win,
-    wout,
+    win_own,
+    wout_own,
     live,
     norms,
     qkv,
@@ -510,8 +510,8 @@
     dx_acc,
     win_got,
     wout_got,
-    gin,
-    gout,
+    gin_far,
+    gout_far,
     gin_half,
     gout_half,
     gin_got,
@@ -531,7 +531,8 @@
     n_dp = lax.axis_size("dp")
     dp, t = lax.axis_index("dp"), lax.axis_index("tensor")
     share = sent.shape[1] // n_dp
-    hidden = win.shape[1]
+    hidden = win_own.shape[1]
+    shift = (share * n_t).bit_length() - 1
     other = 1 - t
     partner = (dp, other)
     own_rows, strip = tokens.shape[1], edge_o.shape[1]
@@ -551,6 +552,9 @@
     def slot_codes(shape, axis):
         q = lax.broadcasted_iota(jnp.int32, shape, axis)
         return q + (q >> (share.bit_length() - 1)) * share * (n_t - 1) + t * share
+
+    def band(m):
+        return pl.ds(pl.multiple_of(m * rows, 16), rows)
 
     def image(i):
         return pl.ds(pl.multiple_of(i * rows, 16), rows)
@@ -621,7 +625,7 @@
 
     def w_copy(i):
         return pltpu.make_async_remote_copy(
-            src_ref=(win, wout)[i],
+            src_ref=(win_own, wout_own)[i],
             dst_ref=(win_got, wout_got)[i],
             send_sem=w_sems.at[0, i],
             recv_sem=w_sems.at[1, i],
@@ -710,7 +714,7 @@
         cot = cot_all[m].astype(F32)
         scaled = []
         for k in range(2):
-            gate = jnp.sum(jnp.where(lane == expert_col[m, :, k : k + 1], probs, 0.0), axis=-1, keepdims=True)
+            gate = jnp.sum(jnp.where(lane == flat_col[m, :, k : k + 1] >> shift, probs, 0.0), axis=-1, keepdims=True)
             gates[m, :, k : k + 1] = gate
             scaled.append((gate * cot).astype(BF16))
         codes = slot_codes((n_dp * share, 1), 0)
@@ -728,20 +732,22 @@
 
     def clear(i, carry):
         cols = pl.ds(pl.multiple_of(i * tile, tile), tile)
-        for into in (gin, gin_mine):
+        for into in (gin_far, gin_mine):
             into[:, cols] = jnp.zeros((d, tile), F32)
-        for into in (gout, gout_mine):
+        for into in (gout_far, gout_mine):
             into[cols, :] = jnp.zeros((tile, d), F32)
         return carry
 
     lax.fori_loop(0, hidden // tile, clear, 0)
 
-    def expert_step(m, carry):
-        every(lambda k: go_copy(m, k).wait_recv())
-        y_acc[...] = jnp.zeros_like(y_acc)
-        dx_acc[...] = jnp.zeros_like(dx_acc)
-
-        def chunk(win, wout, gin, gout, i, inner):
+    slots = n_dp * share
+    sums = ((y_acc, dx_acc), (mix.at[pl.ds(0, slots)], dx.at[pl.ds(0, slots)]))
+
+    def expert_half(m, own):
+        y_sum, dx_sum = sums[m % 2]
+        win, wout, gin, gout = (win_own, wout_own, gin_mine, gout_mine) if own else (win_got, wout_got, gin_far, gout_far)
+
+        def chunk(i, inner):
             cols = pl.ds(pl.multiple_of(i * tile, tile), tile)
             x = got[m, :, :d]
             dprod = got[m, :, d:]
@@ -755,43 +761,40 @@
             dpre = (dot(dprod, w2, ((1,), (1,))) * slope).astype(BF16)
             gin[:, cols] += dot(x, dpre, ((0,), (0,)))
             gout[cols, :] += dot(active, dprod, ((0,), (0,)))
-            y_acc[...] += dot(active, w2, ((1,), (0,)))
-            dx_acc[...] += dot(dpre, w1, ((1,), (1,)))
+            y_sum[...] += dot(active, w2, ((1,), (0,)))
+            dx_sum[...] += dot(dpre, w1, ((1,), (1,)))
             return inner
 
-        def own_half():
-            lax.fori_loop(0, hidden // tile, functools.partial(chunk, win, wout, gin_mine, gout_mine), 0)
-
-        def other_half():
-            lax.fori_loop(0, hidden // tile, functools.partial(chunk, win_got, wout_got, gin, gout), 0)
-
-        @pl.when(m < batches - 1)
-        def _():
-            own_half()
-
-            @pl.when(m == 0)
-            def _():
-                w_copy(0).wait_recv()
-                w_copy(1).wait_recv()
-
-            other_half()
-
-        @pl.when(m == batches - 1)
-        def _():
-            other_half()
-            gin_half[...] = gin[...].astype(BF16)
-            gout_half[...] = gout[...].astype(BF16)
-            grad_copy(0).start()
-            grad_copy(1).start()
-            own_half()
-
-        got[m, :, :d] = y_acc[...].astype(BF16)
-        got[m, :, d:] = dx_acc[...].astype(BF16)
+        lax.fori_loop(0, hidden // tile, chunk, 0)
+
+    def expert_begin(m):
+        every(lambda k: go_copy(m, k).wait_recv())
+        for ref in sums[m % 2]:
+            ref[...] = jnp.zeros((slots, d), F32)
+
+    def expert_end(m):
+        got[m, :, :d] = sums[m % 2][0][...].astype(BF16)
+        got[m, :, d:] = sums[m % 2][1][...].astype(BF16)
         every(lambda k: back_copy(m, k).start())
         ret[m, part(dp)] = got[m, part(dp)]
-        return carry
-
-    lax.fori_loop(0, batches, expert_step, 0)
+
+    last = batches - 1
+    for m in range(last):
+        expert_begin(m)
+        expert_half(m, True)
+    w_copy(0).wait_recv()
+    w_copy(1).wait_recv()
+    for m in range(last):
+        expert_half(m, False)
+        expert_end(m)
+    expert_begin(last)
+    expert_half(last, False)
+    gin_half[...] = gin_far[...].astype(BF16)
+    gout_half[...] = gout_far[...].astype(BF16)
+    grad_copy(0).start()
+    grad_copy(1).start()
+    expert_half(last, True)
+    expert_end(last)
 
     def combine(m, carry):
         every(lambda k: back_copy(m, k).wait_recv())
@@ -813,8 +816,8 @@
                 pay[m, :, 2 * d :] = dg.astype(BF16)
                 pay_copy(m).start()
             else:
-                mix[m] = mixture
-                dx[m] = d_rows
+                mix[band(m)] = mixture
+                dx[band(m)] = d_rows
                 dgate[m] = dg
         return carry
 
@@ -826,7 +829,7 @@
     def retreat(m):
         pay_copy(m).wait_recv()
         hidden = hidden_in[m]
-        result = (hidden + mix[m] + paid[m, :, :d].astype(F32)).astype(BF16)
+        result = (hidden + mix[band(m)] + paid[m, :, :d].astype(F32)).astype(BF16)
         out[m, :head] = result[:head]
         edge_o[m] = result[head:]
         edge_copy(0, m).start()
@@ -836,9 +839,9 @@
         dg = dgate[m] + paid[m, :, 2 * d :].astype(F32)
         dprobs = jnp.zeros_like(probs)
         for k in range(2):
-            dprobs = dprobs + jnp.where(lane == expert_col[m, image(t), k : k + 1], dg[:, k : k + 1], 0.0)
+            dprobs = dprobs + jnp.where(lane == flat_col[m, image(t), k : k + 1] >> shift, dg[:, k : k + 1], 0.0)
         dlogits = probs * (dprobs - jnp.sum(dprobs * probs, axis=-1, keepdims=True))
-        dc = dx[m] + paid[m, :, d : 2 * d].astype(F32)
+        dc = dx[band(m)] + paid[m, :, d : 2 * d].astype(F32)
         for piece in two_parts(dlogits):
             grouter[...] += dot(c, piece, ((0,), (0,)))
             dc = dc + dot(piece, router[...], ((1,), (1,)))
@@ -952,7 +955,7 @@
     lax.fori_loop(0, batches, drain, 0)
 
 
-def layer(held, moved, router, flat, expert_of, order, win, wout, live, norms, qkv, proj, statics):
+def layer(held, moved, router, flat, order, win, wout, live, norms, qkv, proj, statics):
     batches, own_rows, d = held[0].shape
     experts, n_dp, n_t, block, count, factor, cap = statics
     rows, strip = live.shape[1], moved[0].shape[1]
@@ -972,7 +975,7 @@
             jax.ShapeDtypeStruct((d, half), F32),
             jax.ShapeDtypeStruct((half, d), F32),
         ],
-        in_specs=[ANYWHERE] * 15,
+        in_specs=[ANYWHERE] * 14,
         out_specs=[ANYWHERE] * 8,
         scratch_shapes=[
             pltpu.VMEM((batches, rows, d), BF16),
@@ -996,8 +999,8 @@
             pltpu.VMEM((batches, slots, 2 * d), BF16),
             pltpu.VMEM((batches, rows, 2 * d + 128), BF16),
             pltpu.VMEM((batches, rows, 2 * d + 128), BF16),
-            pltpu.VMEM((batches, rows, d), F32),
-            pltpu.VMEM((batches, rows, d), F32),
+            pltpu.VMEM((max(batches * rows, slots), d), F32),
+            pltpu.VMEM((max(batches * rows, slots), d), F32),
             pltpu.VMEM((batches, rows, 128), F32),
             pltpu.VMEM((rows, wide), BF16),
             pltpu.VMEM((d, wide), F32),
@@ -1032,7 +1035,6 @@
         router,
         flat,
         flat.transpose(0, 2, 1),
-        expert_of.transpose(0, 2, 1),
         order,
         win,
         wout,
@@ -1333,9 +1335,8 @@
     edge = own_rows - SEQ
     factor = width ** (-0.5)
 
-    small = jnp.concatenate(
-        [w_router] + [v[:, None] for v in (gain_attn, shift_attn, gain_moe, shift_moe)], axis=1
-    )
+    vectors = jnp.stack([gain_attn, shift_attn, gain_moe, shift_moe])
+    small = jnp.concatenate([w_router, vectors.T], axis=1)
     small = jnp.pad(small, ((0, 0), (0, 128 - small.shape[1])))
     qkv_block = w_qkv.reshape(-1, heads_here, 3, width).transpose(0, 2, 1, 3).reshape(-1, 3 * block)
     strip = -(-edge // 16) * 16
@@ -1344,8 +1345,8 @@
     )
     router = jnp.where(jnp.arange(128) < experts, small, 0)
     norms = jnp.pad(small[:, experts : experts + 4].astype(F32).T, ((0, 4), (0, 0)))
-    order = jnp.arange(d, dtype=jnp.int32).reshape(n_t, heads_here, n_dp, -1)
-    order = order.transpose(2, 0, 1, 3).reshape(d, 1)
+    order = np.arange(d, dtype=np.int32).reshape(n_t, heads_here, n_dp, -1)
+    order = jnp.asarray(order.transpose(2, 0, 1, 3).reshape(d, 1))
 
     def lay(v, axis, fill=0):
         def rows_of(low, high):
@@ -1373,7 +1374,6 @@
     slot = jnp.sum(ahead * hits, axis=-1).astype(jnp.int32)
     keep = (live[:, None, :] > 0) & (slot < cap)
     flat = lay(jnp.where(keep, picks * cap + slot, -1), 2, -1)
-    expert_of = lay(jnp.where(keep, picks, -1), 2, -1)
     live_own = own(lay(live.astype(F32)[:, :, None], 1), 1)
 
     output, grad_x, grad_qkv, grad_proj, grad_router, grad_norms, grad_in, grad_out = layer(
@@ -1381,7 +1381,6 @@
         moved,
         router,
         flat,
-        expert_of,
         order,
         w_in[0],
         w_out[0],
@@ -1425,7 +1424,7 @@
     block = w_qkv.shape[1] * (w_qkv.shape[2] // 3)
     edge = tokens.shape[1] - SEQ
     fits = tokens.shape[1] % 16 == 0 and 0 < edge <= SEQ // 2 and args[3].shape[0] == 1
-    if n_t == 2 and images == 2 and fits and block % 128 == 0 and w_qkv.shape[2] == 192 and args[0].shape[0] > 1:
+    if n_t == 2 and images == 2 and fits and block % 128 == 0 and w_qkv.shape[2] == 192 and args[0].shape[0] == 3:
         return fast(*args)
     return general(*args)
 

time: 288 us -> 283 us (0.983)
  local copies, waits for them, and re-layouts: 25.6 us -> 19.2 us
    pallas_call x1, Pallas kernels: 195 us -> 189 us  [layer(): pl.pallas_call(functools.partial(layer_kernel, experts, n_t, block, count...]
    pallas_call x1, Pallas kernels: 29.1 us -> 33.9 us  [scatter_grads(): pl.pallas_call(functools.partial(scatter_kernel, ny, nz, n_t, heads), out...]
    broadcast_in_dim x4 -> x0, local copies, waits for them, and re-layouts: 2.98 us -> none  [fast(): v[:, None]]
where the time goes in v8:
time: 283 us; the launch traced here: 282 us
  Pallas kernels  254 us (90%)
  local copies, waits for them, and re-layouts  19.2 us (7%)
  other arithmetic  7.61 us (3%)
    pallas_call x1, Pallas kernels, layer(): pl.pallas_call(functools.partial(layer_kernel, experts, n_t, block, count...  189 us
    pallas_call x1, Pallas kernels, scatter_grads(): pl.pallas_call(functools.partial(scatter_kernel, ny, nz, n_t, heads), out...  33.9 us
    pallas_call x1, Pallas kernels, gather_weights(): pl.pallas_call(functools.partial(gather_kernel, ny, nz, n_t, len(side)),...  31 us
    unnamed x34, local copies, waits for them, and re-layouts  9.71 us

profile of v8, /device:TPU:0, one launch (start us, length us, event | category | flops | bytes accessed | tf_op | source)
XLA Modules:
  0.0 282.0 jit_solution(3970842200976803081)
XLA Ops:
  0.7 0.7 pad_maximum_fusion
  1.4 0.7 slice_compare_fusion
  2.2 1.4 fusion.22.refs_2_
  4.3 0.7 slice_bitcast_fusion
  5.0 1.3 reshape.56.refs_1_
  6.3 0.7 fusion.24
  7.1 0.8 copy.65
  8.1 0.7 reshape.55.refs_0_
  10.4 0.8 concatenate.15
  11.2 0.8 constant_dynamic-slice_fusion.live
  11.9 1.1 copy.69
  13.0 31.0 %shard_map.230 = (bf16[4,2,2,32,1536]{4,3,2,1,0:T(8,128)(2,1)}, bf16[4,2,2,2,16,512]{5,4,3,2,1,0:T(8,128)(2,1)}, bf16[4,2,2,2,16,128]{5,4,3,2,1,0:T(8,128)(2,1)}...) custom-call(bf16[32,768]{1,0:T(8,128)(2,1)} %reshape.55.refs_0_, bf16[16,512]{1,0:T(8,128)(2,1)} %reshape.56.refs_1_, ...), custom_call_target="tpu_custom_call" | custom-call | tf_op jit(solution)/shard_map/pallas_call | solution.py:223
  44.1 1.0 slice.75
  45.8 1.6 broadcast_select_fusion.router
  47.4 188.7 %shard_map.231 = (bf16[3,256,512]{2,1,0:T(8,128)(2,1)}, f32[3,256,512]{2,1,0:T(8,128)}, bf16[512,1536]{1,0:T(8,128)(2,1)}, bf16[512,512]{1,0:T(8,128)(2,1)}, f32...) custom-call(bf16[3,256,512]{2,1,0:T(8,128)(2,1)} %tokens.1, ...), custom_call_target="tpu_custom_call" | custom-call | tf_op jit(solution)/shard_map/pallas_call | solution.py:966
  236.1 0.8 slice.62
  237.1 1.8 pad_add_fusion
  238.9 33.9 %shard_map.232 = (f32[32,4,192]{2,1,0:T(4,128)}, f32[4,4,512]{2,1,0:T(4,128)}, f32[16,128]{1,0:T(8,128)}) custom-call(bf16[4,2,2,32,1536]{4,3,2,1,0:T(8,128)(2,1)} %bitcast.58, bf16[4,2,2,2,16,512]{5,4,3,2,1,0:T(8,128)(2,1)} %bitcast.67, f32[4,2,2,2,16,128]{5,4,3,2,1,0:T(8,128)} %bitcast.62), custom_call_target="tpu_custom_call" | custom-call | tf_op jit(solution)/shard_map/pallas_call | solution.py:403
  272.8 1.6 slice_reduce_fusion.1
  274.4 0.9 copy.91
  275.3 1.1 copy.92
  277.7 1.3 copy.95
  279.0 1.0 copy-done
  280.1 1.3 copy.96
  (48 shorter events, 5.3 us)
Async XLA Ops:
  0.6 9.1 %copy-start.7 = (s32[3,512,2]{1,2,0:T(2,128)S(1)}, s32[3,512,2]{1,2,0:T(2,128)}, u32[]{:S(2)}) copy-start(s32[3,512,2]{1,2,0:T(2,128)} %param.26) | copy-start | bytes 36868
  0.7 45.2 %copy-start.9 = (pred[128]{0:T(512)(128)(4,1)}, pred[128]{0:T(512)(128)(4,1)S(1)}, u32[]{:S(2)}) copy-start(pred[128]{0:T(512)(128)(4,1)S(1)} %iota_compare_fusion.2) | copy-start | bytes 388
  10.0 34.1 %copy-start.6 = (s32[3,2,416]{2,1,0:T(2,128)}, s32[3,2,416]{2,1,0:T(2,128)S(1)}, u32[]{:S(2)}) copy-start(s32[3,2,416]{2,1,0:T(2,128)S(1)} %concatenate.14.flat_row) | copy-start | bytes 29956
  236.1 38.3 %copy-start.3 = (bf16[3,256,512]{2,1,0:T(8,128)(2,1)S(1)}, bf16[3,256,512]{2,1,0:T(8,128)(2,1)}, u32[]{:S(2)}) copy-start(bf16[3,256,512]{2,1,0:T(8,128)(2,1)} %get-tuple-element.60) | copy-start | bytes 2359300
  238.9 36.4 %copy-start.2 = (f32[3,256,512]{2,1,0:T(8,128)S(1)}, f32[3,256,512]{2,1,0:T(8,128)}, u32[]{:S(2)}) copy-start(f32[3,256,512]{2,1,0:T(8,128)} %get-tuple-element.61) | copy-start | bytes 4718596
  274.4 2.0 copy-start.5
  275.3 1.8 copy-start.8
  275.3 2.4 copy-start.1
  277.7 2.3 copy-start
  280.1 1.3 copy-start.4

commit v9 on v8

--- a/solution.py
+++ b/solution.py
@@ -728,7 +728,7 @@
 
     lax.fori_loop(0, batches, dispatch, 0)
 
-    tile = 256
+    tile = min(512, hidden)
 
     def clear(i, carry):
         cols = pl.ds(pl.multiple_of(i * tile, tile), tile)

time: 283 us -> 281 us (level)
  no operation moved by 1% of the time
where the time goes in v9:
time: 281 us; the launch traced here: 280 us
  Pallas kernels  252 us (90%)
  local copies, waits for them, and re-layouts  19.2 us (7%)
  other arithmetic  7.61 us (3%)
    pallas_call x1, Pallas kernels, layer(): pl.pallas_call(functools.partial(layer_kernel, experts, n_t, block, count...  186 us
    pallas_call x1, Pallas kernels, scatter_grads(): pl.pallas_call(functools.partial(scatter_kernel, ny, nz, n_t, heads), out...  34.5 us
    pallas_call x1, Pallas kernels, gather_weights(): pl.pallas_call(functools.partial(gather_kernel, ny, nz, n_t, len(side)),...  31 us
    unnamed x34, local copies, waits for them, and re-layouts  9.71 us

profile of v9, /device:TPU:0, one launch (start us, length us, event | category | flops | bytes accessed | tf_op | source)
XLA Modules:
  0.0 280.3 jit_solution(1491116099850181457)
XLA Ops:
  0.7 0.7 pad_maximum_fusion
  1.4 0.7 slice_compare_fusion
  2.2 1.4 fusion.22.refs_2_
  4.3 0.7 slice_bitcast_fusion
  5.0 1.3 reshape.56.refs_1_
  6.3 0.7 fusion.24
  7.1 0.8 copy.65
  8.1 0.7 reshape.55.refs_0_
  10.4 0.8 concatenate.15
  11.2 0.8 constant_dynamic-slice_fusion.live
  11.9 1.1 copy.69
  13.0 31.0 %shard_map.230 = (bf16[4,2,2,32,1536]{4,3,2,1,0:T(8,128)(2,1)}, bf16[4,2,2,2,16,512]{5,4,3,2,1,0:T(8,128)(2,1)}, bf16[4,2,2,2,16,128]{5,4,3,2,1,0:T(8,128)(2,1)}...) custom-call(bf16[32,768]{1,0:T(8,128)(2,1)} %reshape.55.refs_0_, bf16[16,512]{1,0:T(8,128)(2,1)} %reshape.56.refs_1_, ...), custom_call_target="tpu_custom_call" | custom-call | tf_op jit(solution)/shard_map/pallas_call | solution.py:223
  44.1 1.0 slice.75
  45.8 1.6 broadcast_select_fusion.router
  47.4 186.4 %shard_map.231 = (bf16[3,256,512]{2,1,0:T(8,128)(2,1)}, f32[3,256,512]{2,1,0:T(8,128)}, bf16[512,1536]{1,0:T(8,128)(2,1)}, bf16[512,512]{1,0:T(8,128)(2,1)}, f32...) custom-call(bf16[3,256,512]{2,1,0:T(8,128)(2,1)} %tokens.1, ...), custom_call_target="tpu_custom_call" | custom-call | tf_op jit(solution)/shard_map/pallas_call | solution.py:966
  233.9 0.8 slice.62
  234.8 1.8 pad_add_fusion
  236.6 34.5 %shard_map.232 = (f32[32,4,192]{2,1,0:T(4,128)}, f32[4,4,512]{2,1,0:T(4,128)}, f32[16,128]{1,0:T(8,128)}) custom-call(bf16[4,2,2,32,1536]{4,3,2,1,0:T(8,128)(2,1)} %bitcast.58, bf16[4,2,2,2,16,512]{5,4,3,2,1,0:T(8,128)(2,1)} %bitcast.67, f32[4,2,2,2,16,128]{5,4,3,2,1,0:T(8,128)} %bitcast.62), custom_call_target="tpu_custom_call" | custom-call | tf_op jit(solution)/shard_map/pallas_call | solution.py:403
  271.1 1.6 slice_reduce_fusion.1
  272.7 0.9 copy.91
  273.6 1.1 copy.92
  276.0 1.3 copy.95
  277.4 1.0 copy-done
  278.4 1.3 copy.96
  (48 shorter events, 5.3 us)
Async XLA Ops:
  0.6 9.1 %copy-start.7 = (s32[3,512,2]{1,2,0:T(2,128)S(1)}, s32[3,512,2]{1,2,0:T(2,128)}, u32[]{:S(2)}) copy-start(s32[3,512,2]{1,2,0:T(2,128)} %param.26) | copy-start | bytes 36868
  0.7 45.2 %copy-start.9 = (pred[128]{0:T(512)(128)(4,1)}, pred[128]{0:T(512)(128)(4,1)S(1)}, u32[]{:S(2)}) copy-start(pred[128]{0:T(512)(128)(4,1)S(1)} %iota_compare_fusion.2) | copy-start | bytes 388
  10.0 34.1 %copy-start.6 = (s32[3,2,416]{2,1,0:T(2,128)}, s32[3,2,416]{2,1,0:T(2,128)S(1)}, u32[]{:S(2)}) copy-start(s32[3,2,416]{2,1,0:T(2,128)S(1)} %concatenate.14.flat_row) | copy-start | bytes 29956
  233.9 38.9 %copy-start.3 = (bf16[3,256,512]{2,1,0:T(8,128)(2,1)S(1)}, bf16[3,256,512]{2,1,0:T(8,128)(2,1)}, u32[]{:S(2)}) copy-start(bf16[3,256,512]{2,1,0:T(8,128)(2,1)} %get-tuple-element.60) | copy-start | bytes 2359300
  236.6 37.0 %copy-start.2 = (f32[3,256,512]{2,1,0:T(8,128)S(1)}, f32[3,256,512]{2,1,0:T(8,128)}, u32[]{:S(2)}) copy-start(f32[3,256,512]{2,1,0:T(8,128)} %get-tuple-element.61) | copy-start | bytes 4718596
  272.7 2.0 copy-start.5
  273.6 1.8 copy-start.8
  273.6 2.4 copy-start.1
  276.0 2.3 copy-start
  278.4 1.3 copy-start.4

commit v10 on v9

--- a/solution.py
+++ b/solution.py
@@ -1343,7 +1343,7 @@
     qkv, proj, small, *moved = gather_weights(
         qkv_block, w_proj.reshape(-1, d), small, n_dp, n_t, (tokens, cotangent), strip
     )
-    router = jnp.where(jnp.arange(128) < experts, small, 0)
+    router = small
     norms = jnp.pad(small[:, experts : experts + 4].astype(F32).T, ((0, 4), (0, 0)))
     order = np.arange(d, dtype=np.int32).reshape(n_t, heads_here, n_dp, -1)
     order = jnp.asarray(order.transpose(2, 0, 1, 3).reshape(d, 1))

time: 281 us -> 277 us (0.986)
  other arithmetic: 7.61 us -> 3.67 us
    unnamed x34 -> x44, local copies, waits for them, and re-layouts: 9.71 us -> 8.9 us
where the time goes in v10:
time: 277 us
  Pallas kernels  252 us (91%)
  local copies, waits for them, and re-layouts  19.5 us (7%)
  other arithmetic  3.67 us (1%)
    pallas_call x1, Pallas kernels, layer(): pl.pallas_call(functools.partial(layer_kernel, experts, n_t, block, count...  186 us
    pallas_call x1, Pallas kernels, scatter_grads(): pl.pallas_call(functools.partial(scatter_kernel, ny, nz, n_t, heads), out...  34.5 us
    pallas_call x1, Pallas kernels, gather_weights(): pl.pallas_call(functools.partial(gather_kernel, ny, nz, n_t, len(side)),...  31 us
    unnamed x44, local copies, waits for them, and re-layouts  8.9 us

profile of v10, /device:TPU:0, one launch (start us, length us, event | category | flops | bytes accessed | tf_op | source)
XLA Modules:
  0.0 276.6 jit_solution(17469649894823344830)
XLA Ops:
  0.6 0.7 fusion.24
  1.3 0.7 slice_bitcast_fusion
  2.2 0.7 copy.86
  3.6 0.7 slice_compare_fusion
  4.3 0.7 and_select_fusion
  5.3 1.1 copy.71
  7.0 0.8 concatenate.15
  7.8 0.7 constant_dynamic-slice_fusion.live
  8.7 0.7 reshape.55.refs_0_
  10.2 0.7 fusion.22.refs_2_
  10.9 31.0 %shard_map.230 = (bf16[4,2,2,32,1536]{4,3,2,1,0:T(8,128)(2,1)}, bf16[4,2,2,2,16,512]{5,4,3,2,1,0:T(8,128)(2,1)}, bf16[4,2,2,2,16,128]{5,4,3,2,1,0:T(8,128)(2,1)}...) custom-call(bf16[32,768]{1,0:T(8,128)(2,1)} %reshape.55.refs_0_, bf16[16,512]{1,0:T(8,128)(2,1)} %reshape.56.refs_1_, ...), custom_call_target="tpu_custom_call" | custom-call | tf_op jit(solution)/shard_map/pallas_call | solution.py:223
  41.9 1.0 slice.75
  43.7 186.4 %shard_map.231 = (bf16[3,256,512]{2,1,0:T(8,128)(2,1)}, f32[3,256,512]{2,1,0:T(8,128)}, bf16[512,1536]{1,0:T(8,128)(2,1)}, bf16[512,512]{1,0:T(8,128)(2,1)}, f32...) custom-call(bf16[3,256,512]{2,1,0:T(8,128)(2,1)} %tokens.1, ...), custom_call_target="tpu_custom_call" | custom-call | tf_op jit(solution)/shard_map/pallas_call | solution.py:966
  230.1 1.1 copy.76
  231.3 0.7 slice_bitcast_fusion.1
  232.1 0.8 copy.77
  232.9 34.5 %shard_map.232 = (f32[32,4,192]{2,1,0:T(4,128)}, f32[4,4,512]{2,1,0:T(4,128)}, f32[16,128]{1,0:T(8,128)}) custom-call(bf16[4,2,2,32,1536]{4,3,2,1,0:T(8,128)(2,1)} %bitcast.58, bf16[4,2,2,2,16,512]{5,4,3,2,1,0:T(8,128)(2,1)} %bitcast.67, f32[4,2,2,2,16,128]{5,4,3,2,1,0:T(8,128)} %bitcast.62), custom_call_target="tpu_custom_call" | custom-call | tf_op jit(solution)/shard_map/pallas_call | solution.py:403
  267.5 1.6 slice_reduce_fusion.1
  269.0 0.9 copy.94
  269.9 1.1 copy.95
  271.1 0.7 copy.96
  272.4 1.3 copy.98
  273.7 1.0 copy-done
  274.7 1.3 copy.99
  (58 shorter events, 4.5 us)
Async XLA Ops:
  2.9 5.6 %copy-start.7 = (bf16[32,4,192]{2,1,0:T(4,128)(2,1)S(1)}, bf16[32,4,192]{2,1,0:T(4,128)(2,1)}, u32[]{:S(2)}) copy-start(bf16[32,4,192]{2,1,0:T(4,128)(2,1)} %param.16) | copy-start | bytes 147460
  3.5 5.9 %copy-start.9 = (bf16[4,4,512]{2,1,0:T(4,128)(2,1)S(1)}, bf16[4,4,512]{2,1,0:T(4,128)(2,1)}, u32[]{:S(2)}) copy-start(bf16[4,4,512]{2,1,0:T(4,128)(2,1)} %param.17) | copy-start | bytes 49156
  3.5 6.6 %copy-start.11 = (bf16[16]{0:T(256)(128)(2,1)S(1)}, bf16[16]{0:T(256)(128)(2,1)}, u32[]{:S(2)}) copy-start(bf16[16]{0:T(256)(128)(2,1)} %param.24) | copy-start | bytes 100
  3.6 6.5 %copy-start.12 = (bf16[16]{0:T(256)(128)(2,1)S(1)}, bf16[16]{0:T(256)(128)(2,1)}, u32[]{:S(2)}) copy-start(bf16[16]{0:T(256)(128)(2,1)} %param.23) | copy-start | bytes 100
  3.6 6.5 %copy-start.13 = (bf16[16]{0:T(256)(128)(2,1)S(1)}, bf16[16]{0:T(256)(128)(2,1)}, u32[]{:S(2)}) copy-start(bf16[16]{0:T(256)(128)(2,1)} %param.22) | copy-start | bytes 100
  3.6 6.5 %copy-start.14 = (bf16[16]{0:T(256)(128)(2,1)S(1)}, bf16[16]{0:T(256)(128)(2,1)}, u32[]{:S(2)}) copy-start(bf16[16]{0:T(256)(128)(2,1)} %param.21) | copy-start | bytes 100
  3.6 6.6 %copy-start.10 = (bf16[16,16]{1,0:T(8,128)(2,1)S(1)}, bf16[16,16]{1,0:T(8,128)(2,1)}, u32[]{:S(2)}) copy-start(bf16[16,16]{1,0:T(8,128)(2,1)} %param.20) | copy-start | bytes 1540
  5.3 1.7 copy-start.6
  230.1 38.9 %copy-start.3 = (bf16[3,256,512]{2,1,0:T(8,128)(2,1)S(1)}, bf16[3,256,512]{2,1,0:T(8,128)(2,1)}, u32[]{:S(2)}) copy-start(bf16[3,256,512]{2,1,0:T(8,128)(2,1)} %get-tuple-element.60) | copy-start | bytes 2359300
  232.9 37.0 %copy-start.2 = (f32[3,256,512]{2,1,0:T(8,128)S(1)}, f32[3,256,512]{2,1,0:T(8,128)}, u32[]{:S(2)}) copy-start(f32[3,256,512]{2,1,0:T(8,128)} %get-tuple-element.61) | copy-start | bytes 4718596
  269.0 2.0 copy-start.5
  269.9 1.8 copy-start.8
  269.9 2.4 copy-start.1
  272.4 2.3 copy-start
  274.7 1.3 copy-start.4
